TPU v7x, 8 devices: a whole 2x2x1 slice. The times are simulated.
8 devices in a mesh: data: 1 (over z), fsdp: 2 (over y), ep: 4 (over x, core).
Axes of the slice: x: 2, y: 2, z: 1, core: 2. Of those that a mesh axis runs over, the one named last changes fastest.
Arguments:
- tokens: bfloat16 [64, 512, 1024], P(('data', 'fsdp', 'ep'))
- w_qkv: bfloat16 [1024, 3, 16, 64], P('fsdp')
- w_out: bfloat16 [16, 64, 1024], P(None, None, 'fsdp')
- w_gate: bfloat16 [32, 1024, 512], P('ep', 'fsdp')
- w_up: bfloat16 [32, 1024, 512], P('ep', 'fsdp')
- w_down: bfloat16 [32, 512, 1024], P('ep', None, 'fsdp')
- expert_idx: int32 [64, 512, 8], P(('data', 'fsdp', 'ep'))
- expert_slot: int32 [64, 512, 8], P(('data', 'fsdp', 'ep'))
- gate_wts: bfloat16 [64, 512, 8], P(('data', 'fsdp', 'ep'))
- d_out: bfloat16 [64, 512, 1024], P(('data', 'fsdp', 'ep'))
Outputs:
- output 1: bfloat16 [64, 512, 1024], P(('data', 'fsdp', 'ep'))
- output 2: bfloat16 [64, 512, 1024], P(('data', 'fsdp', 'ep'))
- output 3: float32 [32, 1024, 512], P(('data', 'ep'), 'fsdp')
- output 4: float32 [32, 1024, 512], P(('data', 'ep'), 'fsdp')
- output 5: float32 [32, 512, 1024], P(('data', 'ep'), None, 'fsdp')
All inputs are finite; a program needn't handle non-finite values.
Results may differ from a plain program's by a relative error of at most 0.02.
Values are sent between devices in bfloat16 or wider.
A program may use at most 1 GiB of HBM per device.

v0:
```python
import functools
import math

import jax
import jax.numpy as jnp
from jax import lax
from jax.experimental import pallas as pl
from jax.experimental.pallas import tpu as pltpu
from jax.sharding import PartitionSpec as P


F32 = jnp.float32
BF16 = jnp.bfloat16
BLOCK = 256
TILE = 256
ALIGN = 16
LANES = 128
LOG2E = math.log2(math.e)
EPS = 1e-6
VMEM_BYTES = 60 * 2 ** 20


def settings(gflop, mbytes):
    return {
        'compiler_params': pltpu.CompilerParams(dimension_semantics=('arbitrary',), vmem_limit_bytes=VMEM_BYTES),
        'cost_estimate': pl.CostEstimate(flops=gflop * 10 ** 9, bytes_accessed=mbytes * 10 ** 6, transcendentals=0),
    }


def nt_dot(lhs, rhs):
    return lax.dot_general(lhs, rhs, (((1,), (1,)), ((), ())), preferred_element_type=F32)


def tn_dot(lhs, rhs):
    return lax.dot_general(lhs, rhs, (((0,), (0,)), ((), ())), preferred_element_type=F32)


def lanes_of(head, values):
    lane = lax.broadcasted_iota(jnp.int32, values.shape, 1)
    return jnp.where((lane >= LANES // 2) == bool(head), values, jnp.zeros_like(values))


def attention_kernel(x_ref, w_ref, h_ref, qkv_ref, ctx, *, head_dim):
    seq_len, d_model = x_ref.shape[1:]
    n_fsdp, n_ep, rows, half = w_ref.shape
    n_qkv = rows * 3 // 4
    x = x_ref[0].astype(F32)
    normed = (x * lax.rsqrt(jnp.mean(x * x, axis=-1, keepdims=True) + EPS)).astype(BF16)
    for p in range(n_ep):
        part = nt_dot(normed[:, :half], w_ref[0, p, :n_qkv]) + nt_dot(normed[:, half:], w_ref[1, p, :n_qkv])
        qkv_ref[0, :, p * n_qkv:(p + 1) * n_qkv] = part.astype(BF16)
    scale = head_dim ** -0.5 * LOG2E

    def pair(i, carry):
        q2, k2, v2 = (qkv_ref[0, :, pl.ds(pl.multiple_of(t * d_model + i * LANES, LANES), LANES)] for t in range(3))
        for first in range(0, seq_len, BLOCK):
            end = first + BLOCK
            keys, vals = k2[:end], v2[:end]
            causal = lax.broadcasted_iota(jnp.int32, (BLOCK, end), 0) + first >= lax.broadcasted_iota(jnp.int32, (BLOCK, end), 1)
            both = []
            for head in range(2):
                scores = nt_dot(lanes_of(head, q2[first:end]), keys) * scale
                scores = jnp.where(causal, scores, -1e30)
                probs = jnp.exp2(scores - jnp.max(scores, axis=-1, keepdims=True))
                probs = (probs * (1.0 / jnp.sum(probs, axis=-1, keepdims=True))).astype(BF16)
                both.append(jnp.dot(probs, vals, preferred_element_type=F32))
            lane = lax.broadcasted_iota(jnp.int32, (BLOCK, LANES), 1)
            ctx[first:end, pl.ds(pl.multiple_of(i * LANES, LANES), LANES)] = jnp.where(lane < LANES // 2, both[0], both[1]).astype(BF16)
        return carry

    lax.fori_loop(0, d_model // LANES, pair, 0)
    for f in range(n_fsdp):
        w_out = jnp.concatenate([w_ref[f, p, n_qkv:] for p in range(n_ep)], axis=0)
        cols = slice(f * half, (f + 1) * half)
        h_ref[0, :, cols] = (x_ref[0, :, cols].astype(F32) + jnp.dot(ctx[...], w_out, preferred_element_type=F32)).astype(BF16)


def attention(tokens, weights, head_dim):
    n_seq, seq_len, d_model = tokens.shape
    seq_spec = pl.BlockSpec((1, seq_len, d_model), lambda s: (s, 0, 0))
    qkv_spec = pl.BlockSpec((1, seq_len, 3 * d_model), lambda s: (s, 0, 0))
    w_spec = pl.BlockSpec(weights.shape, lambda s: (0, 0, 0, 0))
    return pl.pallas_call(
        functools.partial(attention_kernel, head_dim=head_dim),
        grid=(n_seq,),
        in_specs=[seq_spec, w_spec],
        out_specs=[seq_spec, qkv_spec],
        out_shape=[jax.ShapeDtypeStruct(tokens.shape, BF16), jax.ShapeDtypeStruct((n_seq, seq_len, 3 * d_model), BF16)],
        scratch_shapes=[pltpu.VMEM((seq_len, d_model), BF16)],
        name='attention',
        **settings(90, 60),
    )(tokens, weights)


def attention_grad_kernel(dh_ref, x_ref, qkv_ref, w_ref, dx_ref, dctx, dqkv, *, head_dim):
    seq_len, d_model = x_ref.shape[1:]
    n_fsdp, n_ep, rows, half = w_ref.shape
    n_qkv = rows * 3 // 4
    n_out = rows - n_qkv
    dh = dh_ref[0]
    for p in range(n_ep):
        part = nt_dot(dh[:, :half], w_ref[0, p, n_qkv:]) + nt_dot(dh[:, half:], w_ref[1, p, n_qkv:])
        dctx[:, p * n_out:(p + 1) * n_out] = part.astype(BF16)
    scale = head_dim ** -0.5

    def pair(i, carry):
        col = pl.multiple_of(i * LANES, LANES)
        q2, k2, v2 = (qkv_ref[0, :, pl.ds(pl.multiple_of(t * d_model + i * LANES, LANES), LANES)] for t in range(3))
        d2 = dctx[:, pl.ds(col, LANES)]
        dk = [jnp.zeros((BLOCK, LANES), F32)] * (seq_len // BLOCK)
        dv = list(dk)
        for first in range(0, seq_len, BLOCK):
            end = first + BLOCK
            keys, vals = k2[:end], v2[:end]
            causal = lax.broadcasted_iota(jnp.int32, (end, BLOCK), 1) + first >= lax.broadcasted_iota(jnp.int32, (end, BLOCK), 0)
            dq = jnp.zeros((BLOCK, LANES), F32)
            for head in range(2):
                q, d = lanes_of(head, q2[first:end]), lanes_of(head, d2[first:end])
                scores = jnp.where(causal, nt_dot(keys, q) * (scale * LOG2E), -1e30)
                probs = jnp.exp2(scores - jnp.max(scores, axis=0, keepdims=True))
                probs = probs * (1.0 / jnp.sum(probs, axis=0, keepdims=True))
                d_probs = nt_dot(vals, d)
                d_scores = probs * (d_probs - jnp.sum(probs * d_probs, axis=0, keepdims=True))
                d_scores = (d_scores * scale).astype(BF16)
                dv_part = jnp.dot(probs.astype(BF16), d, preferred_element_type=F32)
                dk_part = jnp.dot(d_scores, q, preferred_element_type=F32)
                dq = dq + tn_dot(d_scores, lanes_of(head, keys))
                for n in range(end // BLOCK):
                    dk[n] = dk[n] + dk_part[n * BLOCK:(n + 1) * BLOCK]
                    dv[n] = dv[n] + dv_part[n * BLOCK:(n + 1) * BLOCK]
            dqkv[first:end, pl.ds(col, LANES)] = dq.astype(BF16)
        for n in range(seq_len // BLOCK):
            dqkv[n * BLOCK:(n + 1) * BLOCK, pl.ds(pl.multiple_of(d_model + i * LANES, LANES), LANES)] = dk[n].astype(BF16)
            dqkv[n * BLOCK:(n + 1) * BLOCK, pl.ds(pl.multiple_of(2 * d_model + i * LANES, LANES), LANES)] = dv[n].astype(BF16)
        return carry

    lax.fori_loop(0, d_model // LANES, pair, 0)
    x = x_ref[0].astype(F32)
    d_normed = []
    for f in range(n_fsdp):
        w_qkv = jnp.concatenate([w_ref[f, p, :n_qkv] for p in range(n_ep)], axis=0)
        d_normed.append(jnp.dot(dqkv[...], w_qkv, preferred_element_type=F32).astype(BF16))
    d_normed = jnp.concatenate(d_normed, axis=1).astype(F32)
    inv = lax.rsqrt(jnp.mean(x * x, axis=-1, keepdims=True) + EPS)
    proj = jnp.mean(d_normed * x, axis=-1, keepdims=True)
    d_x = (d_normed * inv - x * (inv * inv * inv * proj)).astype(BF16).astype(F32)
    dx_ref[0] = (dh_ref[0].astype(F32) + d_x).astype(BF16)


def attention_grad(d_h, tokens, qkv, weights, head_dim):
    n_seq, seq_len, d_model = tokens.shape
    seq_spec = pl.BlockSpec((1, seq_len, d_model), lambda s: (s, 0, 0))
    qkv_spec = pl.BlockSpec((1, seq_len, 3 * d_model), lambda s: (s, 0, 0))
    w_spec = pl.BlockSpec(weights.shape, lambda s: (0, 0, 0, 0))
    return pl.pallas_call(
        functools.partial(attention_grad_kernel, head_dim=head_dim),
        grid=(n_seq,),
        in_specs=[seq_spec, seq_spec, qkv_spec, w_spec],
        out_specs=seq_spec,
        out_shape=jax.ShapeDtypeStruct(tokens.shape, BF16),
        scratch_shapes=[pltpu.VMEM((seq_len, d_model), BF16), pltpu.VMEM((seq_len, 3 * d_model), BF16)],
        name='attention_grad',
        **settings(150, 70),
    )(d_h, tokens, qkv, weights)


def capacity_of(tok_count, top_k, num_experts):
    return max(8, (5 * tok_count * top_k // (4 * num_experts) + 7) // 8 * 8)


def route_kernel(loc_ref, dest_ref, start_ref, rows_ref, off_ref, total, *, n_local):
    top_k = loc_ref.shape[1]
    ids = lax.broadcasted_iota(jnp.int32, (n_local, BLOCK), 0)
    upper = (lax.broadcasted_iota(jnp.int32, (BLOCK, BLOCK), 0) <= lax.broadcasted_iota(jnp.int32, (BLOCK, BLOCK), 1)).astype(F32).astype(BF16)
    before = (lax.broadcasted_iota(jnp.int32, (n_local, n_local), 0) > lax.broadcasted_iota(jnp.int32, (n_local, n_local), 1)).astype(F32).astype(BF16)

    @pl.when(pl.program_id(0) == 0)
    def _():
        total[...] = jnp.zeros(total.shape, jnp.int32)

    so_far = total[...]
    for s in range(loc_ref.shape[0]):
        for p in range(loc_ref.shape[2] // BLOCK):
            q = s * (loc_ref.shape[2] // BLOCK) + p
            loc = loc_ref[s, :, p * BLOCK:(p + 1) * BLOCK]
            member = jnp.zeros((n_local, BLOCK), F32)
            for j in range(top_k):
                member = jnp.where(loc[j:j + 1] == ids, 1.0, member)
            count = jnp.dot(member.astype(BF16), upper, preferred_element_type=F32)
            units = (count[:, BLOCK - 1:].astype(jnp.int32) + (ALIGN - 1)) // ALIGN
            units = jnp.broadcast_to(units, (n_local, LANES))
            start = jnp.dot(before, units.astype(F32).astype(BF16), preferred_element_type=F32).astype(jnp.int32) * ALIGN
            place = start[:, :1] + count.astype(jnp.int32) - 1
            for j in range(top_k):
                row = jnp.sum(jnp.where(loc[j:j + 1] == ids, place, 0), axis=0, keepdims=True)
                dest_ref[q, j:j + 1, :] = jnp.where(loc[j:j + 1] >= 0, row, -1)
            start_ref[q] = start
            rows_ref[q] = units * ALIGN
            off_ref[q] = so_far
            so_far = so_far + units * ALIGN
    total[...] = so_far


def route(local_ids, n_local):
    n_seq, top_k, seq_len = local_ids.shape
    per_seq = seq_len // BLOCK
    step = 2 if n_seq % 2 == 0 else 1
    n_blocks = n_seq * per_seq
    seg = jax.ShapeDtypeStruct((n_blocks, n_local, LANES), jnp.int32)
    seg_spec = pl.BlockSpec((step * per_seq, n_local, LANES), lambda s: (s, 0, 0))
    dest, *segs = pl.pallas_call(
        functools.partial(route_kernel, n_local=n_local),
        grid=(n_seq // step,),
        in_specs=[pl.BlockSpec((step, top_k, seq_len), lambda s: (s, 0, 0))],
        out_specs=[pl.BlockSpec((step * per_seq, top_k, BLOCK), lambda s: (s, 0, 0)), seg_spec, seg_spec, seg_spec],
        out_shape=[jax.ShapeDtypeStruct((n_blocks, top_k, BLOCK), jnp.int32), seg, seg, seg],
        scratch_shapes=[pltpu.VMEM((n_local, LANES), jnp.int32)],
        name='route',
        **settings(1, 3),
    )(local_ids)
    return dest, [part[:, :, 0] for part in segs]


def one_hot(dest_ref, gate_ref, first_row):
    rows = lax.broadcasted_iota(jnp.int32, (TILE, BLOCK), 0) + first_row
    dest = dest_ref[0]
    gate = gate_ref[0]
    picked = jnp.zeros((TILE, BLOCK), F32)
    for j in range(dest.shape[0]):
        picked = jnp.where(rows == dest[j:j + 1], gate[j:j + 1], picked)
    return picked


def dispatch_kernel(start_ref, rows_ref, off_ref, h_ref, dout_ref, dest_ref, gate_ref, *refs, base):
    r_hbm, d_hbm, u_s, rbuf, dbuf, sem = refs[-6:]
    step = pl.program_id(0)
    n_blocks = pl.num_programs(0)
    b = step + base
    n_exp = rows_ref.shape[1]
    slot = lax.rem(b, 2)

    def total(blk):
        return start_ref[blk, n_exp - 1] + rows_ref[blk, n_exp - 1]

    def drain(blk, which):
        n = pl.multiple_of(total(blk), ALIGN)

        @pl.when(n > 0)
        def _():
            pltpu.make_async_copy(rbuf.at[which, pl.ds(0, n), :], rbuf.at[which, pl.ds(0, n), :], sem.at[0, which]).wait()
            pltpu.make_async_copy(dbuf.at[which, pl.ds(0, n), :], dbuf.at[which, pl.ds(0, n), :], sem.at[1, which]).wait()

    @pl.when(step >= 2)
    def _():
        drain(b - 2, slot)

    hf = h_ref[...].astype(F32)
    u_s[...] = (hf * lax.rsqrt(jnp.mean(hf * hf, axis=-1, keepdims=True) + EPS)).astype(BF16)

    def tile(i, carry):
        first = pl.multiple_of(i * TILE, TILE)
        picked = one_hot(dest_ref, gate_ref, first)
        ones = jnp.where(picked > 0, 1.0, 0.0).astype(BF16)
        rbuf[slot, pl.ds(first, TILE), :] = jnp.dot(ones, u_s[...], preferred_element_type=F32).astype(BF16)
        dbuf[slot, pl.ds(first, TILE), :] = jnp.dot(picked.astype(BF16), dout_ref[...], preferred_element_type=F32).astype(BF16)
        return carry

    lax.fori_loop(0, (total(b) + (TILE - 1)) // TILE, tile, 0)

    def send(e, carry):
        n = pl.multiple_of(rows_ref[b, e], ALIGN)
        src = pl.multiple_of(start_ref[b, e], ALIGN)
        dst = pl.multiple_of(off_ref[b, e], ALIGN)

        @pl.when(n > 0)
        def _():
            pltpu.make_async_copy(rbuf.at[slot, pl.ds(src, n), :], r_hbm.at[e, pl.ds(dst, n), :], sem.at[0, slot]).start()
            pltpu.make_async_copy(dbuf.at[slot, pl.ds(src, n), :], d_hbm.at[e, pl.ds(dst, n), :], sem.at[1, slot]).start()

        return carry

    lax.fori_loop(0, n_exp, send, 0)

    @pl.when(step == n_blocks - 1)
    def _():
        @pl.when(n_blocks > 1)
        def _():
            drain(b - 1, 1 - slot)

        drain(b, slot)


def block_rows(top_k, n_local):
    return -(-(BLOCK * top_k + n_local * (ALIGN - 1)) // TILE) * TILE


def dispatch(h_tok, dout_tok, dest, gate, segs, base, held, n_local, max_rows):
    tok_count, d_model = h_tok.shape
    top_k = dest.shape[1]
    n_blocks = tok_count // BLOCK
    buf_rows = block_rows(top_k, n_local)
    tok_spec = pl.BlockSpec((BLOCK, d_model), lambda b, *_: (b, 0))
    map_spec = pl.BlockSpec((1, top_k, BLOCK), lambda b, *_: (b + base, 0, 0))
    rows_shape = jax.ShapeDtypeStruct((n_local, max_rows, d_model), BF16)
    hbm = pl.BlockSpec(memory_space=pl.ANY)
    return pl.pallas_call(
        functools.partial(dispatch_kernel, base=base),
        grid_spec=pltpu.PrefetchScalarGridSpec(
            num_scalar_prefetch=3,
            grid=(n_blocks,),
            in_specs=[tok_spec, tok_spec, map_spec, map_spec] + [hbm] * len(held),
            out_specs=[hbm, hbm],
            scratch_shapes=[
                pltpu.VMEM((BLOCK, d_model), BF16),
                pltpu.VMEM((2, buf_rows, d_model), BF16),
                pltpu.VMEM((2, buf_rows, d_model), BF16),
                pltpu.SemaphoreType.DMA((2, 2)),
            ],
        ),
        out_shape=[rows_shape, rows_shape],
        input_output_aliases={7: 0, 8: 1} if held else {},
        name='dispatch',
        **settings(40, 90),
    )(*segs, h_tok, dout_tok, dest, gate, *held)


def expert_kernel(count_ref, flip_ref, r_hbm, d_hbm, w_lo, w_hi, y_hbm, dr_hbm, dw_ref, rbuf, dbuf, ybuf, drbuf, done, in_sem, out_sem, *, expert_of):
    step = pl.program_id(0)
    n_steps = pl.num_programs(0)
    expert = expert_of(step)
    n_rows = count_ref[expert]
    n_tiles = jnp.maximum((n_rows + (TILE - 1)) // TILE, 1)
    half = dw_ref.shape[-1]

    def copies(who, i, slot, load):
        rows = pl.ds(pl.multiple_of(i * TILE, TILE), TILE)
        pairs = ((r_hbm, rbuf), (d_hbm, dbuf)) if load else ((ybuf, y_hbm), (drbuf, dr_hbm))
        for k, (src, dst) in enumerate(pairs):
            src = src.at[who, rows, :] if load else src.at[slot]
            dst = dst.at[slot] if load else dst.at[who, rows, :]
            yield pltpu.make_async_copy(src, dst, (in_sem if load else out_sem).at[k, slot])

    def start(*args):
        for copy in copies(*args):
            copy.start()

    def wait(*args):
        for copy in copies(*args):
            copy.wait()

    @pl.when(step == 0)
    def _():
        done[0] = 0
        start(expert, 0, 0, True)

    before = done[0]
    dw_ref[...] = jnp.zeros(dw_ref.shape, F32)

    def tile(i, carry):
        slot = lax.rem(before + i, 2)

        @pl.when(i + 1 < n_tiles)
        def _():
            start(expert, i + 1, 1 - slot, True)

        @pl.when((i + 1 == n_tiles) & (step + 1 < n_steps))
        def _():
            start(expert_of(step + 1), 0, 1 - slot, True)

        wait(expert, i, slot, True)

        @pl.when(before + i >= 2)
        def _():
            wait(expert, i, slot, False)

        valid = lax.broadcasted_iota(jnp.int32, (TILE, 1), 0) + i * TILE < n_rows
        r = jnp.where(valid, rbuf[slot], 0)
        dy = jnp.where(valid, dbuf[slot], 0)
        w1, w3, w2 = (jnp.concatenate([w[0, 0, t, 0] for w in (w_lo, w_hi)], axis=t // 2) for t in range(3))
        act_a = jnp.dot(r, w1, preferred_element_type=F32)
        act_b = jnp.dot(r, w3, preferred_element_type=F32)
        d_g = nt_dot(dy, w2)
        sig = 1.0 / (1.0 + jnp.exp(-act_a))
        silu = act_a * sig
        g = (silu * act_b).astype(BF16)
        d_up = (d_g * silu).astype(BF16)
        d_gate = (d_g * act_b * sig * (1.0 + act_a * (1.0 - sig))).astype(BF16)
        ybuf[slot] = jnp.dot(g, w2, preferred_element_type=F32).astype(BF16)
        drbuf[slot] = (nt_dot(d_gate, w1) + nt_dot(d_up, w3)).astype(BF16)
        start(expert, i, slot, False)
        for f in range(2):
            part = slice(f * half, (f + 1) * half)
            to = lax.rem(f + flip_ref[0], 2)
            for t, (lhs, rhs) in enumerate(((r[:, part], d_gate), (r[:, part], d_up), (g, dy[:, part]))):
                dw_ref[to, 0, t, 0] += tn_dot(lhs, rhs)
        return carry

    lax.fori_loop(0, n_tiles, tile, 0)
    done[0] = before + n_tiles

    @pl.when(step == n_steps - 1)
    def _():
        last = before + n_tiles - 1
        wait(expert, 0, lax.rem(last, 2), False)

        @pl.when(last >= 1)
        def _():
            wait(expert, 0, lax.rem(last + 1, 2), False)


def experts(rows, d_rows, weights, counts, flips, first, local_experts):
    d_model = rows.shape[2]
    n_fsdp, n_side, three, size, half, _ = weights.shape

    def expert_of(g):
        return g // size * local_experts + first + lax.rem(g, size)

    def side(g, flip):
        return lax.rem(g // size + flip[1], n_side)

    def w_spec(f):
        return pl.BlockSpec((1, 1, three, 1, half, half), lambda g, _, flip: (lax.rem(f + flip[0], n_fsdp), side(g, flip), 0, lax.rem(g, size), 0, 0))

    hbm = pl.BlockSpec(memory_space=pl.ANY)
    return pl.pallas_call(
        functools.partial(expert_kernel, expert_of=expert_of),
        grid_spec=pltpu.PrefetchScalarGridSpec(
            num_scalar_prefetch=2,
            grid=(n_side * size,),
            in_specs=[hbm, hbm, w_spec(0), w_spec(1)],
            out_specs=[hbm, hbm, pl.BlockSpec((n_fsdp, 1, three, 1, half, half), lambda g, _, flip: (0, side(g, flip), 0, lax.rem(g, size), 0, 0))],
            scratch_shapes=[pltpu.VMEM((2, TILE, d_model), BF16)] * 4 + [pltpu.SMEM((1,), jnp.int32)] + [pltpu.SemaphoreType.DMA((2, 2))] * 2,
        ),
        out_shape=[jax.ShapeDtypeStruct(rows.shape, BF16)] * 2 + [jax.ShapeDtypeStruct(weights.shape, F32)],
        input_output_aliases={2: 0, 3: 1},
        name='experts',
        **settings(56 * size, 100 * size),
    )(counts, flips, rows, d_rows, weights, weights)


def combine_kernel(start_ref, rows_ref, off_ref, y_hbm, dr_hbm, dest_ref, gate_ref, *refs, base, own):
    ybuf, dbuf, acc_y, acc_d, sem = refs[-5:]
    step = pl.program_id(0)
    n_blocks = pl.num_programs(0)
    b = step + base
    n_exp = rows_ref.shape[1]
    slot = lax.rem(step, 2)

    def total(blk):
        return start_ref[blk, n_exp - 1] + rows_ref[blk, n_exp - 1]

    def fetch(blk, which):
        def one(e, carry):
            n = pl.multiple_of(rows_ref[blk, e], ALIGN)
            dst = pl.multiple_of(start_ref[blk, e], ALIGN)
            src = pl.multiple_of(off_ref[blk, e], ALIGN)

            @pl.when(n > 0)
            def _():
                pltpu.make_async_copy(y_hbm.at[e, pl.ds(src, n), :], ybuf.at[which, pl.ds(dst, n), :], sem.at[0, which]).start()
                pltpu.make_async_copy(dr_hbm.at[e, pl.ds(src, n), :], dbuf.at[which, pl.ds(dst, n), :], sem.at[1, which]).start()

            return carry

        lax.fori_loop(0, n_exp, one, 0)

    @pl.when(step == 0)
    def _():
        ybuf[...] = jnp.zeros(ybuf.shape, BF16)
        dbuf[...] = jnp.zeros(dbuf.shape, BF16)
        fetch(b, 0)

    @pl.when(step + 1 < n_blocks)
    def _():
        fetch(b + 1, 1 - slot)

    n = pl.multiple_of(total(b), ALIGN)

    @pl.when(n > 0)
    def _():
        pltpu.make_async_copy(ybuf.at[slot, pl.ds(0, n), :], ybuf.at[slot, pl.ds(0, n), :], sem.at[0, slot]).wait()
        pltpu.make_async_copy(dbuf.at[slot, pl.ds(0, n), :], dbuf.at[slot, pl.ds(0, n), :], sem.at[1, slot]).wait()

    acc_y[...] = jnp.zeros(acc_y.shape, F32)
    acc_d[...] = jnp.zeros(acc_d.shape, F32)

    def tile(i, carry):
        first = pl.multiple_of(i * TILE, TILE)
        picked = one_hot(dest_ref, gate_ref, first)
        ones = jnp.where(picked > 0, 1.0, 0.0).astype(BF16)
        acc_y[...] += tn_dot(picked.astype(BF16), ybuf[slot, pl.ds(first, TILE), :])
        acc_d[...] += tn_dot(ones, dbuf[slot, pl.ds(first, TILE), :])
        return carry

    lax.fori_loop(0, (n + (TILE - 1)) // TILE, tile, 0)

    if not own:
        out_y, out_d = refs[:2]
        out_y[...] = acc_y[...]
        out_d[...] = acc_d[...]
        return
    more_y, more_d, h_ref, dout_ref, out_ref, dh_ref = refs[:6]
    hf = h_ref[...].astype(F32)
    out_ref[...] = (hf + (acc_y[...] + more_y[...])).astype(BF16)
    d_u = (acc_d[...] + more_d[...]).astype(BF16).astype(F32)
    inv = lax.rsqrt(jnp.mean(hf * hf, axis=-1, keepdims=True) + EPS)
    proj = jnp.mean(d_u * hf, axis=-1, keepdims=True)
    d_norm = (d_u * inv - hf * (inv * inv * inv * proj)).astype(BF16).astype(F32)
    dh_ref[...] = (dout_ref[...].astype(F32) + d_norm).astype(BF16)


def combine(y_rows, dr_rows, dest, gate, segs, base, n_blocks, extra):
    n_local, _, d_model = y_rows.shape
    top_k = dest.shape[1]
    buf_rows = block_rows(top_k, n_local)
    tok_spec = pl.BlockSpec((BLOCK, d_model), lambda b, *_: (b, 0))
    map_spec = pl.BlockSpec((1, top_k, BLOCK), lambda b, *_: (b + base, 0, 0))
    hbm = pl.BlockSpec(memory_space=pl.ANY)
    out = jax.ShapeDtypeStruct((n_blocks * BLOCK, d_model), BF16 if extra else F32)
    return pl.pallas_call(
        functools.partial(combine_kernel, base=base, own=bool(extra)),
        grid_spec=pltpu.PrefetchScalarGridSpec(
            num_scalar_prefetch=3,
            grid=(n_blocks,),
            in_specs=[hbm, hbm, map_spec, map_spec] + [tok_spec] * len(extra),
            out_specs=[tok_spec, tok_spec],
            scratch_shapes=[
                pltpu.VMEM((2, buf_rows, d_model), BF16),
                pltpu.VMEM((2, buf_rows, d_model), BF16),
                pltpu.VMEM((BLOCK, d_model), F32),
                pltpu.VMEM((BLOCK, d_model), F32),
                pltpu.SemaphoreType.DMA((2, 2)),
            ],
        ),
        out_shape=[out, out],
        name='combine',
        **settings(45, 120),
    )(*segs, y_rows, dr_rows, dest, gate, *extra)


def place_kernel(*refs, n_parts):
    for k, out_ref in enumerate(refs[-3:]):
        value = refs[0][k]
        for part_ref in refs[1:n_parts]:
            value = value + part_ref[k]
        out_ref[...] = value


def place(parts, held, first, n_total):
    three, size, rows, cols = parts[0].shape
    hbm = pl.BlockSpec(memory_space=pl.ANY)
    return pl.pallas_call(
        functools.partial(place_kernel, n_parts=len(parts)),
        grid=(size,),
        in_specs=[pl.BlockSpec((three, 1, rows, cols), lambda i: (0, i, 0, 0))] * len(parts) + [hbm] * len(held),
        out_specs=[pl.BlockSpec((1, rows, cols), lambda i: (first + i, 0, 0))] * three,
        out_shape=[jax.ShapeDtypeStruct((n_total, rows, cols), F32)] * three,
        input_output_aliases={len(parts) + k: k for k in range(len(held))},
        name='place',
        **settings(1, 12),
    )(*parts, *held)


CHUNKS = (3, 3)
CORES = 2


def solution(mesh):
    ep_size, fsdp_size = mesh.shape['ep'], mesh.shape['fsdp']
    tok_spec = P(('data', 'fsdp', 'ep'))
    in_specs = (tok_spec, P('fsdp'), P(None, None, 'fsdp'), P('ep', 'fsdp'), P('ep', 'fsdp'), P('ep', None, 'fsdp'), tok_spec, tok_spec, tok_spec, tok_spec)
    out_specs = (tok_spec, tok_spec, P(('data', 'ep'), 'fsdp'), P(('data', 'ep'), 'fsdp'), P(('data', 'ep'), None, 'fsdp'))

    def device_fn(tokens, w_qkv, w_out, w_gate, w_up, w_down, expert_idx, expert_slot, gate_wts, d_out):
        n_seq, seq_len, d_model = tokens.shape
        tok_count = n_seq * seq_len
        top_k = expert_idx.shape[2]
        local_experts, half, _ = w_gate.shape
        num_experts = local_experts * ep_size
        n_side = ep_size // CORES
        n_local = local_experts * n_side
        n_blocks = tok_count // BLOCK
        capacity = capacity_of(tok_count, top_k, num_experts)
        max_rows = -(-(CORES * (capacity + n_blocks * (ALIGN - 1))) // TILE) * TILE
        ep = lax.axis_index('ep')
        groups = [[c + CORES * i for i in range(fsdp_size * n_side)] for c in range(CORES)]

        fsdp, side = lax.axis_index('fsdp'), ep // CORES
        flips = jnp.stack([fsdp, side]).astype(jnp.int32)

        def swap(values):
            return lax.ppermute(values, 'ep', [(i, i ^ 1) for i in range(ep_size)])

        def swap_x(values):
            return lax.ppermute(values, 'ep', [(i, i ^ CORES) for i in range(ep_size)])

        def swap_y(values):
            return lax.ppermute(values, 'fsdp', [(i, i ^ 1) for i in range(fsdp_size)])

        def own_weights(part):
            return jnp.stack([w_gate[part], w_up[part], w_down[part]], axis=0)

        _, head_dim, _ = w_out.shape
        qkv_rows = w_qkv.transpose(1, 2, 3, 0).reshape(-1, half)
        qkv_rows = lax.dynamic_slice_in_dim(qkv_rows, ep * (3 * d_model // ep_size), 3 * d_model // ep_size, axis=0)
        out_rows = lax.dynamic_slice_in_dim(w_out.reshape(-1, half), ep * (d_model // ep_size), d_model // ep_size, axis=0)
        attn_w = lax.all_gather(jnp.concatenate([qkv_rows, out_rows], axis=0), ('fsdp', 'ep'), axis=0, tiled=False)
        attn_w = attn_w.reshape(fsdp_size, ep_size, -1, half)
        weights, first = [], 0
        for size in CHUNKS:
            mine = own_weights(slice(first, first + size))
            full = lax.all_gather(mine, ('fsdp', 'ep'), axis=0, tiled=False, axis_index_groups=groups)
            weights.append(full.reshape(fsdp_size, n_side, *mine.shape))
            first += size
        mid = first + (local_experts - first) // 2
        attn_w, w_a, w_b = lax.optimization_barrier((attn_w, own_weights(slice(first, mid)), own_weights(slice(mid, local_experts))))
        w_ax, w_ay, w_bx, w_by = swap_x(w_a), swap_y(w_a), swap_x(w_b), swap_y(w_b)

        dout_tok = d_out.reshape(tok_count, d_model)
        dout_other = swap(dout_tok)
        kept_ids = jnp.where(expert_slot >= 0, expert_idx, -1).transpose(0, 2, 1)
        all_ids = jnp.concatenate([kept_ids, swap(kept_ids)], axis=0)
        owner = all_ids // local_experts
        mine_too = (all_ids >= 0) & (lax.rem(owner, CORES) == lax.rem(ep, CORES))
        local_ids = jnp.where(mine_too, owner // CORES * local_experts + lax.rem(all_ids, local_experts), -1)
        dest, segs = route(local_ids, n_local)
        counts = jnp.sum(segs[1], axis=0)
        gate = gate_wts.transpose(0, 2, 1)
        gate = jnp.concatenate([gate, swap(gate)], axis=0).astype(F32)
        gate = gate.reshape(2 * n_seq, top_k, seq_len // BLOCK, BLOCK).transpose(0, 2, 1, 3).reshape(2 * n_blocks, top_k, BLOCK)

        tokens, dest, segs, counts, gate = lax.optimization_barrier((tokens, dest, segs, counts, gate))
        h_seq, qkv = attention(tokens, attn_w, head_dim)
        w_axy, w_byx = swap_y(w_ax), swap_x(w_by)
        w_rest = jnp.stack([jnp.concatenate(pair, axis=1) for pair in ((w_a, w_b), (w_ax, w_bx), (w_ay, w_by), (w_axy, w_byx))])
        w_rest = w_rest.reshape(fsdp_size, n_side, *w_rest.shape[1:])
        h_tok = h_seq.reshape(tok_count, d_model)
        h_other = swap(h_tok)
        held = dispatch(h_tok, dout_tok, dest, gate, segs, 0, [], n_local, max_rows)
        rows, d_rows = dispatch(h_other, dout_other, dest, gate, segs, n_blocks, held, n_local, max_rows)
        done, start = [], 0
        for n, size in enumerate(CHUNKS):
            rows, d_rows, d_w = experts(rows, d_rows, weights[n], counts, jnp.zeros_like(flips), start, local_experts)
            d_w = d_w.reshape(fsdp_size * n_side, *d_w.shape[2:])
            d_w = lax.psum_scatter(d_w, ('fsdp', 'ep'), scatter_dimension=0, tiled=False, axis_index_groups=groups)
            done.append(([d_w], start))
            start += size
            if n == 0:
                rows, d_rows, d_rest = experts(rows, d_rows, w_rest, counts, flips, first, local_experts)
                d_a, d_b = d_rest[:, :, :, :mid - first], d_rest[:, :, :, mid - first:]
                more_a, more_b = swap_x(d_a[:, 1]), swap_y(d_b[1])
                d_a, d_b = d_a[:, 0] + more_a, d_b[0] + more_b
                more_a, more_b = swap_y(d_a[1]), swap_x(d_b[1])
                done += [([d_a[0], more_a], first), ([d_b[0], more_b], mid)]
        sums = combine(rows, d_rows, dest, gate, segs, n_blocks, n_blocks, [])
        more = [swap(value) for value in sums]
        layer_out, d_h = combine(rows, d_rows, dest, gate, segs, 0, n_blocks, [*more, h_tok, dout_tok])
        d_tokens = attention_grad(d_h.reshape(n_seq, seq_len, d_model), tokens, qkv, attn_w, head_dim)
        d_ws = []
        for parts, where in done:
            d_ws = place(parts, d_ws, where, local_experts)
        return layer_out.reshape(n_seq, seq_len, d_model), d_tokens, *d_ws

    return jax.shard_map(device_fn, mesh=mesh, in_specs=in_specs, out_specs=out_specs, check_vma=False)
```

profile of v0, /device:TPU:7, one launch (start us, length us, event | category | flops | bytes accessed | tf_op | source)
XLA Modules:
  0.0 1586.1 jit_solution(7311856056896116668)
XLA Ops:
  7.2 1.8 copy-done
  9.1 0.9 constant_dynamic-slice_fusion.1
  10.0 1.0 constant_dynamic-slice_fusion
  11.0 2.2 pad_maximum_fusion.5
  13.2 0.0 all-gather.9.cloned.1.call-start
  13.3 3.4 slice_bitcast_fusion.10
  16.6 2.3 slice_bitcast_fusion.8
  18.9 2.5 pad_maximum_fusion.1
  21.5 0.8 copy-done.4
  22.3 0.1 copy-done.5
  22.4 0.8 collective-permute-start
  23.2 0.5 collective-permute-start.3
  23.7 3.6 pad_maximum_fusion.2
  27.3 0.0 reduce-scatter.9.cloned.1.call-start
  27.4 1.3 slice_bitcast_fusion.16
  28.6 1.3 slice_bitcast_fusion.15
  29.9 1.3 slice_bitcast_fusion.14
  31.2 2.1 pad_maximum_fusion.3
  33.3 0.7 pad_maximum_fusion.6
  34.1 1.0 fusion.4.loc_ref
  35.1 9.2 route.1
  44.3 2.8 copy.41
  47.1 3.8 copy.43
  50.9 2.8 copy.42
  53.7 1.9 slice_reduce_fusion
  55.6 1.3 slice_bitcast_fusion.20
  56.9 5.5 all-gather.7.cloned.1.call-done
  62.5 157.9 %attention.1 = (bf16[8,512,1024]{2,1,0:T(8,128)(2,1)}, bf16[8,512,3072]{2,1,0:T(8,128)(2,1)}) custom-call(bf16[8,512,1024]{2,1,0:T(8,128)(2,1)} %x_ref.1, bf16[2,4,1024,512]{3,2,1,0:T(8,128)(2,1)} %bitcast.109), custom_call_target="tpu_custom_call" | custom-call | flops 89999998976 | bytes 60000000 | tf_op jit(solution)/shard_map/attention/pallas_call | solution.py:83
  220.4 0.3 collective-permute-start.2
  220.7 46.1 %dispatch.2 = (bf16[16,3072,1024]{2,1,0:T(8,128)(2,1)}, bf16[16,3072,1024]{2,1,0:T(8,128)(2,1)}) custom-call(s32[32,16]{1,0:T(8,128)} %get-tuple-element.54.start_ref, s32[32,16]{1,0:T(8,128)} %get-tuple-element.55.rows_ref, s32[32,16]{1,0:T(8,128)} %get-tuple-element.56.off_ref, bf16[4096,1024]{1,0:T(8,128)(2,1)} %bitcast.96, bf16[4096,1024]{1,0:T(8,128)(2,1)} %bitcast.93, ...), custom_call_target="tpu_custom_call" | custom-call | flops 40000000000 | bytes 90000000 | tf_op jit(solution)/shard_map/dispatch/pallas_call | solution.py:306
  266.8 46.8 %dispatch.3 = (bf16[16,3072,1024]{2,1,0:T(8,128)(2,1)}, bf16[16,3072,1024]{2,1,0:T(8,128)(2,1)}) custom-call(s32[32,16]{1,0:T(8,128)} %get-tuple-element.54.start_ref, s32[32,16]{1,0:T(8,128)} %get-tuple-element.55.rows_ref, s32[32,16]{1,0:T(8,128)} %get-tuple-element.56.off_ref, ...), custom_call_target="tpu_custom_call", output_to_operand_aliasing={{0}: (7, {}), {1}: (8, {})} | custom-call | flops 40000000000 | bytes 90000000 | tf_op jit(solution)/shard_map/dispatch/pallas_call | solution.py:306
  313.6 0.5 broadcast_2_flip_ref.2.flip_ref
  314.2 127.4 %experts.3 = (bf16[16,3072,1024]{2,1,0:T(8,128)(2,1)}, bf16[16,3072,1024]{2,1,0:T(8,128)(2,1)}, f32[2,2,3,3,512,512]{5,4,3,2,1,0:T(8,128)}) custom-call(s32[16]{0:T(128)} %get-tuple-element.57.count_ref, s32[2]{0:T(128)} %broadcast_2_flip_ref.2.flip_ref, ...), custom_call_target="tpu_custom_call", output_to_operand_aliasing={{0}: (2, {}), {1}: (3, {})} | custom-call | flops 167999995904 | bytes 300000000 | tf_op jit(solution)/shard_map/experts/pallas_call | solution.py:425
  441.6 1.0 collective-permute-start.4
  442.7 51.8 %collective-permute-start.7 = (bf16[3,1,512,512]{3,2,1,0:T(8,128)(2,1)}, bf16[3,1,512,512]{3,2,1,0:T(8,128)(2,1)}, u32[]{:S(2)}, u32[]{:S(2)}) collective-permute-start(bf16[3,1,512,512]{3,2,1,0:T(8,128)(2,1)} %get-tuple-element.70), channel_id=1, source_target_pairs={{0,4},{4,0},{1,5},{5,1},{2,6},{6,2},{3,7},{7,3}} | collective-permute-start | bytes 4718600 | tf_op jit(solution)/shard_map/ppermute | solution.py:598
  494.6 67.3 %collective-permute-start.8 = (bf16[3,1,512,512]{3,2,1,0:T(8,128)(2,1)}, bf16[3,1,512,512]{3,2,1,0:T(8,128)(2,1)}, u32[]{:S(2)}, u32[]{:S(2)}) collective-permute-start(bf16[3,1,512,512]{3,2,1,0:T(8,128)(2,1)} %collective-permute-done.4), channel_id=1, source_target_pairs={{0,4},{4,0},{1,5},{5,1},{2,6},{6,2},{3,7},{7,3}} | collective-permute-start | bytes 4718600 | tf_op jit(solution)/shard_map/ppermute | solution.py:598
  561.8 1.5 collective-permute-start.9
  563.3 0.7 pad_add_fusion.1.flip_ref
  564.0 2.2 maximum_bitcast_fusion
  566.1 2.2 maximum_bitcast_fusion.1
  568.3 60.9 %collective-permute-done.6 = bf16[3,1,512,512]{3,2,1,0:T(8,128)(2,1)} collective-permute-done((bf16[3,1,512,512]{3,2,1,0:T(8,128)(2,1)}, bf16[3,1,512,512]{3,2,1,0:T(8,128)(2,1)}, u32[]{:S(2)}, u32[]{:S(2)}) %collective-permute-start.6) | collective-permute-done | bytes 1572896 | tf_op jit(solution)/shard_map/ppermute | solution.py:598
  629.3 2.2 maximum_bitcast_fusion.2
  631.4 50.3 %collective-permute-done.8 = bf16[3,1,512,512]{3,2,1,0:T(8,128)(2,1)} collective-permute-done((bf16[3,1,512,512]{3,2,1,0:T(8,128)(2,1)}, bf16[3,1,512,512]{3,2,1,0:T(8,128)(2,1)}, u32[]{:S(2)}, u32[]{:S(2)}) %collective-permute-start.8) | collective-permute-done | bytes 1572896 | tf_op jit(solution)/shard_map/ppermute | solution.py:598
  681.8 2.2 maximum_bitcast_fusion.3
  683.9 5.6 pad_maximum_fusion
  689.5 95.9 %experts.4 = (bf16[16,3072,1024]{2,1,0:T(8,128)(2,1)}, bf16[16,3072,1024]{2,1,0:T(8,128)(2,1)}, f32[2,2,3,2,512,512]{5,4,3,2,1,0:T(8,128)}) custom-call(s32[16]{0:T(128)} %get-tuple-element.57.count_ref, s32[2]{0:T(128)} %pad_add_fusion.1.flip_ref, bf16[16,3072,1024]{2,1,0:T(8,128)(2,1)} %get-tuple-element.67.r_hbm, ...), custom_call_target="tpu_custom_call", output_to_operand_aliasing={{0}: (2, {}), {1}: (3, {})} | custom-call | flops 112000000000 | bytes 200000000 | tf_op jit(solution)/shard_map/experts/pallas_call | solution.py:425
  785.4 158.6 %experts.5 = (bf16[16,3072,1024]{2,1,0:T(8,128)(2,1)}, bf16[16,3072,1024]{2,1,0:T(8,128)(2,1)}, f32[2,2,3,3,512,512]{5,4,3,2,1,0:T(8,128)}) custom-call(s32[16]{0:T(128)} %get-tuple-element.57.count_ref, s32[2]{0:T(128)} %broadcast_2_flip_ref.2.flip_ref, ...), custom_call_target="tpu_custom_call", output_to_operand_aliasing={{0}: (2, {}), {1}: (3, {})} | custom-call | flops 167999995904 | bytes 300000000 | tf_op jit(solution)/shard_map/experts/pallas_call | solution.py:425
  944.0 53.1 %combine.2 = (f32[4096,1024]{1,0:T(8,128)}, f32[4096,1024]{1,0:T(8,128)}) custom-call(s32[32,16]{1,0:T(8,128)} %get-tuple-element.54.start_ref, s32[32,16]{1,0:T(8,128)} %get-tuple-element.55.rows_ref, s32[32,16]{1,0:T(8,128)} %get-tuple-element.56.off_ref, bf16[16,3072,1024]{2,1,0:T(8,128)(2,1)} %get-tuple-element.73.y_hbm, ...), custom_call_target="tpu_custom_call" | custom-call | flops 44999999488 | bytes 120000000 | tf_op jit(solution)/shard_map/combine/pallas_call | solution.py:520
  997.2 0.5 collective-permute-start.11
  997.7 3.6 slice_bitcast_fusion
  1001.3 13.2 collective-permute-start.14
  1014.5 3.8 slice_bitcast_fusion.2
  1018.3 267.2 %collective-permute-done.14 = f32[2,3,1,512,512]{4,3,1,2,0:T(8,128)} collective-permute-done((f32[2,3,1,512,512]{4,3,1,2,0:T(8,128)S(1)}, f32[2,3,1,512,512]{4,3,1,2,0:T(8,128)}, u32[]{:S(2)}, u32[]{:S(2)}) %collective-permute-start.14) | collective-permute-done | bytes 6291488 | tf_op jit(solution)/shard_map/ppermute | solution.py:595
  1285.5 6.5 fusion
  1292.0 3.4 slice_bitcast_fusion.4
  1295.5 6.4 fusion.1
  1301.8 3.5 slice_bitcast_fusion.6
  1305.3 1.3 collective-permute-start.13
  1306.6 61.7 %combine.3 = (bf16[4096,1024]{1,0:T(8,128)(2,1)}, bf16[4096,1024]{1,0:T(8,128)(2,1)}) custom-call(s32[32,16]{1,0:T(8,128)} %get-tuple-element.54.start_ref, s32[32,16]{1,0:T(8,128)} %get-tuple-element.55.rows_ref, s32[32,16]{1,0:T(8,128)} %get-tuple-element.56.off_ref, bf16[16,3072,1024]{2,1,0:T(8,128)(2,1)} %get-tuple-element.73.y_hbm, ...), custom_call_target="tpu_custom_call" | custom-call | flops 44999999488 | bytes 120000000 | tf_op jit(solution)/shard_map/combine/pallas_call | solution.py:520
  1368.3 185.1 %attention_grad.1 = bf16[8,512,1024]{2,1,0:T(8,128)(2,1)} custom-call(bf16[8,512,1024]{2,1,0:T(8,128)(2,1)} %bitcast.112, bf16[8,512,1024]{2,1,0:T(8,128)(2,1)} %x_ref.1, bf16[8,512,3072]{2,1,0:T(8,128)(2,1)} %get-tuple-element.79.qkv_ref, bf16[2,4,1024,512]{3,2,1,0:T(8,128)(2,1)} %bitcast.110), custom_call_target="tpu_custom_call" | custom-call | flops 149999992832 | bytes 70000000 | tf_op jit(solution)/shard_map/attention_grad/pallas_call | solution.py:155
  1553.4 8.3 place.4
  1561.6 4.6 place.5
  1566.3 4.6 place.6
  1570.9 8.4 place.7
  (45 shorter events, 0.6 us)
Async XLA Ops:
  7.2 1.9 copy-start
  7.2 55.3 %all-gather.7.cloned.1.call-start = ((), (), s32[]{:S(2)}) async-start(), calls=%async_computation.2 | async-start | bytes 9437184 | tf_op jit(solution)/shard_map/all_gather | solution.py:607
  13.2 300.4 %all-gather.9.cloned.1.call-start = ((), (), s32[]{:S(2)}) async-start(), calls=%async_computation.3 | async-start | bytes 23592960 | tf_op jit(solution)/shard_map/all_gather | solution.py:612
  13.2 3.4 copy-start.2
  21.4 0.9 copy-start.4
  21.4 1.0 copy-start.5
  21.4 764.0 %all-gather.11.cloned.1.call-start = ((), (), s32[]{:S(2)}) async-start(), calls=%async_computation.4 | async-start | bytes 23592960 | tf_op jit(solution)/shard_map/all_gather | solution.py:612
  22.4 11.6 collective-permute-start
  23.2 10.1 collective-permute-start.1
  23.2 243.5 %collective-permute-start.3 = (bf16[4096,1024]{1,0:T(8,128)(2,1)}, bf16[4096,1024]{1,0:T(8,128)(2,1)}, u32[]{:S(2)}, u32[]{:S(2)}) collective-permute-start(bf16[4096,1024]{1,0:T(8,128)(2,1)} %bitcast.92), channel_id=1, source_target_pairs={{0,1},{1,0},{2,3},{3,2},{4,5},{5,4},{6,7},{7,6}} | collective-permute-start | bytes 25165832 | tf_op jit(solution)/shard_map/ppermute | solution.py:592
  27.3 1526.1 %reduce-scatter.9.cloned.1.call-start = ((), (), s32[]{:S(2)}) async-start(), calls=%async_computation.6 | async-start | bytes 47185920
  29.9 3.4 copy-start.6
  44.3 6.6 copy-start.3
  220.4 46.4 %collective-permute-start.2 = (bf16[4096,1024]{1,0:T(8,128)(2,1)}, bf16[4096,1024]{1,0:T(8,128)(2,1)}, u32[]{:S(2)}, u32[]{:S(2)}) collective-permute-start(bf16[4096,1024]{1,0:T(8,128)(2,1)} %bitcast.95), channel_id=1, source_target_pairs={{0,1},{1,0},{2,3},{3,2},{4,5},{5,4},{6,7},{7,6}} | collective-permute-start | bytes 25165832 | tf_op jit(solution)/shard_map/ppermute | solution.py:592
  441.6 1129.3 %reduce-scatter.7.cloned.1.call-start = ((), (), s32[]{:S(2)}) async-start(), calls=%async_computation.5 | async-start | bytes 47185920
  441.6 52.9 %collective-permute-start.4 = (bf16[3,1,512,512]{3,2,1,0:T(8,128)(2,1)}, bf16[3,1,512,512]{3,2,1,0:T(8,128)(2,1)}, u32[]{:S(2)}, u32[]{:S(2)}) collective-permute-start(bf16[3,1,512,512]{3,2,1,0:T(8,128)(2,1)} %get-tuple-element.69), channel_id=1, source_target_pairs={{0,2},{1,3},{2,0},{3,1},{4,6},{5,7},{6,4},{7,5}} | collective-permute-start | bytes 4718600 | tf_op jit(solution)/shard_map/ppermute | solution.py:595
  442.7 119.2 %collective-permute-start.7 = (bf16[3,1,512,512]{3,2,1,0:T(8,128)(2,1)}, bf16[3,1,512,512]{3,2,1,0:T(8,128)(2,1)}, u32[]{:S(2)}, u32[]{:S(2)}) collective-permute-start(bf16[3,1,512,512]{3,2,1,0:T(8,128)(2,1)} %get-tuple-element.70), channel_id=1, source_target_pairs={{0,4},{4,0},{1,5},{5,1},{2,6},{6,2},{3,7},{7,3}} | collective-permute-start | bytes 4718600 | tf_op jit(solution)/shard_map/ppermute | solution.py:598
  494.5 71.7 %collective-permute-start.5 = (bf16[3,1,512,512]{3,2,1,0:T(8,128)(2,1)}, bf16[3,1,512,512]{3,2,1,0:T(8,128)(2,1)}, u32[]{:S(2)}, u32[]{:S(2)}) collective-permute-start(bf16[3,1,512,512]{3,2,1,0:T(8,128)(2,1)} %get-tuple-element.70), channel_id=1, source_target_pairs={{0,2},{1,3},{2,0},{3,1},{4,6},{5,7},{6,4},{7,5}} | collective-permute-start | bytes 4718600 | tf_op jit(solution)/shard_map/ppermute | solution.py:595
  494.5 134.7 %collective-permute-start.6 = (bf16[3,1,512,512]{3,2,1,0:T(8,128)(2,1)}, bf16[3,1,512,512]{3,2,1,0:T(8,128)(2,1)}, u32[]{:S(2)}, u32[]{:S(2)}) collective-permute-start(bf16[3,1,512,512]{3,2,1,0:T(8,128)(2,1)} %get-tuple-element.69), channel_id=1, source_target_pairs={{0,4},{4,0},{1,5},{5,1},{2,6},{6,2},{3,7},{7,3}} | collective-permute-start | bytes 4718600 | tf_op jit(solution)/shard_map/ppermute | solution.py:598
  494.6 187.2 %collective-permute-start.8 = (bf16[3,1,512,512]{3,2,1,0:T(8,128)(2,1)}, bf16[3,1,512,512]{3,2,1,0:T(8,128)(2,1)}, u32[]{:S(2)}, u32[]{:S(2)}) collective-permute-start(bf16[3,1,512,512]{3,2,1,0:T(8,128)(2,1)} %collective-permute-done.4), channel_id=1, source_target_pairs={{0,4},{4,0},{1,5},{5,1},{2,6},{6,2},{3,7},{7,3}} | collective-permute-start | bytes 4718600 | tf_op jit(solution)/shard_map/ppermute | solution.py:598
  561.8 119.9 %collective-permute-start.9 = (bf16[3,1,512,512]{3,2,1,0:T(8,128)(2,1)}, bf16[3,1,512,512]{3,2,1,0:T(8,128)(2,1)}, u32[]{:S(2)}, u32[]{:S(2)}) collective-permute-start(bf16[3,1,512,512]{3,2,1,0:T(8,128)(2,1)} %collective-permute-done.7), channel_id=1, source_target_pairs={{0,2},{1,3},{2,0},{3,1},{4,6},{5,7},{6,4},{7,5}} | collective-permute-start | bytes 4718600 | tf_op jit(solution)/shard_map/ppermute | solution.py:595
  997.2 309.4 %collective-permute-start.10 = (f32[4096,1024]{1,0:T(8,128)}, f32[4096,1024]{1,0:T(8,128)}, u32[]{:S(2)}, u32[]{:S(2)}) collective-permute-start(f32[4096,1024]{1,0:T(8,128)} %get-tuple-element.75), channel_id=1, source_target_pairs={{0,1},{1,0},{2,3},{3,2},{4,5},{5,4},{6,7},{7,6}} | collective-permute-start | bytes 50331656 | tf_op jit(solution)/shard_map/ppermute | solution.py:592
  997.2 309.4 %collective-permute-start.11 = (f32[4096,1024]{1,0:T(8,128)}, f32[4096,1024]{1,0:T(8,128)}, u32[]{:S(2)}, u32[]{:S(2)}) collective-permute-start(f32[4096,1024]{1,0:T(8,128)} %get-tuple-element.76), channel_id=1, source_target_pairs={{0,1},{1,0},{2,3},{3,2},{4,5},{5,4},{6,7},{7,6}} | collective-permute-start | bytes 50331656 | tf_op jit(solution)/shard_map/ppermute | solution.py:592
  1001.3 284.2 %collective-permute-start.14 = (f32[2,3,1,512,512]{4,3,1,2,0:T(8,128)S(1)}, f32[2,3,1,512,512]{4,3,1,2,0:T(8,128)}, u32[]{:S(2)}, u32[]{:S(2)}) collective-permute-start(f32[2,3,1,512,512]{4,3,1,2,0:T(8,128)S(1)} %slice_bitcast_fusion), channel_id=1, source_target_pairs={{0,2},{1,3},{2,0},{3,1},{4,6},{5,7},{6,4},{7,5}} | collective-permute-start | bytes 18874376 | tf_op jit(solution)/shard_map/ppermute | solution.py:595
  1018.3 277.2 %collective-permute-start.12 = (f32[2,3,1,512,512]{4,3,1,2,0:T(8,128)S(1)}, f32[2,3,1,512,512]{4,3,1,2,0:T(8,128)}, u32[]{:S(2)}, u32[]{:S(2)}) collective-permute-start(f32[2,3,1,512,512]{4,3,1,2,0:T(8,128)S(1)} %slice_bitcast_fusion.2), channel_id=1, source_target_pairs={{0,4},{4,0},{1,5},{5,1},{2,6},{6,2},{3,7},{7,3}} | collective-permute-start | bytes 18874376 | tf_op jit(solution)/shard_map/ppermute | solution.py:598
  1295.4 266.2 %collective-permute-start.15 = (f32[3,1,512,512]{3,2,1,0:T(8,128)}, f32[3,1,512,512]{3,2,1,0:T(8,128)}, u32[]{:S(2)}, u32[]{:S(2)}) collective-permute-start(f32[3,1,512,512]{3,2,1,0:T(8,128)} %get-tuple-element.95), channel_id=1, source_target_pairs={{0,4},{4,0},{1,5},{5,1},{2,6},{6,2},{3,7},{7,3}} | collective-permute-start | bytes 9437192 | tf_op jit(solution)/shard_map/ppermute | solution.py:598
  1305.3 261.0 %collective-permute-start.13 = (f32[3,1,512,512]{3,2,1,0:T(8,128)}, f32[3,1,512,512]{3,2,1,0:T(8,128)}, u32[]{:S(2)}, u32[]{:S(2)}) collective-permute-start(f32[3,1,512,512]{3,2,1,0:T(8,128)} %get-tuple-element.97), channel_id=1, source_target_pairs={{0,2},{1,3},{2,0},{3,1},{4,6},{5,7},{6,4},{7,5}} | collective-permute-start | bytes 9437192 | tf_op jit(solution)/shard_map/ppermute | solution.py:595
  1570.9 8.4 copy-start.1
Sparse Core Ops, SparseCore 0:
  13.3 49.1 all-gather.6
  64.9 169.9 all-gather.8
  237.2 170.1 all-gather.10
  441.7 451.5 reduce-scatter.8
  944.2 531.0 reduce-scatter.6
where the time goes:
time: 1600 us; the launch traced here: 1590 us
  Pallas kernels  968 us (60%)
  waiting for transfers between devices  384 us (24%)
  starting transfers between devices  138 us (9%)
  other arithmetic  41.8 us (3%)
  local copies, waits for them, and re-layouts  39.7 us (2%)
    pallas_call x3, Pallas kernels, experts(): pl.pallas_call(functools.partial(expert_kernel, expert_of=expert_of), gri...  382 us
    ppermute x5, waiting for transfers between devices, swap_x(): return lax.ppermute(values, 'ep', [(i, i ^ CORES) for i in range(ep_size)])  267 us
    pallas_call x1, Pallas kernels, attention_grad(): pl.pallas_call(functools.partial(attention_grad_kernel, head_dim=head_dim...  185 us
    pallas_call x1, Pallas kernels, attention(): pl.pallas_call(functools.partial(attention_kernel, head_dim=head_dim), gr...  158 us
    ppermute x5, starting transfers between devices, swap_y(): return lax.ppermute(values, 'fsdp', [(i, i ^ 1) for i in range(fsdp_size)])  119 us
    pallas_call x2, Pallas kernels, combine(): pl.pallas_call(functools.partial(combine_kernel, base=base, own=bool(extr...  115 us
    ppermute x5, waiting for transfers between devices, swap_y(): return lax.ppermute(values, 'fsdp', [(i, i ^ 1) for i in range(fsdp_size)])  111 us
    pallas_call x2, Pallas kernels, dispatch(): pl.pallas_call(functools.partial(dispatch_kernel, base=base), grid_spec=p...  92.9 us
  transfers between devices with their start and end apart: 21, of which 4 were waited for; matrix products, arithmetic and copies ran while one was open for 5% of the time, Pallas kernels for 60%

commit v1 on v0

--- a/solution.py
+++ b/solution.py
@@ -638,20 +638,18 @@
         h_other = swap(h_tok)
         held = dispatch(h_tok, dout_tok, dest, gate, segs, 0, [], n_local, max_rows)
         rows, d_rows = dispatch(h_other, dout_other, dest, gate, segs, n_blocks, held, n_local, max_rows)
-        done, start = [], 0
+        rows, d_rows, d_rest = experts(rows, d_rows, w_rest, counts, flips, first, local_experts)
+        d_a, d_b = d_rest[:, :, :, :mid - first], d_rest[:, :, :, mid - first:]
+        more_a, more_b = swap_x(d_a[:, 1]), swap_y(d_b[1])
+        d_a, d_b = d_a[:, 0] + more_a, d_b[0] + more_b
+        more_a, more_b = swap_y(d_a[1]), swap_x(d_b[1])
+        done, start = [([d_a[0], more_a], first), ([d_b[0], more_b], mid)], 0
         for n, size in enumerate(CHUNKS):
             rows, d_rows, d_w = experts(rows, d_rows, weights[n], counts, jnp.zeros_like(flips), start, local_experts)
             d_w = d_w.reshape(fsdp_size * n_side, *d_w.shape[2:])
             d_w = lax.psum_scatter(d_w, ('fsdp', 'ep'), scatter_dimension=0, tiled=False, axis_index_groups=groups)
-            done.append(([d_w], start))
+            done.insert(0 if n == 0 else len(done), ([d_w], start))
             start += size
-            if n == 0:
-                rows, d_rows, d_rest = experts(rows, d_rows, w_rest, counts, flips, first, local_experts)
-                d_a, d_b = d_rest[:, :, :, :mid - first], d_rest[:, :, :, mid - first:]
-                more_a, more_b = swap_x(d_a[:, 1]), swap_y(d_b[1])
-                d_a, d_b = d_a[:, 0] + more_a, d_b[0] + more_b
-                more_a, more_b = swap_y(d_a[1]), swap_x(d_b[1])
-                done += [([d_a[0], more_a], first), ([d_b[0], more_b], mid)]
         sums = combine(rows, d_rows, dest, gate, segs, n_blocks, n_blocks, [])
         more = [swap(value) for value in sums]
         layer_out, d_h = combine(rows, d_rows, dest, gate, segs, 0, n_blocks, [*more, h_tok, dout_tok])

time: 1600 us -> 1600 us (level)
  waiting for transfers between devices: 384 us -> 463 us
  starting transfers between devices: 138 us -> 59.1 us
    ppermute x5, waiting for transfers between devices: 267 us -> 0.01 us  [swap_x(): return lax.ppermute(values, 'ep', [(i, i ^ CORES) for i in range(ep_size)])]
    ppermute x5, waiting for transfers between devices: 111 us -> 359 us  [swap_y(): return lax.ppermute(values, 'fsdp', [(i, i ^ 1) for i in range(fsdp_size)])]
    ppermute x5, starting transfers between devices: 119 us -> 3.46 us  [swap_y(): return lax.ppermute(values, 'fsdp', [(i, i ^ 1) for i in range(fsdp_size)])]
    unnamed x7, waiting for transfers between devices: 0.09 us -> 96.2 us
    ppermute x6, starting transfers between devices: 2.08 us -> 54.3 us  [swap(): return lax.ppermute(values, 'ep', [(i, i ^ 1) for i in range(ep_size)])]
    ppermute x5, starting transfers between devices: 17 us -> 0.52 us  [swap_x(): return lax.ppermute(values, 'ep', [(i, i ^ CORES) for i in range(ep_size)])]
  transfers between devices with their start and end apart: 21 -> 21, of which waited for: 4 -> 6; matrix products, arithmetic and copies ran while one was open for 5% -> 5% of each run, Pallas kernels for 60% -> 61%
where the time goes in v1:
time: 1600 us; the launch traced here: 1580 us
  Pallas kernels  967 us (60%)
  waiting for transfers between devices  463 us (29%)
  starting transfers between devices  59.1 us (4%)
  other arithmetic  41.4 us (3%)
  local copies, waits for them, and re-layouts  37.8 us (2%)
    pallas_call x3, Pallas kernels, experts(): pl.pallas_call(functools.partial(expert_kernel, expert_of=expert_of), gri...  381 us
    ppermute x5, waiting for transfers between devices, swap_y(): return lax.ppermute(values, 'fsdp', [(i, i ^ 1) for i in range(fsdp_size)])  359 us
    pallas_call x1, Pallas kernels, attention_grad(): pl.pallas_call(functools.partial(attention_grad_kernel, head_dim=head_dim...  185 us
    pallas_call x1, Pallas kernels, attention(): pl.pallas_call(functools.partial(attention_kernel, head_dim=head_dim), gr...  158 us
    pallas_call x2, Pallas kernels, combine(): pl.pallas_call(functools.partial(combine_kernel, base=base, own=bool(extr...  115 us
    unnamed x7, waiting for transfers between devices  96.2 us
    pallas_call x2, Pallas kernels, dispatch(): pl.pallas_call(functools.partial(dispatch_kernel, base=base), grid_spec=p...  93 us
    ppermute x6, starting transfers between devices, swap(): return lax.ppermute(values, 'ep', [(i, i ^ 1) for i in range(ep_size)])  54.3 us
  transfers between devices with their start and end apart: 21, of which 6 were waited for; matrix products, arithmetic and copies ran while one was open for 5% of the time, Pallas kernels for 61%

profile of v1, /device:TPU:7, one launch (start us, length us, event | category | flops | bytes accessed | tf_op | source)
XLA Modules:
  0.0 1582.8 jit_solution(12440392789635732671)
XLA Ops:
  7.2 1.1 constant_dynamic-slice_fusion
  8.4 0.8 copy-done
  9.2 1.1 pad_maximum_fusion.5
  10.4 3.4 slice_bitcast_fusion.10
  13.8 2.3 slice_bitcast_fusion.8
  16.1 2.5 pad_maximum_fusion.1
  18.6 0.8 collective-permute-start.1
  19.5 0.8 collective-permute-start
  20.4 1.3 slice_bitcast_fusion.16
  21.6 1.3 slice_bitcast_fusion.15
  22.9 1.3 slice_bitcast_fusion.14
  24.2 2.0 pad_maximum_fusion.3
  26.2 0.9 maximum_convert_fusion
  27.1 0.7 pad_maximum_fusion.6
  27.9 1.0 fusion.4.loc_ref
  28.9 9.2 route.1
  38.1 3.8 copy.41
  41.9 3.8 copy.42
  45.7 2.8 copy.43
  48.5 1.9 slice_reduce_fusion
  50.3 1.3 slice_bitcast_fusion.20
  51.7 7.9 all-gather.7.cloned.1.call-done
  59.6 157.9 %attention.1 = (bf16[8,512,1024]{2,1,0:T(8,128)(2,1)}, bf16[8,512,3072]{2,1,0:T(8,128)(2,1)}) custom-call(bf16[8,512,1024]{2,1,0:T(8,128)(2,1)} %x_ref.1, bf16[2,4,1024,512]{3,2,1,0:T(8,128)(2,1)} %bitcast.107), custom_call_target="tpu_custom_call" | custom-call | flops 89999998976 | bytes 60000000 | tf_op jit(solution)/shard_map/attention/pallas_call | solution.py:83
  217.5 0.3 collective-permute-start.2
  217.8 1.2 collective-permute-start.6
  219.0 0.2 collective-permute-start.4
  219.3 0.9 collective-permute-start.7
  220.1 3.6 pad_maximum_fusion.2
  223.7 0.5 reduce-scatter.9.cloned.1.call-start
  224.3 0.7 pad_add_fusion.1.flip_ref
  224.9 46.6 %collective-permute-done.6 = bf16[3,1,512,512]{3,2,1,0:T(8,128)(2,1)} collective-permute-done((bf16[3,1,512,512]{3,2,1,0:T(8,128)(2,1)}, bf16[3,1,512,512]{3,2,1,0:T(8,128)(2,1)}, u32[]{:S(2)}, u32[]{:S(2)}) %collective-permute-start.6) | collective-permute-done | bytes 1572896 | tf_op jit(solution)/shard_map/ppermute | solution.py:598
  271.5 0.1 collective-permute-start.5
  271.7 1.3 collective-permute-start.8
  273.0 65.9 %collective-permute-done.7 = bf16[3,1,512,512]{3,2,1,0:T(8,128)(2,1)} collective-permute-done((bf16[3,1,512,512]{3,2,1,0:T(8,128)(2,1)}, bf16[3,1,512,512]{3,2,1,0:T(8,128)(2,1)}, u32[]{:S(2)}, u32[]{:S(2)}) %collective-permute-start.7) | collective-permute-done | bytes 1572896 | tf_op jit(solution)/shard_map/ppermute | solution.py:598
  339.0 0.1 collective-permute-start.9
  339.1 46.1 %dispatch.2 = (bf16[16,3072,1024]{2,1,0:T(8,128)(2,1)}, bf16[16,3072,1024]{2,1,0:T(8,128)(2,1)}) custom-call(s32[32,16]{1,0:T(8,128)} %get-tuple-element.54.start_ref, s32[32,16]{1,0:T(8,128)} %get-tuple-element.55.rows_ref, s32[32,16]{1,0:T(8,128)} %get-tuple-element.56.off_ref, bf16[4096,1024]{1,0:T(8,128)(2,1)} %bitcast.96, bf16[4096,1024]{1,0:T(8,128)(2,1)} %bitcast.93, ...), custom_call_target="tpu_custom_call" | custom-call | flops 40000000000 | bytes 90000000 | tf_op jit(solution)/shard_map/dispatch/pallas_call | solution.py:306
  385.2 2.2 maximum_bitcast_fusion
  387.4 2.2 maximum_bitcast_fusion.2
  389.6 2.2 maximum_bitcast_fusion.1
  391.8 9.7 collective-permute-done.8
  401.5 2.2 maximum_bitcast_fusion.3
  403.7 5.5 pad_maximum_fusion
  409.1 46.9 %dispatch.3 = (bf16[16,3072,1024]{2,1,0:T(8,128)(2,1)}, bf16[16,3072,1024]{2,1,0:T(8,128)(2,1)}) custom-call(s32[32,16]{1,0:T(8,128)} %get-tuple-element.54.start_ref, s32[32,16]{1,0:T(8,128)} %get-tuple-element.55.rows_ref, s32[32,16]{1,0:T(8,128)} %get-tuple-element.56.off_ref, ...), custom_call_target="tpu_custom_call", output_to_operand_aliasing={{0}: (7, {}), {1}: (8, {})} | custom-call | flops 40000000000 | bytes 90000000 | tf_op jit(solution)/shard_map/dispatch/pallas_call | solution.py:306
  456.0 95.2 %experts.3 = (bf16[16,3072,1024]{2,1,0:T(8,128)(2,1)}, bf16[16,3072,1024]{2,1,0:T(8,128)(2,1)}, f32[2,2,3,2,512,512]{5,4,3,2,1,0:T(8,128)}) custom-call(s32[16]{0:T(128)} %get-tuple-element.57.count_ref, s32[2]{0:T(128)} %pad_add_fusion.1.flip_ref, bf16[16,3072,1024]{2,1,0:T(8,128)(2,1)} %get-tuple-element.65.r_hbm, ...), custom_call_target="tpu_custom_call", output_to_operand_aliasing={{0}: (2, {}), {1}: (3, {})} | custom-call | flops 112000000000 | bytes 200000000 | tf_op jit(solution)/shard_map/experts/pallas_call | solution.py:425
  551.3 0.5 broadcast_2_flip_ref.2.flip_ref
  551.8 127.0 %experts.4 = (bf16[16,3072,1024]{2,1,0:T(8,128)(2,1)}, bf16[16,3072,1024]{2,1,0:T(8,128)(2,1)}, f32[2,2,3,3,512,512]{5,4,3,2,1,0:T(8,128)}) custom-call(s32[16]{0:T(128)} %get-tuple-element.57.count_ref, s32[2]{0:T(128)} %broadcast_2_flip_ref.2.flip_ref, ...), custom_call_target="tpu_custom_call", output_to_operand_aliasing={{0}: (2, {}), {1}: (3, {})} | custom-call | flops 167999995904 | bytes 300000000 | tf_op jit(solution)/shard_map/experts/pallas_call | solution.py:425
  678.8 0.2 reduce-scatter.7.cloned.1.call-start
  679.1 158.7 %experts.5 = (bf16[16,3072,1024]{2,1,0:T(8,128)(2,1)}, bf16[16,3072,1024]{2,1,0:T(8,128)(2,1)}, f32[2,2,3,3,512,512]{5,4,3,2,1,0:T(8,128)}) custom-call(s32[16]{0:T(128)} %get-tuple-element.57.count_ref, s32[2]{0:T(128)} %broadcast_2_flip_ref.2.flip_ref, ...), custom_call_target="tpu_custom_call", output_to_operand_aliasing={{0}: (2, {}), {1}: (3, {})} | custom-call | flops 167999995904 | bytes 300000000 | tf_op jit(solution)/shard_map/experts/pallas_call | solution.py:425
  837.8 53.3 %combine.2 = (f32[4096,1024]{1,0:T(8,128)}, f32[4096,1024]{1,0:T(8,128)}) custom-call(s32[32,16]{1,0:T(8,128)} %get-tuple-element.54.start_ref, s32[32,16]{1,0:T(8,128)} %get-tuple-element.55.rows_ref, s32[32,16]{1,0:T(8,128)} %get-tuple-element.56.off_ref, bf16[16,3072,1024]{2,1,0:T(8,128)(2,1)} %get-tuple-element.73.y_hbm, ...), custom_call_target="tpu_custom_call" | custom-call | flops 44999999488 | bytes 120000000 | tf_op jit(solution)/shard_map/combine/pallas_call | solution.py:520
  891.0 52.3 %collective-permute-start.10 = (f32[4096,1024]{1,0:T(8,128)}, f32[4096,1024]{1,0:T(8,128)}, u32[]{:S(2)}, u32[]{:S(2)}) collective-permute-start(f32[4096,1024]{1,0:T(8,128)} %get-tuple-element.75), channel_id=1, source_target_pairs={{0,1},{1,0},{2,3},{3,2},{4,5},{5,4},{6,7},{7,6}} | collective-permute-start | bytes 50331656 | tf_op jit(solution)/shard_map/ppermute | solution.py:592
  943.4 3.6 slice_bitcast_fusion.2
  947.0 3.5 slice_bitcast_fusion
  950.6 236.5 %collective-permute-done.12 = f32[2,3,1,512,512]{4,3,1,2,0:T(8,128)} collective-permute-done((f32[2,3,1,512,512]{4,3,1,2,0:T(8,128)S(1)}, f32[2,3,1,512,512]{4,3,1,2,0:T(8,128)}, u32[]{:S(2)}, u32[]{:S(2)}) %collective-permute-start.12) | collective-permute-done | bytes 6291488 | tf_op jit(solution)/shard_map/ppermute | solution.py:598
  1187.1 6.5 fusion.1
  1193.6 3.4 slice_bitcast_fusion.6
  1197.0 6.5 fusion
  1203.5 3.4 slice_bitcast_fusion.4
  1206.9 62.0 %combine.3 = (bf16[4096,1024]{1,0:T(8,128)(2,1)}, bf16[4096,1024]{1,0:T(8,128)(2,1)}) custom-call(s32[32,16]{1,0:T(8,128)} %get-tuple-element.54.start_ref, s32[32,16]{1,0:T(8,128)} %get-tuple-element.55.rows_ref, s32[32,16]{1,0:T(8,128)} %get-tuple-element.56.off_ref, bf16[16,3072,1024]{2,1,0:T(8,128)(2,1)} %get-tuple-element.73.y_hbm, ...), custom_call_target="tpu_custom_call" | custom-call | flops 44999999488 | bytes 120000000 | tf_op jit(solution)/shard_map/combine/pallas_call | solution.py:520
  1268.9 184.8 %attention_grad.1 = bf16[8,512,1024]{2,1,0:T(8,128)(2,1)} custom-call(bf16[8,512,1024]{2,1,0:T(8,128)(2,1)} %bitcast.110, bf16[8,512,1024]{2,1,0:T(8,128)(2,1)} %x_ref.1, bf16[8,512,3072]{2,1,0:T(8,128)(2,1)} %get-tuple-element.79.qkv_ref, bf16[2,4,1024,512]{3,2,1,0:T(8,128)(2,1)} %bitcast.108), custom_call_target="tpu_custom_call" | custom-call | flops 149999992832 | bytes 70000000 | tf_op jit(solution)/shard_map/attention_grad/pallas_call | solution.py:155
  1453.7 8.3 place.4
  1462.0 4.8 place.5
  1466.9 4.6 place.6
  1471.5 96.1 %reduce-scatter.7.cloned.1.call-done = f32[1,3,3,512,512]{4,3,2,1,0:T(8,128)} async-done(((f32[4,3,3,512,512]{4,3,2,1,0:T(8,128)}), f32[1,3,3,512,512]{4,3,2,1,0:T(8,128)}) %reduce-scatter.7.cloned.1.call-update) | async-done | bytes 9437200
  1567.6 8.4 place.7
  (43 shorter events, 0.6 us)
Async XLA Ops:
  7.2 2.0 copy-start
  7.2 52.4 %all-gather.7.cloned.1.call-start = ((), (), s32[]{:S(2)}) async-start(), calls=%async_computation.2 | async-start | bytes 9437184 | tf_op jit(solution)/shard_map/all_gather | solution.py:607
  10.3 541.0 %all-gather.9.cloned.1.call-start = ((), (), s32[]{:S(2)}) async-start(), calls=%async_computation.3 | async-start | bytes 23592960 | tf_op jit(solution)/shard_map/all_gather | solution.py:612
  10.3 3.4 copy-start.2
  18.5 0.9 copy-start.4
  18.5 1.0 copy-start.5
  18.6 660.5 %all-gather.11.cloned.1.call-start = ((), (), s32[]{:S(2)}) async-start(), calls=%async_computation.4 | async-start | bytes 23592960 | tf_op jit(solution)/shard_map/all_gather | solution.py:612
  18.6 7.6 collective-permute-start.1
  19.5 8.3 collective-permute-start
  20.3 388.8 %collective-permute-start.3 = (bf16[4096,1024]{1,0:T(8,128)(2,1)}, bf16[4096,1024]{1,0:T(8,128)(2,1)}, u32[]{:S(2)}, u32[]{:S(2)}) collective-permute-start(bf16[4096,1024]{1,0:T(8,128)(2,1)} %bitcast.92), channel_id=1, source_target_pairs={{0,1},{1,0},{2,3},{3,2},{4,5},{5,4},{6,7},{7,6}} | collective-permute-start | bytes 25165832 | tf_op jit(solution)/shard_map/ppermute | solution.py:592
  38.1 7.6 copy-start.3
  217.5 191.6 %collective-permute-start.2 = (bf16[4096,1024]{1,0:T(8,128)(2,1)}, bf16[4096,1024]{1,0:T(8,128)(2,1)}, u32[]{:S(2)}, u32[]{:S(2)}) collective-permute-start(bf16[4096,1024]{1,0:T(8,128)(2,1)} %bitcast.95), channel_id=1, source_target_pairs={{0,1},{1,0},{2,3},{3,2},{4,5},{5,4},{6,7},{7,6}} | collective-permute-start | bytes 25165832 | tf_op jit(solution)/shard_map/ppermute | solution.py:592
  217.8 53.7 %collective-permute-start.6 = (bf16[3,1,512,512]{3,2,1,0:T(8,128)(2,1)}, bf16[3,1,512,512]{3,2,1,0:T(8,128)(2,1)}, u32[]{:S(2)}, u32[]{:S(2)}) collective-permute-start(bf16[3,1,512,512]{3,2,1,0:T(8,128)(2,1)} %get-tuple-element.67), channel_id=1, source_target_pairs={{0,4},{4,0},{1,5},{5,1},{2,6},{6,2},{3,7},{7,3}} | collective-permute-start | bytes 4718600 | tf_op jit(solution)/shard_map/ppermute | solution.py:598
  219.0 52.6 %collective-permute-start.4 = (bf16[3,1,512,512]{3,2,1,0:T(8,128)(2,1)}, bf16[3,1,512,512]{3,2,1,0:T(8,128)(2,1)}, u32[]{:S(2)}, u32[]{:S(2)}) collective-permute-start(bf16[3,1,512,512]{3,2,1,0:T(8,128)(2,1)} %get-tuple-element.67), channel_id=1, source_target_pairs={{0,2},{1,3},{2,0},{3,1},{4,6},{5,7},{6,4},{7,5}} | collective-permute-start | bytes 4718600 | tf_op jit(solution)/shard_map/ppermute | solution.py:595
  219.3 119.7 %collective-permute-start.7 = (bf16[3,1,512,512]{3,2,1,0:T(8,128)(2,1)}, bf16[3,1,512,512]{3,2,1,0:T(8,128)(2,1)}, u32[]{:S(2)}, u32[]{:S(2)}) collective-permute-start(bf16[3,1,512,512]{3,2,1,0:T(8,128)(2,1)} %get-tuple-element.68), channel_id=1, source_target_pairs={{0,4},{4,0},{1,5},{5,1},{2,6},{6,2},{3,7},{7,3}} | collective-permute-start | bytes 4718600 | tf_op jit(solution)/shard_map/ppermute | solution.py:598
  223.7 1230.0 %reduce-scatter.9.cloned.1.call-start = ((), (), s32[]{:S(2)}) async-start(), calls=%async_computation.6 | async-start | bytes 47185920
  271.5 118.0 %collective-permute-start.5 = (bf16[3,1,512,512]{3,2,1,0:T(8,128)(2,1)}, bf16[3,1,512,512]{3,2,1,0:T(8,128)(2,1)}, u32[]{:S(2)}, u32[]{:S(2)}) collective-permute-start(bf16[3,1,512,512]{3,2,1,0:T(8,128)(2,1)} %get-tuple-element.68), channel_id=1, source_target_pairs={{0,2},{1,3},{2,0},{3,1},{4,6},{5,7},{6,4},{7,5}} | collective-permute-start | bytes 4718600 | tf_op jit(solution)/shard_map/ppermute | solution.py:595
  271.7 129.8 %collective-permute-start.8 = (bf16[3,1,512,512]{3,2,1,0:T(8,128)(2,1)}, bf16[3,1,512,512]{3,2,1,0:T(8,128)(2,1)}, u32[]{:S(2)}, u32[]{:S(2)}) collective-permute-start(bf16[3,1,512,512]{3,2,1,0:T(8,128)(2,1)} %collective-permute-done.4), channel_id=1, source_target_pairs={{0,4},{4,0},{1,5},{5,1},{2,6},{6,2},{3,7},{7,3}} | collective-permute-start | bytes 4718600 | tf_op jit(solution)/shard_map/ppermute | solution.py:598
  339.0 62.5 %collective-permute-start.9 = (bf16[3,1,512,512]{3,2,1,0:T(8,128)(2,1)}, bf16[3,1,512,512]{3,2,1,0:T(8,128)(2,1)}, u32[]{:S(2)}, u32[]{:S(2)}) collective-permute-start(bf16[3,1,512,512]{3,2,1,0:T(8,128)(2,1)} %collective-permute-done.7), channel_id=1, source_target_pairs={{0,2},{1,3},{2,0},{3,1},{4,6},{5,7},{6,4},{7,5}} | collective-permute-start | bytes 4718600 | tf_op jit(solution)/shard_map/ppermute | solution.py:595
  678.8 888.8 %reduce-scatter.7.cloned.1.call-start = ((), (), s32[]{:S(2)}) async-start(), calls=%async_computation.5 | async-start | bytes 47185920
  891.0 315.9 %collective-permute-start.10 = (f32[4096,1024]{1,0:T(8,128)}, f32[4096,1024]{1,0:T(8,128)}, u32[]{:S(2)}, u32[]{:S(2)}) collective-permute-start(f32[4096,1024]{1,0:T(8,128)} %get-tuple-element.75), channel_id=1, source_target_pairs={{0,1},{1,0},{2,3},{3,2},{4,5},{5,4},{6,7},{7,6}} | collective-permute-start | bytes 50331656 | tf_op jit(solution)/shard_map/ppermute | solution.py:592
  943.4 263.6 %collective-permute-start.11 = (f32[4096,1024]{1,0:T(8,128)}, f32[4096,1024]{1,0:T(8,128)}, u32[]{:S(2)}, u32[]{:S(2)}) collective-permute-start(f32[4096,1024]{1,0:T(8,128)} %get-tuple-element.76), channel_id=1, source_target_pairs={{0,1},{1,0},{2,3},{3,2},{4,5},{5,4},{6,7},{7,6}} | collective-permute-start | bytes 50331656 | tf_op jit(solution)/shard_map/ppermute | solution.py:592
  947.0 240.1 %collective-permute-start.12 = (f32[2,3,1,512,512]{4,3,1,2,0:T(8,128)S(1)}, f32[2,3,1,512,512]{4,3,1,2,0:T(8,128)}, u32[]{:S(2)}, u32[]{:S(2)}) collective-permute-start(f32[2,3,1,512,512]{4,3,1,2,0:T(8,128)S(1)} %slice_bitcast_fusion.2), channel_id=1, source_target_pairs={{0,4},{4,0},{1,5},{5,1},{2,6},{6,2},{3,7},{7,3}} | collective-permute-start | bytes 18874376 | tf_op jit(solution)/shard_map/ppermute | solution.py:598
  950.6 246.5 %collective-permute-start.14 = (f32[2,3,1,512,512]{4,3,1,2,0:T(8,128)S(1)}, f32[2,3,1,512,512]{4,3,1,2,0:T(8,128)}, u32[]{:S(2)}, u32[]{:S(2)}) collective-permute-start(f32[2,3,1,512,512]{4,3,1,2,0:T(8,128)S(1)} %slice_bitcast_fusion), channel_id=1, source_target_pairs={{0,2},{1,3},{2,0},{3,1},{4,6},{5,7},{6,4},{7,5}} | collective-permute-start | bytes 18874376 | tf_op jit(solution)/shard_map/ppermute | solution.py:595
  1197.0 269.8 %collective-permute-start.13 = (f32[3,1,512,512]{3,2,1,0:T(8,128)}, f32[3,1,512,512]{3,2,1,0:T(8,128)}, u32[]{:S(2)}, u32[]{:S(2)}) collective-permute-start(f32[3,1,512,512]{3,2,1,0:T(8,128)} %get-tuple-element.97), channel_id=1, source_target_pairs={{0,2},{1,3},{2,0},{3,1},{4,6},{5,7},{6,4},{7,5}} | collective-permute-start | bytes 9437192 | tf_op jit(solution)/shard_map/ppermute | solution.py:595
  1206.9 255.1 %collective-permute-start.15 = (f32[3,1,512,512]{3,2,1,0:T(8,128)}, f32[3,1,512,512]{3,2,1,0:T(8,128)}, u32[]{:S(2)}, u32[]{:S(2)}) collective-permute-start(f32[3,1,512,512]{3,2,1,0:T(8,128)} %get-tuple-element.95), channel_id=1, source_target_pairs={{0,4},{4,0},{1,5},{5,1},{2,6},{6,2},{3,7},{7,3}} | collective-permute-start | bytes 9437192 | tf_op jit(solution)/shard_map/ppermute | solution.py:598
  1567.6 8.4 copy-start.1
Sparse Core Ops, SparseCore 0:
  10.4 49.1 all-gather.6
  62.0 180.0 all-gather.8
  244.4 240.3 all-gather.10
  678.9 494.6 reduce-scatter.8
  1176.5 391.0 reduce-scatter.6

commit v2 on v1

--- a/solution.py
+++ b/solution.py
@@ -222,13 +222,13 @@
 
 
 def one_hot(dest_ref, gate_ref, first_row):
-    rows = lax.broadcasted_iota(jnp.int32, (TILE, BLOCK), 0) + first_row
-    dest = dest_ref[0]
+    rows = lax.broadcasted_iota(jnp.int32, (TILE, BLOCK), 0).astype(F32).astype(BF16)
+    dest = jnp.clip(dest_ref[0] - first_row, -1, TILE).astype(F32).astype(BF16)
     gate = gate_ref[0]
-    picked = jnp.zeros((TILE, BLOCK), F32)
+    picked = jnp.zeros((TILE, BLOCK), BF16)
     for j in range(dest.shape[0]):
         picked = jnp.where(rows == dest[j:j + 1], gate[j:j + 1], picked)
-    return picked
+    return picked, jnp.where(picked > 0, jnp.ones_like(picked), jnp.zeros_like(picked))
 
 
 def dispatch_kernel(start_ref, rows_ref, off_ref, h_ref, dout_ref, dest_ref, gate_ref, *refs, base):
@@ -259,10 +259,9 @@
 
     def tile(i, carry):
         first = pl.multiple_of(i * TILE, TILE)
-        picked = one_hot(dest_ref, gate_ref, first)
-        ones = jnp.where(picked > 0, 1.0, 0.0).astype(BF16)
+        picked, ones = one_hot(dest_ref, gate_ref, first)
         rbuf[slot, pl.ds(first, TILE), :] = jnp.dot(ones, u_s[...], preferred_element_type=F32).astype(BF16)
-        dbuf[slot, pl.ds(first, TILE), :] = jnp.dot(picked.astype(BF16), dout_ref[...], preferred_element_type=F32).astype(BF16)
+        dbuf[slot, pl.ds(first, TILE), :] = jnp.dot(picked, dout_ref[...], preferred_element_type=F32).astype(BF16)
         return carry
 
     lax.fori_loop(0, (total(b) + (TILE - 1)) // TILE, tile, 0)
@@ -324,7 +323,7 @@
     )(*segs, h_tok, dout_tok, dest, gate, *held)
 
 
-def expert_kernel(count_ref, flip_ref, r_hbm, d_hbm, w_lo, w_hi, y_hbm, dr_hbm, dw_ref, rbuf, dbuf, ybuf, drbuf, done, in_sem, out_sem, *, expert_of):
+def expert_kernel(count_ref, flip_ref, r_hbm, d_hbm, w_lo, w_hi, y_hbm, dr_hbm, dw_ref, rbuf, dbuf, ybuf, drbuf, done, in_sem, out_sem, *, expert_of, x_first):
     step = pl.program_id(0)
     n_steps = pl.num_programs(0)
     expert = expert_of(step)
@@ -376,7 +375,7 @@
         valid = lax.broadcasted_iota(jnp.int32, (TILE, 1), 0) + i * TILE < n_rows
         r = jnp.where(valid, rbuf[slot], 0)
         dy = jnp.where(valid, dbuf[slot], 0)
-        w1, w3, w2 = (jnp.concatenate([w[0, 0, t, 0] for w in (w_lo, w_hi)], axis=t // 2) for t in range(3))
+        w1, w3, w2 = (jnp.concatenate([w[0, t, 0] for w in (w_lo, w_hi)], axis=t // 2) for t in range(3))
         act_a = jnp.dot(r, w1, preferred_element_type=F32)
         act_b = jnp.dot(r, w3, preferred_element_type=F32)
         d_g = nt_dot(dy, w2)
@@ -392,7 +391,7 @@
             part = slice(f * half, (f + 1) * half)
             to = lax.rem(f + flip_ref[0], 2)
             for t, (lhs, rhs) in enumerate(((r[:, part], d_gate), (r[:, part], d_up), (g, dy[:, part]))):
-                dw_ref[to, 0, t, 0] += tn_dot(lhs, rhs)
+                dw_ref[(0, to, t, 0) if x_first else (to, 0, t, 0)] += tn_dot(lhs, rhs)
         return carry
 
     lax.fori_loop(0, n_tiles, tile, 0)
@@ -408,9 +407,11 @@
             wait(expert, 0, lax.rem(last + 1, 2), False)
 
 
-def experts(rows, d_rows, weights, counts, flips, first, local_experts):
+def experts(rows, d_rows, weights, counts, flips, first, local_experts, x_first=False):
     d_model = rows.shape[2]
-    n_fsdp, n_side, three, size, half, _ = weights.shape
+    n_owners, three, size, half, _ = weights.shape
+    n_fsdp = d_model // half
+    n_side = n_owners // n_fsdp
 
     def expert_of(g):
         return g // size * local_experts + first + lax.rem(g, size)
@@ -419,19 +420,25 @@
         return lax.rem(g // size + flip[1], n_side)
 
     def w_spec(f):
-        return pl.BlockSpec((1, 1, three, 1, half, half), lambda g, _, flip: (lax.rem(f + flip[0], n_fsdp), side(g, flip), 0, lax.rem(g, size), 0, 0))
+        return pl.BlockSpec((1, three, 1, half, half), lambda g, _, flip: (lax.rem(f + flip[0], n_fsdp) * n_side + side(g, flip), 0, lax.rem(g, size), 0, 0))
+
+    def dw_index(g, _, flip):
+        place = (side(g, flip), 0) if x_first else (0, side(g, flip))
+        return (*place, 0, lax.rem(g, size), 0, 0)
 
     hbm = pl.BlockSpec(memory_space=pl.ANY)
+    grads = (n_side, n_fsdp) if x_first else (n_fsdp, n_side)
+    dw_block = (1, n_fsdp) if x_first else (n_fsdp, 1)
     return pl.pallas_call(
-        functools.partial(expert_kernel, expert_of=expert_of),
+        functools.partial(expert_kernel, expert_of=expert_of, x_first=x_first),
         grid_spec=pltpu.PrefetchScalarGridSpec(
             num_scalar_prefetch=2,
             grid=(n_side * size,),
             in_specs=[hbm, hbm, w_spec(0), w_spec(1)],
-            out_specs=[hbm, hbm, pl.BlockSpec((n_fsdp, 1, three, 1, half, half), lambda g, _, flip: (0, side(g, flip), 0, lax.rem(g, size), 0, 0))],
+            out_specs=[hbm, hbm, pl.BlockSpec((*dw_block, three, 1, half, half), dw_index)],
             scratch_shapes=[pltpu.VMEM((2, TILE, d_model), BF16)] * 4 + [pltpu.SMEM((1,), jnp.int32)] + [pltpu.SemaphoreType.DMA((2, 2))] * 2,
         ),
-        out_shape=[jax.ShapeDtypeStruct(rows.shape, BF16)] * 2 + [jax.ShapeDtypeStruct(weights.shape, F32)],
+        out_shape=[jax.ShapeDtypeStruct(rows.shape, BF16)] * 2 + [jax.ShapeDtypeStruct((*grads, three, size, half, half), F32)],
         input_output_aliases={2: 0, 3: 1},
         name='experts',
         **settings(56 * size, 100 * size),
@@ -486,9 +493,8 @@
 
     def tile(i, carry):
         first = pl.multiple_of(i * TILE, TILE)
-        picked = one_hot(dest_ref, gate_ref, first)
-        ones = jnp.where(picked > 0, 1.0, 0.0).astype(BF16)
-        acc_y[...] += tn_dot(picked.astype(BF16), ybuf[slot, pl.ds(first, TILE), :])
+        picked, ones = one_hot(dest_ref, gate_ref, first)
+        acc_y[...] += tn_dot(picked, ybuf[slot, pl.ds(first, TILE), :])
         acc_d[...] += tn_dot(ones, dbuf[slot, pl.ds(first, TILE), :])
         return carry
 
@@ -561,7 +567,7 @@
     )(*parts, *held)
 
 
-CHUNKS = (3, 3)
+CHUNKS = (2, 4)
 CORES = 2
 
 
@@ -610,7 +616,7 @@
         for size in CHUNKS:
             mine = own_weights(slice(first, first + size))
             full = lax.all_gather(mine, ('fsdp', 'ep'), axis=0, tiled=False, axis_index_groups=groups)
-            weights.append(full.reshape(fsdp_size, n_side, *mine.shape))
+            weights.append(full)
             first += size
         mid = first + (local_experts - first) // 2
         attn_w, w_a, w_b = lax.optimization_barrier((attn_w, own_weights(slice(first, mid)), own_weights(slice(mid, local_experts))))
@@ -626,22 +632,23 @@
         dest, segs = route(local_ids, n_local)
         counts = jnp.sum(segs[1], axis=0)
         gate = gate_wts.transpose(0, 2, 1)
-        gate = jnp.concatenate([gate, swap(gate)], axis=0).astype(F32)
+        gate = jnp.concatenate([gate, swap(gate)], axis=0)
         gate = gate.reshape(2 * n_seq, top_k, seq_len // BLOCK, BLOCK).transpose(0, 2, 1, 3).reshape(2 * n_blocks, top_k, BLOCK)
 
         tokens, dest, segs, counts, gate = lax.optimization_barrier((tokens, dest, segs, counts, gate))
         h_seq, qkv = attention(tokens, attn_w, head_dim)
         w_axy, w_byx = swap_y(w_ax), swap_x(w_by)
-        w_rest = jnp.stack([jnp.concatenate(pair, axis=1) for pair in ((w_a, w_b), (w_ax, w_bx), (w_ay, w_by), (w_axy, w_byx))])
-        w_rest = w_rest.reshape(fsdp_size, n_side, *w_rest.shape[1:])
+        w_a = jnp.stack([w_a, w_ax, w_ay, w_axy])
+        w_b = jnp.stack([w_b, w_bx, w_by, w_byx])
         h_tok = h_seq.reshape(tok_count, d_model)
         h_other = swap(h_tok)
         held = dispatch(h_tok, dout_tok, dest, gate, segs, 0, [], n_local, max_rows)
         rows, d_rows = dispatch(h_other, dout_other, dest, gate, segs, n_blocks, held, n_local, max_rows)
-        rows, d_rows, d_rest = experts(rows, d_rows, w_rest, counts, flips, first, local_experts)
-        d_a, d_b = d_rest[:, :, :, :mid - first], d_rest[:, :, :, mid - first:]
-        more_a, more_b = swap_x(d_a[:, 1]), swap_y(d_b[1])
-        d_a, d_b = d_a[:, 0] + more_a, d_b[0] + more_b
+        rows, d_rows, d_a = experts(rows, d_rows, w_a, counts, flips, first, local_experts, x_first=True)
+        more_a = swap_x(d_a[1])
+        rows, d_rows, d_b = experts(rows, d_rows, w_b, counts, flips, mid, local_experts)
+        more_b = swap_y(d_b[1])
+        d_a, d_b = d_a[0] + more_a, d_b[0] + more_b
         more_a, more_b = swap_y(d_a[1]), swap_x(d_b[1])
         done, start = [([d_a[0], more_a], first), ([d_b[0], more_b], mid)], 0
         for n, size in enumerate(CHUNKS):

time: 1600 us -> 1570 us (0.981)
  Pallas kernels: 967 us -> 951 us
    ppermute x5, waiting for transfers between devices: 0.01 us -> 266 us  [swap_x(): return lax.ppermute(values, 'ep', [(i, i ^ CORES) for i in range(ep_size)])]
    ppermute x5, waiting for transfers between devices: 359 us -> 153 us  [swap_y(): return lax.ppermute(values, 'fsdp', [(i, i ^ 1) for i in range(fsdp_size)])]
    unnamed x7, waiting for transfers between devices: 96.2 us -> 33.2 us
    pallas_call x3 -> x4, Pallas kernels: 381 us -> 383 us  [experts(): pl.pallas_call(functools.partial(expert_kernel, expert_of=expert_of, x_fi...]
  transfers between devices with their start and end apart: 21 -> 21, of which waited for: 6 -> 7; matrix products, arithmetic and copies ran while one was open for 5% -> 5% of each run, Pallas kernels for 61% -> 61%
where the time goes in v2:
time: 1570 us; the launch traced here: 1560 us
  Pallas kernels  951 us (61%)
  waiting for transfers between devices  458 us (29%)
  starting transfers between devices  55.7 us (4%)
  local copies, waits for them, and re-layouts  43.8 us (3%)
  other arithmetic  33.6 us (2%)
    pallas_call x4, Pallas kernels, experts(): pl.pallas_call(functools.partial(expert_kernel, expert_of=expert_of, x_fi...  383 us
    ppermute x5, waiting for transfers between devices, swap_x(): return lax.ppermute(values, 'ep', [(i, i ^ CORES) for i in range(ep_size)])  266 us
    pallas_call x1, Pallas kernels, attention_grad(): pl.pallas_call(functools.partial(attention_grad_kernel, head_dim=head_dim...  185 us
    pallas_call x1, Pallas kernels, attention(): pl.pallas_call(functools.partial(attention_kernel, head_dim=head_dim), gr...  158 us
    ppermute x5, waiting for transfers between devices, swap_y(): return lax.ppermute(values, 'fsdp', [(i, i ^ 1) for i in range(fsdp_size)])  153 us
    pallas_call x2, Pallas kernels, combine(): pl.pallas_call(functools.partial(combine_kernel, base=base, own=bool(extr...  108 us
    pallas_call x2, Pallas kernels, dispatch(): pl.pallas_call(functools.partial(dispatch_kernel, base=base), grid_spec=p...  84.8 us
    ppermute x6, starting transfers between devices, swap(): return lax.ppermute(values, 'ep', [(i, i ^ 1) for i in range(ep_size)])  51.6 us
  transfers between devices with their start and end apart: 21, of which 7 were waited for; matrix products, arithmetic and copies ran while one was open for 5% of the time, Pallas kernels for 61%

profile of v2, /device:TPU:7, one launch (start us, length us, event | category | flops | bytes accessed | tf_op | source)
XLA Modules:
  0.0 1557.0 jit_solution(2847787007750623683)
XLA Ops:
  7.2 1.1 constant_dynamic-slice_fusion
  8.4 0.8 copy-done
  9.2 1.0 pad_maximum_fusion.6
  10.3 1.3 slice_bitcast_fusion.13
  11.6 1.7 slice_bitcast_fusion.11
  13.4 2.0 pad_maximum_fusion.3
  15.5 0.7 collective-permute-start.1
  16.2 0.5 collective-permute-start.3
  16.7 1.9 slice_bitcast_fusion.10
  18.6 2.5 slice_bitcast_fusion.8
  21.1 3.1 pad_maximum_fusion.2
  24.3 1.3 slice_bitcast_fusion.16
  25.6 1.3 slice_bitcast_fusion.15
  26.9 1.3 slice_bitcast_fusion.14
  28.2 0.3 pad_maximum_fusion.4
  28.5 0.7 fusion.7
  29.2 1.0 fusion.4.loc_ref
  30.3 9.2 route.1
  39.5 3.8 copy.49
  43.2 3.8 copy.50
  47.0 1.9 slice_reduce_fusion
  48.9 3.8 copy.51
  52.6 1.3 slice_bitcast_fusion.20
  54.0 5.5 all-gather.7.cloned.1.call-done
  59.5 157.9 %attention.1 = (bf16[8,512,1024]{2,1,0:T(8,128)(2,1)}, bf16[8,512,3072]{2,1,0:T(8,128)(2,1)}) custom-call(bf16[8,512,1024]{2,1,0:T(8,128)(2,1)} %x_ref.1, bf16[2,4,1024,512]{3,2,1,0:T(8,128)(2,1)} %bitcast.127), custom_call_target="tpu_custom_call" | custom-call | flops 89999998976 | bytes 60000000 | tf_op jit(solution)/shard_map/attention/pallas_call | solution.py:83
  217.5 0.3 collective-permute-start.2
  217.7 1.2 collective-permute-start.5
  218.9 0.3 collective-permute-start.4
  219.2 0.9 collective-permute-start.8
  220.1 0.6 pad_add_fusion.1.flip_ref
  220.7 67.2 %collective-permute-done.5 = bf16[3,1,512,512]{3,2,0,1:T(8,128)(2,1)} collective-permute-done((bf16[3,1,512,512]{3,2,0,1:T(8,128)(2,1)S(1)}, bf16[3,1,512,512]{3,2,0,1:T(8,128)(2,1)}, u32[]{:S(2)}, u32[]{:S(2)}) %collective-permute-start.5) | collective-permute-done | bytes 1572896 | tf_op jit(solution)/shard_map/ppermute | solution.py:604
  287.9 0.9 collective-permute-start.7
  288.8 0.2 collective-permute-done.4
  289.0 0.4 collective-permute-start.6
  289.4 60.8 %collective-permute-done.8 = bf16[3,1,512,512]{3,2,0,1:T(8,128)(2,1)} collective-permute-done((bf16[3,1,512,512]{3,2,0,1:T(8,128)(2,1)S(1)}, bf16[3,1,512,512]{3,2,0,1:T(8,128)(2,1)}, u32[]{:S(2)}, u32[]{:S(2)}) %collective-permute-start.8) | collective-permute-done | bytes 1572896 | tf_op jit(solution)/shard_map/ppermute | solution.py:604
  350.2 0.1 collective-permute-start.9
  350.3 42.0 %dispatch.2 = (bf16[16,3072,1024]{2,1,0:T(8,128)(2,1)}, bf16[16,3072,1024]{2,1,0:T(8,128)(2,1)}) custom-call(s32[32,16]{1,0:T(8,128)} %get-tuple-element.57.start_ref, s32[32,16]{1,0:T(8,128)} %get-tuple-element.58.rows_ref, s32[32,16]{1,0:T(8,128)} %get-tuple-element.59.off_ref, bf16[4096,1024]{1,0:T(8,128)(2,1)} %bitcast.110, ...), custom_call_target="tpu_custom_call" | custom-call | flops 40000000000 | bytes 90000000 | tf_op jit(solution)/shard_map/dispatch/pallas_call | solution.py:305
  392.3 25.3 %collective-permute-done.6 = bf16[3,1,512,512]{3,2,0,1:T(8,128)(2,1)} collective-permute-done((bf16[3,1,512,512]{3,2,0,1:T(8,128)(2,1)}, bf16[3,1,512,512]{3,2,0,1:T(8,128)(2,1)}, u32[]{:S(2)}, u32[]{:S(2)}) %collective-permute-start.6) | collective-permute-done | bytes 1572896 | tf_op jit(solution)/shard_map/ppermute | solution.py:604
  417.6 5.8 pad_maximum_fusion.w_lo.w_hi
  423.3 5.8 pad_maximum_fusion.1.w_lo.w_hi
  429.1 42.8 %dispatch.3 = (bf16[16,3072,1024]{2,1,0:T(8,128)(2,1)}, bf16[16,3072,1024]{2,1,0:T(8,128)(2,1)}) custom-call(s32[32,16]{1,0:T(8,128)} %get-tuple-element.57.start_ref, s32[32,16]{1,0:T(8,128)} %get-tuple-element.58.rows_ref, s32[32,16]{1,0:T(8,128)} %get-tuple-element.59.off_ref, ...), custom_call_target="tpu_custom_call", output_to_operand_aliasing={{0}: (7, {}), {1}: (8, {})} | custom-call | flops 40000000000 | bytes 90000000 | tf_op jit(solution)/shard_map/dispatch/pallas_call | solution.py:305
  472.0 52.0 %experts.4 = (bf16[16,3072,1024]{2,1,0:T(8,128)(2,1)}, bf16[16,3072,1024]{2,1,0:T(8,128)(2,1)}, f32[2,2,3,1,512,512]{5,4,3,2,1,0:T(8,128)}) custom-call(s32[16]{0:T(128)} %get-tuple-element.60.count_ref, s32[2]{0:T(128)} %pad_add_fusion.1.flip_ref, bf16[16,3072,1024]{2,1,0:T(8,128)(2,1)} %get-tuple-element.68.r_hbm, ...), custom_call_target="tpu_custom_call", output_to_operand_aliasing={{0}: (2, {}), {1}: (3, {})} | custom-call | flops 56000000000 | bytes 100000000 | tf_op jit(solution)/shard_map/experts/pallas_call | solution.py:432
  524.0 46.0 %experts.5 = (bf16[16,3072,1024]{2,1,0:T(8,128)(2,1)}, bf16[16,3072,1024]{2,1,0:T(8,128)(2,1)}, f32[2,2,3,1,512,512]{5,4,3,2,1,0:T(8,128)}) custom-call(s32[16]{0:T(128)} %get-tuple-element.60.count_ref, s32[2]{0:T(128)} %pad_add_fusion.1.flip_ref, bf16[16,3072,1024]{2,1,0:T(8,128)(2,1)} %get-tuple-element.71.r_hbm, ...), custom_call_target="tpu_custom_call", output_to_operand_aliasing={{0}: (2, {}), {1}: (3, {})} | custom-call | flops 56000000000 | bytes 100000000 | tf_op jit(solution)/shard_map/experts/pallas_call | solution.py:432
  570.0 0.5 broadcast_2_flip_ref.2.flip_ref
  570.5 83.5 %experts.6 = (bf16[16,3072,1024]{2,1,0:T(8,128)(2,1)}, bf16[16,3072,1024]{2,1,0:T(8,128)(2,1)}, f32[2,2,3,2,512,512]{5,4,3,2,1,0:T(8,128)}) custom-call(s32[16]{0:T(128)} %get-tuple-element.60.count_ref, s32[2]{0:T(128)} %broadcast_2_flip_ref.2.flip_ref, ...), custom_call_target="tpu_custom_call", output_to_operand_aliasing={{0}: (2, {}), {1}: (3, {})} | custom-call | flops 112000000000 | bytes 200000000 | tf_op jit(solution)/shard_map/experts/pallas_call | solution.py:432
  654.1 201.5 %experts.7 = (bf16[16,3072,1024]{2,1,0:T(8,128)(2,1)}, bf16[16,3072,1024]{2,1,0:T(8,128)(2,1)}, f32[2,2,3,4,512,512]{5,4,3,2,1,0:T(8,128)}) custom-call(s32[16]{0:T(128)} %get-tuple-element.60.count_ref, s32[2]{0:T(128)} %broadcast_2_flip_ref.2.flip_ref, ...), custom_call_target="tpu_custom_call", output_to_operand_aliasing={{0}: (2, {}), {1}: (3, {})} | custom-call | flops 224000000000 | bytes 400000000 | tf_op jit(solution)/shard_map/experts/pallas_call | solution.py:432
  855.7 49.2 %combine.2 = (f32[4096,1024]{1,0:T(8,128)}, f32[4096,1024]{1,0:T(8,128)}) custom-call(s32[32,16]{1,0:T(8,128)} %get-tuple-element.57.start_ref, s32[32,16]{1,0:T(8,128)} %get-tuple-element.58.rows_ref, s32[32,16]{1,0:T(8,128)} %get-tuple-element.59.off_ref, bf16[16,3072,1024]{2,1,0:T(8,128)(2,1)} %get-tuple-element.78.y_hbm, ...), custom_call_target="tpu_custom_call" | custom-call | flops 44999999488 | bytes 120000000 | tf_op jit(solution)/shard_map/combine/pallas_call | solution.py:526
  904.9 50.1 %collective-permute-start.10 = (f32[4096,1024]{1,0:T(8,128)}, f32[4096,1024]{1,0:T(8,128)}, u32[]{:S(2)}, u32[]{:S(2)}) collective-permute-start(f32[4096,1024]{1,0:T(8,128)} %get-tuple-element.80), channel_id=1, source_target_pairs={{0,1},{1,0},{2,3},{3,2},{4,5},{5,4},{6,7},{7,6}} | collective-permute-start | bytes 50331656 | tf_op jit(solution)/shard_map/ppermute | solution.py:598
  955.0 4.1 slice_bitcast_fusion
  959.1 3.0 copy-done.2
  962.1 3.4 slice_bitcast_fusion.2
  965.6 265.9 %collective-permute-done.14 = f32[2,3,1,512,512]{4,3,1,2,0:T(8,128)} collective-permute-done((f32[2,3,1,512,512]{4,3,1,2,0:T(8,128)S(1)}, f32[2,3,1,512,512]{4,3,1,2,0:T(8,128)}, u32[]{:S(2)}, u32[]{:S(2)}) %collective-permute-start.14) | collective-permute-done | bytes 6291488 | tf_op jit(solution)/shard_map/ppermute | solution.py:601
  1231.5 6.6 fusion
  1238.0 3.4 slice_bitcast_fusion.4
  1241.5 4.6 fusion.1
  1246.1 3.4 slice_bitcast_fusion.6
  1249.6 0.2 collective-permute-start.13
  1249.8 58.8 %combine.3 = (bf16[4096,1024]{1,0:T(8,128)(2,1)}, bf16[4096,1024]{1,0:T(8,128)(2,1)}) custom-call(s32[32,16]{1,0:T(8,128)} %get-tuple-element.57.start_ref, s32[32,16]{1,0:T(8,128)} %get-tuple-element.58.rows_ref, s32[32,16]{1,0:T(8,128)} %get-tuple-element.59.off_ref, bf16[16,3072,1024]{2,1,0:T(8,128)(2,1)} %get-tuple-element.78.y_hbm, ...), custom_call_target="tpu_custom_call" | custom-call | flops 44999999488 | bytes 120000000 | tf_op jit(solution)/shard_map/combine/pallas_call | solution.py:526
  1308.6 184.6 %attention_grad.1 = bf16[8,512,1024]{2,1,0:T(8,128)(2,1)} custom-call(bf16[8,512,1024]{2,1,0:T(8,128)(2,1)} %bitcast.130, bf16[8,512,1024]{2,1,0:T(8,128)(2,1)} %x_ref.1, bf16[8,512,3072]{2,1,0:T(8,128)(2,1)} %get-tuple-element.84.qkv_ref, bf16[2,4,1024,512]{3,2,1,0:T(8,128)(2,1)} %bitcast.128), custom_call_target="tpu_custom_call" | custom-call | flops 149999992832 | bytes 70000000 | tf_op jit(solution)/shard_map/attention_grad/pallas_call | solution.py:155
  1493.1 5.1 place.4
  1498.3 4.7 place.5
  1503.0 4.6 place.6
  1507.6 33.2 %reduce-scatter.7.cloned.1.call-done = f32[1,3,4,512,512]{4,3,2,1,0:T(8,128)} async-done(((f32[4,3,4,512,512]{4,3,2,1,0:T(8,128)}), f32[1,3,4,512,512]{4,3,2,1,0:T(8,128)}) %reduce-scatter.7.cloned.1.call-update) | async-done | bytes 12582928
  1540.8 9.4 place.7
  (42 shorter events, 0.6 us)
Async XLA Ops:
  7.2 2.0 copy-start
  7.2 52.3 %all-gather.7.cloned.1.call-start = ((), (), s32[]{:S(2)}) async-start(), calls=%async_computation.2 | async-start | bytes 9437184 | tf_op jit(solution)/shard_map/all_gather | solution.py:613
  10.3 559.8 %all-gather.9.cloned.1.call-start = ((), (), s32[]{:S(2)}) async-start(), calls=%async_computation.3 | async-start | bytes 15728640 | tf_op jit(solution)/shard_map/all_gather | solution.py:618
  11.6 3.9 copy-start.3
  11.6 4.5 copy-start.4
  11.6 4.5 copy-start.5
  15.4 638.7 %all-gather.11.cloned.1.call-start = ((), (), s32[]{:S(2)}) async-start(), calls=%async_computation.4 | async-start | bytes 31457280 | tf_op jit(solution)/shard_map/all_gather | solution.py:618
  15.5 13.0 collective-permute-start.1
  16.2 13.0 collective-permute-start
  16.2 412.9 %collective-permute-start.3 = (bf16[4096,1024]{1,0:T(8,128)(2,1)}, bf16[4096,1024]{1,0:T(8,128)(2,1)}, u32[]{:S(2)}, u32[]{:S(2)}) collective-permute-start(bf16[4096,1024]{1,0:T(8,128)(2,1)} %bitcast.106), channel_id=1, source_target_pairs={{0,1},{1,0},{2,3},{3,2},{4,5},{5,4},{6,7},{7,6}} | collective-permute-start | bytes 25165832 | tf_op jit(solution)/shard_map/ppermute | solution.py:598
  24.3 1468.8 %reduce-scatter.9.cloned.1.call-start = ((), (), s32[]{:S(2)}) async-start(), calls=%async_computation.6 | async-start | bytes 31457280
  217.5 211.7 %collective-permute-start.2 = (bf16[4096,1024]{1,0:T(8,128)(2,1)}, bf16[4096,1024]{1,0:T(8,128)(2,1)}, u32[]{:S(2)}, u32[]{:S(2)}) collective-permute-start(bf16[4096,1024]{1,0:T(8,128)(2,1)} %bitcast.109), channel_id=1, source_target_pairs={{0,1},{1,0},{2,3},{3,2},{4,5},{5,4},{6,7},{7,6}} | collective-permute-start | bytes 25165832 | tf_op jit(solution)/shard_map/ppermute | solution.py:598
  217.7 70.2 %collective-permute-start.5 = (bf16[3,1,512,512]{3,2,0,1:T(8,128)(2,1)S(1)}, bf16[3,1,512,512]{3,2,0,1:T(8,128)(2,1)}, u32[]{:S(2)}, u32[]{:S(2)}) collective-permute-start(bf16[3,1,512,512]{3,2,0,1:T(8,128)(2,1)S(1)} %get-tuple-element.70), channel_id=1, source_target_pairs={{0,4},{4,0},{1,5},{5,1},{2,6},{6,2},{3,7},{7,3}} | collective-permute-start | bytes 4718600 | tf_op jit(solution)/shard_map/ppermute | solution.py:604
  218.9 70.1 %collective-permute-start.4 = (bf16[3,1,512,512]{3,2,0,1:T(8,128)(2,1)S(1)}, bf16[3,1,512,512]{3,2,0,1:T(8,128)(2,1)}, u32[]{:S(2)}, u32[]{:S(2)}) collective-permute-start(bf16[3,1,512,512]{3,2,0,1:T(8,128)(2,1)S(1)} %get-tuple-element.70), channel_id=1, source_target_pairs={{0,2},{1,3},{2,0},{3,1},{4,6},{5,7},{6,4},{7,5}} | collective-permute-start | bytes 4718600 | tf_op jit(solution)/shard_map/ppermute | solution.py:601
  219.2 130.9 %collective-permute-start.8 = (bf16[3,1,512,512]{3,2,0,1:T(8,128)(2,1)S(1)}, bf16[3,1,512,512]{3,2,0,1:T(8,128)(2,1)}, u32[]{:S(2)}, u32[]{:S(2)}) collective-permute-start(bf16[3,1,512,512]{3,2,0,1:T(8,128)(2,1)S(1)} %get-tuple-element.73), channel_id=1, source_target_pairs={{0,4},{4,0},{1,5},{5,1},{2,6},{6,2},{3,7},{7,3}} | collective-permute-start | bytes 4718600 | tf_op jit(solution)/shard_map/ppermute | solution.py:604
  287.9 135.5 %collective-permute-start.7 = (bf16[3,1,512,512]{3,2,0,1:T(8,128)(2,1)S(1)}, bf16[3,1,512,512]{3,2,0,1:T(8,128)(2,1)}, u32[]{:S(2)}, u32[]{:S(2)}) collective-permute-start(bf16[3,1,512,512]{3,2,0,1:T(8,128)(2,1)S(1)} %get-tuple-element.73), channel_id=1, source_target_pairs={{0,2},{1,3},{2,0},{3,1},{4,6},{5,7},{6,4},{7,5}} | collective-permute-start | bytes 4718600 | tf_op jit(solution)/shard_map/ppermute | solution.py:601
  289.0 128.6 %collective-permute-start.6 = (bf16[3,1,512,512]{3,2,0,1:T(8,128)(2,1)}, bf16[3,1,512,512]{3,2,0,1:T(8,128)(2,1)}, u32[]{:S(2)}, u32[]{:S(2)}) collective-permute-start(bf16[3,1,512,512]{3,2,0,1:T(8,128)(2,1)} %collective-permute-done.4), channel_id=1, source_target_pairs={{0,4},{4,0},{1,5},{5,1},{2,6},{6,2},{3,7},{7,3}} | collective-permute-start | bytes 4718600 | tf_op jit(solution)/shard_map/ppermute | solution.py:604
  350.2 73.2 %collective-permute-start.9 = (bf16[3,1,512,512]{3,2,0,1:T(8,128)(2,1)}, bf16[3,1,512,512]{3,2,0,1:T(8,128)(2,1)}, u32[]{:S(2)}, u32[]{:S(2)}) collective-permute-start(bf16[3,1,512,512]{3,2,0,1:T(8,128)(2,1)} %collective-permute-done.8), channel_id=1, source_target_pairs={{0,2},{1,3},{2,0},{3,1},{4,6},{5,7},{6,4},{7,5}} | collective-permute-start | bytes 4718600 | tf_op jit(solution)/shard_map/ppermute | solution.py:601
  654.1 886.7 %reduce-scatter.7.cloned.1.call-start = ((), (), s32[]{:S(2)}) async-start(), calls=%async_computation.5 | async-start | bytes 62914560
  904.9 344.9 %collective-permute-start.10 = (f32[4096,1024]{1,0:T(8,128)}, f32[4096,1024]{1,0:T(8,128)}, u32[]{:S(2)}, u32[]{:S(2)}) collective-permute-start(f32[4096,1024]{1,0:T(8,128)} %get-tuple-element.80), channel_id=1, source_target_pairs={{0,1},{1,0},{2,3},{3,2},{4,5},{5,4},{6,7},{7,6}} | collective-permute-start | bytes 50331656 | tf_op jit(solution)/shard_map/ppermute | solution.py:598
  954.9 294.8 %collective-permute-start.11 = (f32[4096,1024]{1,0:T(8,128)}, f32[4096,1024]{1,0:T(8,128)}, u32[]{:S(2)}, u32[]{:S(2)}) collective-permute-start(f32[4096,1024]{1,0:T(8,128)} %get-tuple-element.81), channel_id=1, source_target_pairs={{0,1},{1,0},{2,3},{3,2},{4,5},{5,4},{6,7},{7,6}} | collective-permute-start | bytes 50331656 | tf_op jit(solution)/shard_map/ppermute | solution.py:598
  955.0 7.2 copy-start.2
  959.1 272.4 %collective-permute-start.14 = (f32[2,3,1,512,512]{4,3,1,2,0:T(8,128)S(1)}, f32[2,3,1,512,512]{4,3,1,2,0:T(8,128)}, u32[]{:S(2)}, u32[]{:S(2)}) collective-permute-start(f32[2,3,1,512,512]{4,3,1,2,0:T(8,128)S(1)} %slice_bitcast_fusion), channel_id=1, source_target_pairs={{0,2},{1,3},{2,0},{3,1},{4,6},{5,7},{6,4},{7,5}} | collective-permute-start | bytes 18874376 | tf_op jit(solution)/shard_map/ppermute | solution.py:601
  965.6 275.9 %collective-permute-start.12 = (f32[2,3,1,512,512]{4,3,1,2,0:T(8,128)}, f32[2,3,1,512,512]{4,3,1,2,0:T(8,128)}, u32[]{:S(2)}, u32[]{:S(2)}) collective-permute-start(f32[2,3,1,512,512]{4,3,1,2,0:T(8,128)} %slice_bitcast_fusion.2), channel_id=1, source_target_pairs={{0,4},{4,0},{1,5},{5,1},{2,6},{6,2},{3,7},{7,3}} | collective-permute-start | bytes 18874376 | tf_op jit(solution)/shard_map/ppermute | solution.py:604
  1241.5 256.8 %collective-permute-start.15 = (f32[3,1,512,512]{3,2,1,0:T(8,128)}, f32[3,1,512,512]{3,2,1,0:T(8,128)}, u32[]{:S(2)}, u32[]{:S(2)}) collective-permute-start(f32[3,1,512,512]{3,2,1,0:T(8,128)} %get-tuple-element.101), channel_id=1, source_target_pairs={{0,4},{4,0},{1,5},{5,1},{2,6},{6,2},{3,7},{7,3}} | collective-permute-start | bytes 9437192 | tf_op jit(solution)/shard_map/ppermute | solution.py:604
  1249.6 253.5 %collective-permute-start.13 = (f32[3,1,512,512]{3,2,1,0:T(8,128)}, f32[3,1,512,512]{3,2,1,0:T(8,128)}, u32[]{:S(2)}, u32[]{:S(2)}) collective-permute-start(f32[3,1,512,512]{3,2,1,0:T(8,128)} %get-tuple-element.103), channel_id=1, source_target_pairs={{0,2},{1,3},{2,0},{3,1},{4,6},{5,7},{6,4},{7,5}} | collective-permute-start | bytes 9437192 | tf_op jit(solution)/shard_map/ppermute | solution.py:601
  1540.8 9.4 copy-start.1
Sparse Core Ops, SparseCore 0:
  10.4 49.0 all-gather.6
  61.9 116.2 all-gather.8
  180.6 318.7 all-gather.10
  654.2 258.5 reduce-scatter.8
  915.7 625.0 reduce-scatter.6

commit v3 on v2

--- a/solution.py
+++ b/solution.py
@@ -353,7 +353,10 @@
         start(expert, 0, 0, True)
 
     before = done[0]
-    dw_ref[...] = jnp.zeros(dw_ref.shape, F32)
+    for p in range(dw_ref.shape[0]):
+        for q in range(dw_ref.shape[1]):
+            for t in range(dw_ref.shape[2]):
+                clear(dw_ref.at[p, q, t, 0])
 
     def tile(i, carry):
         slot = lax.rem(before + i, 2)
@@ -445,6 +448,14 @@
     )(counts, flips, rows, d_rows, weights, weights)
 
 
+def clear(ref):
+    def rows(i, carry):
+        ref[pl.ds(pl.multiple_of(i * LANES, LANES), LANES), :] = jnp.zeros((LANES, ref.shape[1]), ref.dtype)
+        return carry
+
+    lax.fori_loop(0, ref.shape[0] // LANES, rows, 0)
+
+
 def combine_kernel(start_ref, rows_ref, off_ref, y_hbm, dr_hbm, dest_ref, gate_ref, *refs, base, own):
     ybuf, dbuf, acc_y, acc_d, sem = refs[-5:]
     step = pl.program_id(0)
@@ -473,8 +484,9 @@
 
     @pl.when(step == 0)
     def _():
-        ybuf[...] = jnp.zeros(ybuf.shape, BF16)
-        dbuf[...] = jnp.zeros(dbuf.shape, BF16)
+        for which in range(2):
+            clear(ybuf.at[which])
+            clear(dbuf.at[which])
         fetch(b, 0)
 
     @pl.when(step + 1 < n_blocks)
@@ -619,7 +631,7 @@
             weights.append(full)
             first += size
         mid = first + (local_experts - first) // 2
-        attn_w, w_a, w_b = lax.optimization_barrier((attn_w, own_weights(slice(first, mid)), own_weights(slice(mid, local_experts))))
+        w_a, w_b = own_weights(slice(first, mid)), own_weights(slice(mid, local_experts))
         w_ax, w_ay, w_bx, w_by = swap_x(w_a), swap_y(w_a), swap_x(w_b), swap_y(w_b)
 
         dout_tok = d_out.reshape(tok_count, d_model)

time: 1570 us -> 1610 us (1.025)
  waiting for transfers between devices: 458 us -> 501 us
    ppermute x5, waiting for transfers between devices: 266 us -> 394 us  [swap_x(): return lax.ppermute(values, 'ep', [(i, i ^ CORES) for i in range(ep_size)])]
    ppermute x5, waiting for transfers between devices: 153 us -> 66.1 us  [swap_y(): return lax.ppermute(values, 'fsdp', [(i, i ^ 1) for i in range(fsdp_size)])]
  transfers between devices with their start and end apart: 21 -> 21, of which waited for: 7 -> 7; matrix products, arithmetic and copies ran while one was open for 5% -> 4% of each run, Pallas kernels for 61% -> 59%
where the time goes in v3:
time: 1610 us; the launch traced here: 1600 us
  Pallas kernels  952 us (59%)
  waiting for transfers between devices  501 us (31%)
  starting transfers between devices  57.2 us (4%)
  local copies, waits for them, and re-layouts  42.8 us (3%)
  other arithmetic  34.7 us (2%)
    ppermute x5, waiting for transfers between devices, swap_x(): return lax.ppermute(values, 'ep', [(i, i ^ CORES) for i in range(ep_size)])  394 us
    pallas_call x4, Pallas kernels, experts(): pl.pallas_call(functools.partial(expert_kernel, expert_of=expert_of, x_fi...  383 us
    pallas_call x1, Pallas kernels, attention_grad(): pl.pallas_call(functools.partial(attention_grad_kernel, head_dim=head_dim...  185 us
    pallas_call x1, Pallas kernels, attention(): pl.pallas_call(functools.partial(attention_kernel, head_dim=head_dim), gr...  158 us
    pallas_call x2, Pallas kernels, combine(): pl.pallas_call(functools.partial(combine_kernel, base=base, own=bool(extr...  108 us
    pallas_call x2, Pallas kernels, dispatch(): pl.pallas_call(functools.partial(dispatch_kernel, base=base), grid_spec=p...  84.8 us
    ppermute x5, waiting for transfers between devices, swap_y(): return lax.ppermute(values, 'fsdp', [(i, i ^ 1) for i in range(fsdp_size)])  66.1 us
    ppermute x6, starting transfers between devices, swap(): return lax.ppermute(values, 'ep', [(i, i ^ 1) for i in range(ep_size)])  52.8 us
  transfers between devices with their start and end apart: 21, of which 7 were waited for; matrix products, arithmetic and copies ran while one was open for 4% of the time, Pallas kernels for 59%

profile of v3, /device:TPU:7, one launch (start us, length us, event | category | flops | bytes accessed | tf_op | source)
XLA Modules:
  0.0 1602.5 jit_solution(7566880298426680034)
XLA Ops:
  7.2 1.1 constant_dynamic-slice_fusion
  8.4 0.8 copy-done
  9.2 1.0 pad_maximum_fusion.6
  10.3 1.3 slice_bitcast_fusion.13
  11.6 1.7 slice_bitcast_fusion.11
  13.4 2.0 pad_maximum_fusion.3
  15.5 0.7 collective-permute-start.1
  16.2 0.5 collective-permute-start.3
  16.7 1.9 slice_bitcast_fusion.10
  18.6 2.5 slice_bitcast_fusion.8
  21.1 3.1 pad_maximum_fusion.2
  24.3 2.7 slice_bitcast_fusion.14
  27.0 0.7 fusion.7
  27.7 1.0 fusion.4.loc_ref
  28.8 9.5 route.1
  38.2 2.8 copy.49
  41.0 3.8 copy.50
  44.8 1.9 slice_reduce_fusion
  46.6 3.8 copy.51
  50.4 1.3 slice_bitcast_fusion.20
  51.7 7.9 all-gather.7.cloned.1.call-done
  59.6 157.9 %attention.1 = (bf16[8,512,1024]{2,1,0:T(8,128)(2,1)}, bf16[8,512,3072]{2,1,0:T(8,128)(2,1)}) custom-call(bf16[8,512,1024]{2,1,0:T(8,128)(2,1)} %x_ref.1, bf16[2,4,1024,512]{3,2,1,0:T(8,128)(2,1)} %bitcast.127), custom_call_target="tpu_custom_call" | custom-call | flops 89999998976 | bytes 60000000 | tf_op jit(solution)/shard_map/attention/pallas_call | solution.py:83
  217.6 0.3 collective-permute-start.2
  217.8 1.3 slice_bitcast_fusion.16
  219.1 0.2 fusion.9
  219.4 1.2 collective-permute-start.8
  220.6 0.3 collective-permute-start.7
  220.9 1.4 fusion.10
  222.3 1.2 collective-permute-start.4
  223.4 66.1 %collective-permute-done.8 = bf16[3,1,512,512]{3,2,0,1:T(8,128)(2,1)} collective-permute-done((bf16[3,1,512,512]{3,2,0,1:T(8,128)(2,1)S(1)}, bf16[3,1,512,512]{3,2,0,1:T(8,128)(2,1)}, u32[]{:S(2)}, u32[]{:S(2)}) %collective-permute-start.8) | collective-permute-done | bytes 1572896 | tf_op jit(solution)/shard_map/ppermute | solution.py:616
  289.6 0.8 collective-permute-start.9
  290.4 0.3 collective-permute-done.7
  290.6 0.4 collective-permute-start.5
  291.0 60.9 %collective-permute-done.4 = bf16[3,1,512,512]{3,2,0,1:T(8,128)(2,1)} collective-permute-done((bf16[3,1,512,512]{3,2,0,1:T(8,128)(2,1)}, bf16[3,1,512,512]{3,2,0,1:T(8,128)(2,1)}, u32[]{:S(2)}, u32[]{:S(2)}) %collective-permute-start.4) | collective-permute-done | bytes 1572896 | tf_op jit(solution)/shard_map/ppermute | solution.py:613
  351.9 0.1 collective-permute-start.6
  352.1 0.6 pad_add_fusion.1.flip_ref
  352.7 66.7 %collective-permute-done.9 = bf16[3,1,512,512]{3,2,0,1:T(8,128)(2,1)} collective-permute-done((bf16[3,1,512,512]{3,2,0,1:T(8,128)(2,1)}, bf16[3,1,512,512]{3,2,0,1:T(8,128)(2,1)}, u32[]{:S(2)}, u32[]{:S(2)}) %collective-permute-start.9) | collective-permute-done | bytes 1572896 | tf_op jit(solution)/shard_map/ppermute | solution.py:613
  419.3 5.8 pad_maximum_fusion.1.w_lo.w_hi
  425.1 5.8 pad_maximum_fusion.w_lo.w_hi
  430.9 42.0 %dispatch.2 = (bf16[16,3072,1024]{2,1,0:T(8,128)(2,1)}, bf16[16,3072,1024]{2,1,0:T(8,128)(2,1)}) custom-call(s32[32,16]{1,0:T(8,128)} %get-tuple-element.54.start_ref, s32[32,16]{1,0:T(8,128)} %get-tuple-element.55.rows_ref, s32[32,16]{1,0:T(8,128)} %get-tuple-element.56.off_ref, bf16[4096,1024]{1,0:T(8,128)(2,1)} %bitcast.112, ...), custom_call_target="tpu_custom_call" | custom-call | flops 40000000000 | bytes 90000000 | tf_op jit(solution)/shard_map/dispatch/pallas_call | solution.py:305
  472.9 42.8 %dispatch.3 = (bf16[16,3072,1024]{2,1,0:T(8,128)(2,1)}, bf16[16,3072,1024]{2,1,0:T(8,128)(2,1)}) custom-call(s32[32,16]{1,0:T(8,128)} %get-tuple-element.54.start_ref, s32[32,16]{1,0:T(8,128)} %get-tuple-element.55.rows_ref, s32[32,16]{1,0:T(8,128)} %get-tuple-element.56.off_ref, ...), custom_call_target="tpu_custom_call", output_to_operand_aliasing={{0}: (7, {}), {1}: (8, {})} | custom-call | flops 40000000000 | bytes 90000000 | tf_op jit(solution)/shard_map/dispatch/pallas_call | solution.py:305
  515.7 52.2 %experts.4 = (bf16[16,3072,1024]{2,1,0:T(8,128)(2,1)}, bf16[16,3072,1024]{2,1,0:T(8,128)(2,1)}, f32[2,2,3,1,512,512]{5,4,3,2,1,0:T(8,128)}) custom-call(s32[16]{0:T(128)} %get-tuple-element.57.count_ref, s32[2]{0:T(128)} %pad_add_fusion.1.flip_ref, bf16[16,3072,1024]{2,1,0:T(8,128)(2,1)} %get-tuple-element.64.r_hbm, ...), custom_call_target="tpu_custom_call", output_to_operand_aliasing={{0}: (2, {}), {1}: (3, {})} | custom-call | flops 56000000000 | bytes 100000000 | tf_op jit(solution)/shard_map/experts/pallas_call | solution.py:435
  567.9 46.1 %experts.5 = (bf16[16,3072,1024]{2,1,0:T(8,128)(2,1)}, bf16[16,3072,1024]{2,1,0:T(8,128)(2,1)}, f32[2,2,3,1,512,512]{5,4,3,2,1,0:T(8,128)}) custom-call(s32[16]{0:T(128)} %get-tuple-element.57.count_ref, s32[2]{0:T(128)} %pad_add_fusion.1.flip_ref, bf16[16,3072,1024]{2,1,0:T(8,128)(2,1)} %get-tuple-element.66.r_hbm, ...), custom_call_target="tpu_custom_call", output_to_operand_aliasing={{0}: (2, {}), {1}: (3, {})} | custom-call | flops 56000000000 | bytes 100000000 | tf_op jit(solution)/shard_map/experts/pallas_call | solution.py:435
  614.1 0.5 broadcast_2_flip_ref.2.flip_ref
  614.6 83.5 %experts.6 = (bf16[16,3072,1024]{2,1,0:T(8,128)(2,1)}, bf16[16,3072,1024]{2,1,0:T(8,128)(2,1)}, f32[2,2,3,2,512,512]{5,4,3,2,1,0:T(8,128)}) custom-call(s32[16]{0:T(128)} %get-tuple-element.57.count_ref, s32[2]{0:T(128)} %broadcast_2_flip_ref.2.flip_ref, ...), custom_call_target="tpu_custom_call", output_to_operand_aliasing={{0}: (2, {}), {1}: (3, {})} | custom-call | flops 112000000000 | bytes 200000000 | tf_op jit(solution)/shard_map/experts/pallas_call | solution.py:435
  698.2 201.5 %experts.7 = (bf16[16,3072,1024]{2,1,0:T(8,128)(2,1)}, bf16[16,3072,1024]{2,1,0:T(8,128)(2,1)}, f32[2,2,3,4,512,512]{5,4,3,2,1,0:T(8,128)}) custom-call(s32[16]{0:T(128)} %get-tuple-element.57.count_ref, s32[2]{0:T(128)} %broadcast_2_flip_ref.2.flip_ref, ...), custom_call_target="tpu_custom_call", output_to_operand_aliasing={{0}: (2, {}), {1}: (3, {})} | custom-call | flops 224000000000 | bytes 400000000 | tf_op jit(solution)/shard_map/experts/pallas_call | solution.py:435
  899.7 49.4 %combine.2 = (f32[4096,1024]{1,0:T(8,128)}, f32[4096,1024]{1,0:T(8,128)}) custom-call(s32[32,16]{1,0:T(8,128)} %get-tuple-element.54.start_ref, s32[32,16]{1,0:T(8,128)} %get-tuple-element.55.rows_ref, s32[32,16]{1,0:T(8,128)} %get-tuple-element.56.off_ref, bf16[16,3072,1024]{2,1,0:T(8,128)(2,1)} %get-tuple-element.72.y_hbm, ...), custom_call_target="tpu_custom_call" | custom-call | flops 44999999488 | bytes 120000000 | tf_op jit(solution)/shard_map/combine/pallas_call | solution.py:538
  949.1 51.3 %collective-permute-start.10 = (f32[4096,1024]{1,0:T(8,128)}, f32[4096,1024]{1,0:T(8,128)}, u32[]{:S(2)}, u32[]{:S(2)}) collective-permute-start(f32[4096,1024]{1,0:T(8,128)} %get-tuple-element.74), channel_id=1, source_target_pairs={{0,1},{1,0},{2,3},{3,2},{4,5},{5,4},{6,7},{7,6}} | collective-permute-start | bytes 50331656 | tf_op jit(solution)/shard_map/ppermute | solution.py:610
  1000.5 4.1 slice_bitcast_fusion
  1004.6 3.1 copy-done.2
  1007.7 3.4 slice_bitcast_fusion.2
  1011.1 265.8 %collective-permute-done.14 = f32[2,3,1,512,512]{4,3,1,2,0:T(8,128)} collective-permute-done((f32[2,3,1,512,512]{4,3,1,2,0:T(8,128)S(1)}, f32[2,3,1,512,512]{4,3,1,2,0:T(8,128)}, u32[]{:S(2)}, u32[]{:S(2)}) %collective-permute-start.14) | collective-permute-done | bytes 6291488 | tf_op jit(solution)/shard_map/ppermute | solution.py:613
  1276.9 6.6 fusion
  1283.5 3.4 slice_bitcast_fusion.4
  1286.9 4.5 fusion.1
  1291.4 3.4 slice_bitcast_fusion.6
  1294.8 0.1 collective-permute-start.13
  1294.9 58.7 %combine.3 = (bf16[4096,1024]{1,0:T(8,128)(2,1)}, bf16[4096,1024]{1,0:T(8,128)(2,1)}) custom-call(s32[32,16]{1,0:T(8,128)} %get-tuple-element.54.start_ref, s32[32,16]{1,0:T(8,128)} %get-tuple-element.55.rows_ref, s32[32,16]{1,0:T(8,128)} %get-tuple-element.56.off_ref, bf16[16,3072,1024]{2,1,0:T(8,128)(2,1)} %get-tuple-element.72.y_hbm, ...), custom_call_target="tpu_custom_call" | custom-call | flops 44999999488 | bytes 120000000 | tf_op jit(solution)/shard_map/combine/pallas_call | solution.py:538
  1353.6 184.9 %attention_grad.1 = bf16[8,512,1024]{2,1,0:T(8,128)(2,1)} custom-call(bf16[8,512,1024]{2,1,0:T(8,128)(2,1)} %bitcast.130, bf16[8,512,1024]{2,1,0:T(8,128)(2,1)} %x_ref.1, bf16[8,512,3072]{2,1,0:T(8,128)(2,1)} %get-tuple-element.78.qkv_ref, bf16[2,4,1024,512]{3,2,1,0:T(8,128)(2,1)} %bitcast.128), custom_call_target="tpu_custom_call" | custom-call | flops 149999992832 | bytes 70000000 | tf_op jit(solution)/shard_map/attention_grad/pallas_call | solution.py:155
  1538.5 5.1 place.4
  1543.6 4.8 place.5
  1548.4 4.6 place.6
  1553.0 33.2 %reduce-scatter.7.cloned.1.call-done = f32[1,3,4,512,512]{4,3,2,1,0:T(8,128)} async-done(((f32[4,3,4,512,512]{4,3,2,1,0:T(8,128)}), f32[1,3,4,512,512]{4,3,2,1,0:T(8,128)}) %reduce-scatter.7.cloned.1.call-update) | async-done | bytes 12582928
  1586.3 9.4 place.7
  (46 shorter events, 0.6 us)
Async XLA Ops:
  7.2 2.0 copy-start
  7.2 52.4 %all-gather.7.cloned.1.call-start = ((), (), s32[]{:S(2)}) async-start(), calls=%async_computation.2 | async-start | bytes 9437184 | tf_op jit(solution)/shard_map/all_gather | solution.py:625
  10.3 603.8 %all-gather.9.cloned.1.call-start = ((), (), s32[]{:S(2)}) async-start(), calls=%async_computation.3 | async-start | bytes 15728640 | tf_op jit(solution)/shard_map/all_gather | solution.py:630
  11.6 3.9 copy-start.5
  11.6 4.5 copy-start.6
  11.6 4.5 copy-start.7
  15.4 682.8 %all-gather.11.cloned.1.call-start = ((), (), s32[]{:S(2)}) async-start(), calls=%async_computation.4 | async-start | bytes 31457280 | tf_op jit(solution)/shard_map/all_gather | solution.py:630
  15.5 11.6 collective-permute-start.1
  16.2 11.5 collective-permute-start
  16.2 456.6 %collective-permute-start.3 = (bf16[4096,1024]{1,0:T(8,128)(2,1)}, bf16[4096,1024]{1,0:T(8,128)(2,1)}, u32[]{:S(2)}, u32[]{:S(2)}) collective-permute-start(bf16[4096,1024]{1,0:T(8,128)(2,1)} %bitcast.108), channel_id=1, source_target_pairs={{0,1},{1,0},{2,3},{3,2},{4,5},{5,4},{6,7},{7,6}} | collective-permute-start | bytes 25165832 | tf_op jit(solution)/shard_map/ppermute | solution.py:610
  24.3 1514.2 %reduce-scatter.9.cloned.1.call-start = ((), (), s32[]{:S(2)}) async-start(), calls=%async_computation.6 | async-start | bytes 31457280
  217.5 3.3 copy-start.3
  217.5 3.3 copy-start.4
  217.6 255.3 %collective-permute-start.2 = (bf16[4096,1024]{1,0:T(8,128)(2,1)}, bf16[4096,1024]{1,0:T(8,128)(2,1)}, u32[]{:S(2)}, u32[]{:S(2)}) collective-permute-start(bf16[4096,1024]{1,0:T(8,128)(2,1)} %bitcast.111), channel_id=1, source_target_pairs={{0,1},{1,0},{2,3},{3,2},{4,5},{5,4},{6,7},{7,6}} | collective-permute-start | bytes 25165832 | tf_op jit(solution)/shard_map/ppermute | solution.py:610
  219.4 70.2 %collective-permute-start.8 = (bf16[3,1,512,512]{3,2,0,1:T(8,128)(2,1)S(1)}, bf16[3,1,512,512]{3,2,0,1:T(8,128)(2,1)}, u32[]{:S(2)}, u32[]{:S(2)}) collective-permute-start(bf16[3,1,512,512]{3,2,0,1:T(8,128)(2,1)S(1)} %get-tuple-element.108), channel_id=1, source_target_pairs={{0,4},{4,0},{1,5},{5,1},{2,6},{6,2},{3,7},{7,3}} | collective-permute-start | bytes 4718600 | tf_op jit(solution)/shard_map/ppermute | solution.py:616
  220.6 70.1 %collective-permute-start.7 = (bf16[3,1,512,512]{3,2,0,1:T(8,128)(2,1)S(1)}, bf16[3,1,512,512]{3,2,0,1:T(8,128)(2,1)}, u32[]{:S(2)}, u32[]{:S(2)}) collective-permute-start(bf16[3,1,512,512]{3,2,0,1:T(8,128)(2,1)S(1)} %get-tuple-element.108), channel_id=1, source_target_pairs={{0,2},{1,3},{2,0},{3,1},{4,6},{5,7},{6,4},{7,5}} | collective-permute-start | bytes 4718600 | tf_op jit(solution)/shard_map/ppermute | solution.py:613
  222.3 129.7 %collective-permute-start.4 = (bf16[3,1,512,512]{3,2,0,1:T(8,128)(2,1)}, bf16[3,1,512,512]{3,2,0,1:T(8,128)(2,1)}, u32[]{:S(2)}, u32[]{:S(2)}) collective-permute-start(bf16[3,1,512,512]{3,2,0,1:T(8,128)(2,1)} %get-tuple-element.110), channel_id=1, source_target_pairs={{0,2},{1,3},{2,0},{3,1},{4,6},{5,7},{6,4},{7,5}} | collective-permute-start | bytes 4718600 | tf_op jit(solution)/shard_map/ppermute | solution.py:613
  289.6 129.8 %collective-permute-start.9 = (bf16[3,1,512,512]{3,2,0,1:T(8,128)(2,1)}, bf16[3,1,512,512]{3,2,0,1:T(8,128)(2,1)}, u32[]{:S(2)}, u32[]{:S(2)}) collective-permute-start(bf16[3,1,512,512]{3,2,0,1:T(8,128)(2,1)} %collective-permute-done.8), channel_id=1, source_target_pairs={{0,2},{1,3},{2,0},{3,1},{4,6},{5,7},{6,4},{7,5}} | collective-permute-start | bytes 4718600 | tf_op jit(solution)/shard_map/ppermute | solution.py:613
  290.6 134.5 %collective-permute-start.5 = (bf16[3,1,512,512]{3,2,0,1:T(8,128)(2,1)}, bf16[3,1,512,512]{3,2,0,1:T(8,128)(2,1)}, u32[]{:S(2)}, u32[]{:S(2)}) collective-permute-start(bf16[3,1,512,512]{3,2,0,1:T(8,128)(2,1)} %get-tuple-element.110), channel_id=1, source_target_pairs={{0,4},{4,0},{1,5},{5,1},{2,6},{6,2},{3,7},{7,3}} | collective-permute-start | bytes 4718600 | tf_op jit(solution)/shard_map/ppermute | solution.py:616
  351.9 73.2 %collective-permute-start.6 = (bf16[3,1,512,512]{3,2,0,1:T(8,128)(2,1)}, bf16[3,1,512,512]{3,2,0,1:T(8,128)(2,1)}, u32[]{:S(2)}, u32[]{:S(2)}) collective-permute-start(bf16[3,1,512,512]{3,2,0,1:T(8,128)(2,1)} %collective-permute-done.4), channel_id=1, source_target_pairs={{0,4},{4,0},{1,5},{5,1},{2,6},{6,2},{3,7},{7,3}} | collective-permute-start | bytes 4718600 | tf_op jit(solution)/shard_map/ppermute | solution.py:616
  698.1 888.1 %reduce-scatter.7.cloned.1.call-start = ((), (), s32[]{:S(2)}) async-start(), calls=%async_computation.5 | async-start | bytes 62914560
  949.1 345.7 %collective-permute-start.10 = (f32[4096,1024]{1,0:T(8,128)}, f32[4096,1024]{1,0:T(8,128)}, u32[]{:S(2)}, u32[]{:S(2)}) collective-permute-start(f32[4096,1024]{1,0:T(8,128)} %get-tuple-element.74), channel_id=1, source_target_pairs={{0,1},{1,0},{2,3},{3,2},{4,5},{5,4},{6,7},{7,6}} | collective-permute-start | bytes 50331656 | tf_op jit(solution)/shard_map/ppermute | solution.py:610
  1000.4 294.5 %collective-permute-start.11 = (f32[4096,1024]{1,0:T(8,128)}, f32[4096,1024]{1,0:T(8,128)}, u32[]{:S(2)}, u32[]{:S(2)}) collective-permute-start(f32[4096,1024]{1,0:T(8,128)} %get-tuple-element.75), channel_id=1, source_target_pairs={{0,1},{1,0},{2,3},{3,2},{4,5},{5,4},{6,7},{7,6}} | collective-permute-start | bytes 50331656 | tf_op jit(solution)/shard_map/ppermute | solution.py:610
  1000.5 7.2 copy-start.2
  1004.6 272.3 %collective-permute-start.14 = (f32[2,3,1,512,512]{4,3,1,2,0:T(8,128)S(1)}, f32[2,3,1,512,512]{4,3,1,2,0:T(8,128)}, u32[]{:S(2)}, u32[]{:S(2)}) collective-permute-start(f32[2,3,1,512,512]{4,3,1,2,0:T(8,128)S(1)} %slice_bitcast_fusion), channel_id=1, source_target_pairs={{0,2},{1,3},{2,0},{3,1},{4,6},{5,7},{6,4},{7,5}} | collective-permute-start | bytes 18874376 | tf_op jit(solution)/shard_map/ppermute | solution.py:613
  1011.1 275.8 %collective-permute-start.12 = (f32[2,3,1,512,512]{4,3,1,2,0:T(8,128)}, f32[2,3,1,512,512]{4,3,1,2,0:T(8,128)}, u32[]{:S(2)}, u32[]{:S(2)}) collective-permute-start(f32[2,3,1,512,512]{4,3,1,2,0:T(8,128)} %slice_bitcast_fusion.2), channel_id=1, source_target_pairs={{0,4},{4,0},{1,5},{5,1},{2,6},{6,2},{3,7},{7,3}} | collective-permute-start | bytes 18874376 | tf_op jit(solution)/shard_map/ppermute | solution.py:616
  1286.8 256.7 %collective-permute-start.15 = (f32[3,1,512,512]{3,2,1,0:T(8,128)}, f32[3,1,512,512]{3,2,1,0:T(8,128)}, u32[]{:S(2)}, u32[]{:S(2)}) collective-permute-start(f32[3,1,512,512]{3,2,1,0:T(8,128)} %get-tuple-element.95), channel_id=1, source_target_pairs={{0,4},{4,0},{1,5},{5,1},{2,6},{6,2},{3,7},{7,3}} | collective-permute-start | bytes 9437192 | tf_op jit(solution)/shard_map/ppermute | solution.py:616
  1294.8 253.6 %collective-permute-start.13 = (f32[3,1,512,512]{3,2,1,0:T(8,128)}, f32[3,1,512,512]{3,2,1,0:T(8,128)}, u32[]{:S(2)}, u32[]{:S(2)}) collective-permute-start(f32[3,1,512,512]{3,2,1,0:T(8,128)} %get-tuple-element.97), channel_id=1, source_target_pairs={{0,2},{1,3},{2,0},{3,1},{4,6},{5,7},{6,4},{7,5}} | collective-permute-start | bytes 9437192 | tf_op jit(solution)/shard_map/ppermute | solution.py:613
  1586.3 9.4 copy-start.1
Sparse Core Ops, SparseCore 0:
  10.4 49.1 all-gather.6
  61.9 116.2 all-gather.8
  180.6 318.7 all-gather.10
  698.3 259.3 reduce-scatter.8
  960.6 625.6 reduce-scatter.6

commit v4 on v3

--- a/solution.py
+++ b/solution.py
@@ -51,28 +51,30 @@
         qkv_ref[0, :, p * n_qkv:(p + 1) * n_qkv] = part.astype(BF16)
     scale = head_dim ** -0.5 * LOG2E
 
+    diagonal = lax.broadcasted_iota(jnp.int32, (BLOCK, BLOCK), 1) >= lax.broadcasted_iota(jnp.int32, (BLOCK, BLOCK), 0)
+
     def pair(i, carry):
         q2, k2, v2 = (qkv_ref[0, :, pl.ds(pl.multiple_of(t * d_model + i * LANES, LANES), LANES)] for t in range(3))
         for first in range(0, seq_len, BLOCK):
-            end = first + BLOCK
-            keys, vals = k2[:end], v2[:end]
-            causal = lax.broadcasted_iota(jnp.int32, (BLOCK, end), 0) + first >= lax.broadcasted_iota(jnp.int32, (BLOCK, end), 1)
             both = []
             for head in range(2):
-                scores = nt_dot(lanes_of(head, q2[first:end]), keys) * scale
-                scores = jnp.where(causal, scores, -1e30)
-                probs = jnp.exp2(scores - jnp.max(scores, axis=-1, keepdims=True))
-                probs = (probs * (1.0 / jnp.sum(probs, axis=-1, keepdims=True))).astype(BF16)
-                both.append(jnp.dot(probs, vals, preferred_element_type=F32))
-            lane = lax.broadcasted_iota(jnp.int32, (BLOCK, LANES), 1)
-            ctx[first:end, pl.ds(pl.multiple_of(i * LANES, LANES), LANES)] = jnp.where(lane < LANES // 2, both[0], both[1]).astype(BF16)
+                query = lanes_of(head, q2[first:first + BLOCK])
+                parts = [nt_dot(k2[at:at + BLOCK], query) * scale for at in range(0, first + BLOCK, BLOCK)]
+                parts[-1] = jnp.where(diagonal, parts[-1], -1e30)
+                top = functools.reduce(jnp.maximum, [jnp.max(part, axis=0, keepdims=True) for part in parts])
+                parts = [jnp.exp2(part - top) for part in parts]
+                inverse = 1.0 / sum(jnp.sum(part, axis=0, keepdims=True) for part in parts)
+                probs = jnp.concatenate([(part * inverse).astype(BF16) for part in parts], axis=0)
+                both.append(tn_dot(v2[:first + BLOCK], probs))
+            row = lax.broadcasted_iota(jnp.int32, (LANES, BLOCK), 0)
+            ctx[pl.ds(pl.multiple_of(i * LANES, LANES), LANES), first:first + BLOCK] = jnp.where(row < LANES // 2, both[0], both[1]).astype(BF16)
         return carry
 
     lax.fori_loop(0, d_model // LANES, pair, 0)
     for f in range(n_fsdp):
         w_out = jnp.concatenate([w_ref[f, p, n_qkv:] for p in range(n_ep)], axis=0)
         cols = slice(f * half, (f + 1) * half)
-        h_ref[0, :, cols] = (x_ref[0, :, cols].astype(F32) + jnp.dot(ctx[...], w_out, preferred_element_type=F32)).astype(BF16)
+        h_ref[0, :, cols] = (x_ref[0, :, cols].astype(F32) + tn_dot(ctx[...], w_out)).astype(BF16)
 
 
 def attention(tokens, weights, head_dim):
@@ -86,7 +88,7 @@
         in_specs=[seq_spec, w_spec],
         out_specs=[seq_spec, qkv_spec],
         out_shape=[jax.ShapeDtypeStruct(tokens.shape, BF16), jax.ShapeDtypeStruct((n_seq, seq_len, 3 * d_model), BF16)],
-        scratch_shapes=[pltpu.VMEM((seq_len, d_model), BF16)],
+        scratch_shapes=[pltpu.VMEM((d_model, seq_len), BF16)],
         name='attention',
         **settings(90, 60),
     )(tokens, weights)
@@ -656,19 +658,16 @@
         h_other = swap(h_tok)
         held = dispatch(h_tok, dout_tok, dest, gate, segs, 0, [], n_local, max_rows)
         rows, d_rows = dispatch(h_other, dout_other, dest, gate, segs, n_blocks, held, n_local, max_rows)
-        rows, d_rows, d_a = experts(rows, d_rows, w_a, counts, flips, first, local_experts, x_first=True)
-        more_a = swap_x(d_a[1])
-        rows, d_rows, d_b = experts(rows, d_rows, w_b, counts, flips, mid, local_experts)
-        more_b = swap_y(d_b[1])
-        d_a, d_b = d_a[0] + more_a, d_b[0] + more_b
-        more_a, more_b = swap_y(d_a[1]), swap_x(d_b[1])
-        done, start = [([d_a[0], more_a], first), ([d_b[0], more_b], mid)], 0
+        sums, grads, start = [], [], 0
         for n, size in enumerate(CHUNKS):
+            rows, d_rows, d_w = experts(rows, d_rows, (w_a, w_b)[n], counts, flips, (first, mid)[n], local_experts, x_first=n == 0)
+            sums.append(d_w[0] + (swap_x, swap_y)[n](d_w[1]))
             rows, d_rows, d_w = experts(rows, d_rows, weights[n], counts, jnp.zeros_like(flips), start, local_experts)
             d_w = d_w.reshape(fsdp_size * n_side, *d_w.shape[2:])
-            d_w = lax.psum_scatter(d_w, ('fsdp', 'ep'), scatter_dimension=0, tiled=False, axis_index_groups=groups)
-            done.insert(0 if n == 0 else len(done), ([d_w], start))
+            grads.append(([lax.psum_scatter(d_w, ('fsdp', 'ep'), scatter_dimension=0, tiled=False, axis_index_groups=groups)], start))
             start += size
+        more_a, more_b = swap_y(sums[0][1]), swap_x(sums[1][1])
+        done = [grads[0], ([sums[0][0], more_a], first), ([sums[1][0], more_b], mid), grads[1]]
         sums = combine(rows, d_rows, dest, gate, segs, n_blocks, n_blocks, [])
         more = [swap(value) for value in sums]
         layer_out, d_h = combine(rows, d_rows, dest, gate, segs, 0, n_blocks, [*more, h_tok, dout_tok])

time: 1610 us -> 1640 us (1.019)
  starting transfers between devices: 57.2 us -> 89.7 us
    unnamed x7, waiting for transfers between devices: 33.3 us -> 6.06 us
    ppermute x5, starting transfers between devices: 1.73 us -> 22.4 us  [swap_y(): return lax.ppermute(values, 'fsdp', [(i, i ^ 1) for i in range(fsdp_size)])]
  transfers between devices with their start and end apart: 21 -> 21, of which waited for: 7 -> 9; matrix products, arithmetic and copies ran while one was open for 4% -> 4% of each run, Pallas kernels for 59% -> 57%
where the time goes in v4:
time: 1640 us; the launch traced here: 1620 us
  Pallas kernels  938 us (57%)
  waiting for transfers between devices  505 us (31%)
  starting transfers between devices  89.7 us (5%)
  local copies, waits for them, and re-layouts  43.1 us (3%)
  other arithmetic  33.3 us (2%)
    ppermute x5, waiting for transfers between devices, swap_x(): return lax.ppermute(values, 'ep', [(i, i ^ CORES) for i in range(ep_size)])  407 us
    pallas_call x4, Pallas kernels, experts(): pl.pallas_call(functools.partial(expert_kernel, expert_of=expert_of, x_fi...  383 us
    pallas_call x1, Pallas kernels, attention_grad(): pl.pallas_call(functools.partial(attention_grad_kernel, head_dim=head_dim...  185 us
    pallas_call x1, Pallas kernels, attention(): pl.pallas_call(functools.partial(attention_kernel, head_dim=head_dim), gr...  144 us
    pallas_call x2, Pallas kernels, combine(): pl.pallas_call(functools.partial(combine_kernel, base=base, own=bool(extr...  108 us
    pallas_call x2, Pallas kernels, dispatch(): pl.pallas_call(functools.partial(dispatch_kernel, base=base), grid_spec=p...  84.8 us
    ppermute x5, waiting for transfers between devices, swap_y(): return lax.ppermute(values, 'fsdp', [(i, i ^ 1) for i in range(fsdp_size)])  81.4 us
    ppermute x6, starting transfers between devices, swap(): return lax.ppermute(values, 'ep', [(i, i ^ 1) for i in range(ep_size)])  66.1 us
  transfers between devices with their start and end apart: 21, of which 9 were waited for; matrix products, arithmetic and copies ran while one was open for 4% of the time, Pallas kernels for 57%

profile of v4, /device:TPU:7, one launch (start us, length us, event | category | flops | bytes accessed | tf_op | source)
XLA Modules:
  0.0 1623.0 jit_solution(10522800293582697152)
XLA Ops:
  7.2 1.1 constant_dynamic-slice_fusion
  8.4 0.8 copy-done
  9.2 1.0 pad_maximum_fusion.6
  10.3 1.3 slice_bitcast_fusion.13
  11.6 1.7 slice_bitcast_fusion.11
  13.3 2.0 pad_maximum_fusion.3
  15.4 2.0 slice_bitcast_fusion.10
  17.4 2.8 slice_bitcast_fusion.8
  20.2 3.1 pad_maximum_fusion.2
  23.4 0.8 copy-done.6
  24.2 0.7 collective-permute-start.1
  25.1 0.4 collective-permute-start.3
  25.4 0.3 collective-permute-done.1
  25.8 0.6 fusion.7
  26.4 1.0 fusion.4.loc_ref
  27.5 9.2 route.1
  36.6 2.8 copy.49
  39.4 3.8 copy.50
  43.2 3.8 copy.51
  47.0 1.9 slice_reduce_fusion
  48.9 1.3 slice_bitcast_fusion.20
  50.2 9.5 all-gather.7.cloned.1.call-done
  59.6 144.2 %attention.1 = (bf16[8,512,1024]{2,1,0:T(8,128)(2,1)}, bf16[8,512,3072]{2,1,0:T(8,128)(2,1)}) custom-call(bf16[8,512,1024]{2,1,0:T(8,128)(2,1)} %x_ref.1, bf16[2,4,1024,512]{3,2,1,0:T(8,128)(2,1)} %bitcast.131), custom_call_target="tpu_custom_call" | custom-call | flops 89999998976 | bytes 60000000 | tf_op jit(solution)/shard_map/attention/pallas_call | solution.py:85
  203.8 0.3 collective-permute-start.2
  204.1 2.1 slice_bitcast_fusion.16
  206.2 2.6 slice_bitcast_fusion.14
  208.8 1.4 fusion.10
  210.2 0.8 collective-permute-start.4
  211.0 0.6 collective-permute-start.5
  211.6 68.9 %collective-permute-done.4 = bf16[3,1,512,512]{3,2,0,1:T(8,128)(2,1)S(1)} collective-permute-done((bf16[3,1,512,512]{3,2,0,1:T(8,128)(2,1)}, bf16[3,1,512,512]{3,2,0,1:T(8,128)(2,1)S(1)}, u32[]{:S(2)}, u32[]{:S(2)}) %collective-permute-start.4) | collective-permute-done | bytes 1572896 | tf_op jit(solution)/shard_map/ppermute | solution.py:615
  280.5 1.2 collective-permute-start.6
  281.7 0.6 pad_add_fusion.1.flip_ref
  282.3 62.9 %collective-permute-done.6 = bf16[3,1,512,512]{3,2,0,1:T(8,128)(2,1)} collective-permute-done((bf16[3,1,512,512]{3,2,0,1:T(8,128)(2,1)S(1)}, bf16[3,1,512,512]{3,2,0,1:T(8,128)(2,1)}, u32[]{:S(2)}, u32[]{:S(2)}) %collective-permute-start.6) | collective-permute-done | bytes 1572896 | tf_op jit(solution)/shard_map/ppermute | solution.py:618
  345.3 5.0 pad_maximum_fusion.w_lo.w_hi
  350.3 42.0 %dispatch.2 = (bf16[16,3072,1024]{2,1,0:T(8,128)(2,1)}, bf16[16,3072,1024]{2,1,0:T(8,128)(2,1)}) custom-call(s32[32,16]{1,0:T(8,128)} %get-tuple-element.54.start_ref, s32[32,16]{1,0:T(8,128)} %get-tuple-element.55.rows_ref, s32[32,16]{1,0:T(8,128)} %get-tuple-element.56.off_ref, bf16[4096,1024]{1,0:T(8,128)(2,1)} %bitcast.112, ...), custom_call_target="tpu_custom_call" | custom-call | flops 40000000000 | bytes 90000000 | tf_op jit(solution)/shard_map/dispatch/pallas_call | solution.py:307
  392.3 42.8 %dispatch.3 = (bf16[16,3072,1024]{2,1,0:T(8,128)(2,1)}, bf16[16,3072,1024]{2,1,0:T(8,128)(2,1)}) custom-call(s32[32,16]{1,0:T(8,128)} %get-tuple-element.54.start_ref, s32[32,16]{1,0:T(8,128)} %get-tuple-element.55.rows_ref, s32[32,16]{1,0:T(8,128)} %get-tuple-element.56.off_ref, ...), custom_call_target="tpu_custom_call", output_to_operand_aliasing={{0}: (7, {}), {1}: (8, {})} | custom-call | flops 40000000000 | bytes 90000000 | tf_op jit(solution)/shard_map/dispatch/pallas_call | solution.py:307
  435.2 52.1 %experts.4 = (bf16[16,3072,1024]{2,1,0:T(8,128)(2,1)}, bf16[16,3072,1024]{2,1,0:T(8,128)(2,1)}, f32[2,2,3,1,512,512]{5,4,3,2,1,0:T(8,128)}) custom-call(s32[16]{0:T(128)} %get-tuple-element.57.count_ref, s32[2]{0:T(128)} %pad_add_fusion.1.flip_ref, bf16[16,3072,1024]{2,1,0:T(8,128)(2,1)} %get-tuple-element.64.r_hbm, ...), custom_call_target="tpu_custom_call", output_to_operand_aliasing={{0}: (2, {}), {1}: (3, {})} | custom-call | flops 56000000000 | bytes 100000000 | tf_op jit(solution)/shard_map/experts/pallas_call | solution.py:437
  487.3 0.5 broadcast_2_flip_ref.2.flip_ref
  487.8 83.6 %experts.5 = (bf16[16,3072,1024]{2,1,0:T(8,128)(2,1)}, bf16[16,3072,1024]{2,1,0:T(8,128)(2,1)}, f32[2,2,3,2,512,512]{5,4,3,2,1,0:T(8,128)}) custom-call(s32[16]{0:T(128)} %get-tuple-element.57.count_ref, s32[2]{0:T(128)} %broadcast_2_flip_ref.2.flip_ref, ...), custom_call_target="tpu_custom_call", output_to_operand_aliasing={{0}: (2, {}), {1}: (3, {})} | custom-call | flops 112000000000 | bytes 200000000 | tf_op jit(solution)/shard_map/experts/pallas_call | solution.py:437
  571.5 0.9 copy-done.3
  573.0 20.6 %collective-permute-start.8 = (bf16[3,1,512,512]{3,2,0,1:T(8,128)(2,1)S(1)}, bf16[3,1,512,512]{3,2,0,1:T(8,128)(2,1)S(1)}, u32[]{:S(2)}, u32[]{:S(2)}) collective-permute-start(bf16[3,1,512,512]{3,2,0,1:T(8,128)(2,1)S(1)} %get-tuple-element.108), channel_id=1, source_target_pairs={{0,4},{4,0},{1,5},{5,1},{2,6},{6,2},{3,7},{7,3}} | collective-permute-start | bytes 4718600 | tf_op jit(solution)/shard_map/ppermute | solution.py:618
  593.5 18.4 %collective-permute-done.8 = bf16[3,1,512,512]{3,2,0,1:T(8,128)(2,1)S(1)} collective-permute-done((bf16[3,1,512,512]{3,2,0,1:T(8,128)(2,1)S(1)}, bf16[3,1,512,512]{3,2,0,1:T(8,128)(2,1)S(1)}, u32[]{:S(2)}, u32[]{:S(2)}) %collective-permute-start.8) | collective-permute-done | bytes 1572896 | tf_op jit(solution)/shard_map/ppermute | solution.py:618
  612.0 2.7 collective-permute-done.7
  614.7 67.5 %collective-permute-done.9 = bf16[3,1,512,512]{3,2,0,1:T(8,128)(2,1)S(1)} collective-permute-done((bf16[3,1,512,512]{3,2,0,1:T(8,128)(2,1)S(1)}, bf16[3,1,512,512]{3,2,0,1:T(8,128)(2,1)S(1)}, u32[]{:S(2)}, u32[]{:S(2)}) %collective-permute-start.9) | collective-permute-done | bytes 1572896 | tf_op jit(solution)/shard_map/ppermute | solution.py:615
  682.2 3.2 pad_maximum_fusion.1.w_lo.w_hi
  685.3 46.3 %experts.6 = (bf16[16,3072,1024]{2,1,0:T(8,128)(2,1)}, bf16[16,3072,1024]{2,1,0:T(8,128)(2,1)}, f32[2,2,3,1,512,512]{5,4,3,2,1,0:T(8,128)}) custom-call(s32[16]{0:T(128)} %get-tuple-element.57.count_ref, s32[2]{0:T(128)} %pad_add_fusion.1.flip_ref, bf16[16,3072,1024]{2,1,0:T(8,128)(2,1)} %get-tuple-element.68.r_hbm, ...), custom_call_target="tpu_custom_call", output_to_operand_aliasing={{0}: (2, {}), {1}: (3, {})} | custom-call | flops 56000000000 | bytes 100000000 | tf_op jit(solution)/shard_map/experts/pallas_call | solution.py:437
  731.7 201.2 %experts.7 = (bf16[16,3072,1024]{2,1,0:T(8,128)(2,1)}, bf16[16,3072,1024]{2,1,0:T(8,128)(2,1)}, f32[2,2,3,4,512,512]{5,4,3,2,1,0:T(8,128)}) custom-call(s32[16]{0:T(128)} %get-tuple-element.57.count_ref, s32[2]{0:T(128)} %broadcast_2_flip_ref.2.flip_ref, ...), custom_call_target="tpu_custom_call", output_to_operand_aliasing={{0}: (2, {}), {1}: (3, {})} | custom-call | flops 224000000000 | bytes 400000000 | tf_op jit(solution)/shard_map/experts/pallas_call | solution.py:437
  932.9 48.7 %combine.2 = (f32[4096,1024]{1,0:T(8,128)}, f32[4096,1024]{1,0:T(8,128)}) custom-call(s32[32,16]{1,0:T(8,128)} %get-tuple-element.54.start_ref, s32[32,16]{1,0:T(8,128)} %get-tuple-element.55.rows_ref, s32[32,16]{1,0:T(8,128)} %get-tuple-element.56.off_ref, bf16[16,3072,1024]{2,1,0:T(8,128)(2,1)} %get-tuple-element.72.y_hbm, ...), custom_call_target="tpu_custom_call" | custom-call | flops 44999999488 | bytes 120000000 | tf_op jit(solution)/shard_map/combine/pallas_call | solution.py:540
  981.6 64.6 %collective-permute-start.10 = (f32[4096,1024]{1,0:T(8,128)}, f32[4096,1024]{1,0:T(8,128)}, u32[]{:S(2)}, u32[]{:S(2)}) collective-permute-start(f32[4096,1024]{1,0:T(8,128)} %get-tuple-element.74), channel_id=1, source_target_pairs={{0,1},{1,0},{2,3},{3,2},{4,5},{5,4},{6,7},{7,6}} | collective-permute-start | bytes 50331656 | tf_op jit(solution)/shard_map/ppermute | solution.py:612
  1046.3 3.8 slice_bitcast_fusion
  1050.1 3.1 copy-done.2
  1053.2 0.7 slice_bitcast_fusion.2
  1054.0 268.3 %collective-permute-done.14 = f32[2,3,1,512,512]{4,3,1,2,0:T(8,128)} collective-permute-done((f32[2,3,1,512,512]{4,3,1,2,0:T(8,128)S(1)}, f32[2,3,1,512,512]{4,3,1,2,0:T(8,128)}, u32[]{:S(2)}, u32[]{:S(2)}) %collective-permute-start.14) | collective-permute-done | bytes 6291488 | tf_op jit(solution)/shard_map/ppermute | solution.py:615
  1322.3 6.6 fusion
  1328.9 3.4 slice_bitcast_fusion.4
  1332.3 6.5 fusion.1
  1338.8 3.4 slice_bitcast_fusion.6
  1342.4 59.1 %combine.3 = (bf16[4096,1024]{1,0:T(8,128)(2,1)}, bf16[4096,1024]{1,0:T(8,128)(2,1)}) custom-call(s32[32,16]{1,0:T(8,128)} %get-tuple-element.54.start_ref, s32[32,16]{1,0:T(8,128)} %get-tuple-element.55.rows_ref, s32[32,16]{1,0:T(8,128)} %get-tuple-element.56.off_ref, bf16[16,3072,1024]{2,1,0:T(8,128)(2,1)} %get-tuple-element.72.y_hbm, ...), custom_call_target="tpu_custom_call" | custom-call | flops 44999999488 | bytes 120000000 | tf_op jit(solution)/shard_map/combine/pallas_call | solution.py:540
  1401.5 185.2 %attention_grad.1 = bf16[8,512,1024]{2,1,0:T(8,128)(2,1)} custom-call(bf16[8,512,1024]{2,1,0:T(8,128)(2,1)} %bitcast.134, bf16[8,512,1024]{2,1,0:T(8,128)(2,1)} %x_ref.1, bf16[8,512,3072]{2,1,0:T(8,128)(2,1)} %get-tuple-element.78.qkv_ref, bf16[2,4,1024,512]{3,2,1,0:T(8,128)(2,1)} %bitcast.132), custom_call_target="tpu_custom_call" | custom-call | flops 149999992832 | bytes 70000000 | tf_op jit(solution)/shard_map/attention_grad/pallas_call | solution.py:157
  1586.7 4.8 place.4
  1591.4 4.7 place.5
  1596.1 4.7 place.6
  1600.8 6.0 reduce-scatter.7.cloned.1.call-done
  1606.8 9.4 place.7
  (48 shorter events, 1.5 us)
Async XLA Ops:
  7.2 2.0 copy-start
  7.2 52.5 %all-gather.7.cloned.1.call-start = ((), (), s32[]{:S(2)}) async-start(), calls=%async_computation.2 | async-start | bytes 9437184 | tf_op jit(solution)/shard_map/all_gather | solution.py:627
  10.3 477.0 %all-gather.9.cloned.1.call-start = ((), (), s32[]{:S(2)}) async-start(), calls=%async_computation.3 | async-start | bytes 15728640 | tf_op jit(solution)/shard_map/all_gather | solution.py:632
  15.3 716.3 %all-gather.11.cloned.1.call-start = ((), (), s32[]{:S(2)}) async-start(), calls=%async_computation.4 | async-start | bytes 31457280 | tf_op jit(solution)/shard_map/all_gather | solution.py:632
  23.3 0.8 copy-start.6
  23.3 1.5 copy-start.7
  23.3 1.5 copy-start.8
  23.4 1563.3 %reduce-scatter.9.cloned.1.call-start = ((), (), s32[]{:S(2)}) async-start(), calls=%async_computation.6 | async-start | bytes 31457280
  24.2 1.6 collective-permute-start.1
  24.9 1.5 collective-permute-start
  25.1 367.3 %collective-permute-start.3 = (bf16[4096,1024]{1,0:T(8,128)(2,1)}, bf16[4096,1024]{1,0:T(8,128)(2,1)}, u32[]{:S(2)}, u32[]{:S(2)}) collective-permute-start(bf16[4096,1024]{1,0:T(8,128)(2,1)} %bitcast.108), channel_id=1, source_target_pairs={{0,1},{1,0},{2,3},{3,2},{4,5},{5,4},{6,7},{7,6}} | collective-permute-start | bytes 25165832 | tf_op jit(solution)/shard_map/ppermute | solution.py:612
  203.8 188.5 %collective-permute-start.2 = (bf16[4096,1024]{1,0:T(8,128)(2,1)}, bf16[4096,1024]{1,0:T(8,128)(2,1)}, u32[]{:S(2)}, u32[]{:S(2)}) collective-permute-start(bf16[4096,1024]{1,0:T(8,128)(2,1)} %bitcast.111), channel_id=1, source_target_pairs={{0,1},{1,0},{2,3},{3,2},{4,5},{5,4},{6,7},{7,6}} | collective-permute-start | bytes 25165832 | tf_op jit(solution)/shard_map/ppermute | solution.py:612
  210.2 70.4 %collective-permute-start.4 = (bf16[3,1,512,512]{3,2,0,1:T(8,128)(2,1)}, bf16[3,1,512,512]{3,2,0,1:T(8,128)(2,1)S(1)}, u32[]{:S(2)}, u32[]{:S(2)}) collective-permute-start(bf16[3,1,512,512]{3,2,0,1:T(8,128)(2,1)} %get-tuple-element.110), channel_id=1, source_target_pairs={{0,2},{1,3},{2,0},{3,1},{4,6},{5,7},{6,4},{7,5}} | collective-permute-start | bytes 4718600 | tf_op jit(solution)/shard_map/ppermute | solution.py:615
  211.0 71.4 %collective-permute-start.5 = (bf16[3,1,512,512]{3,2,0,1:T(8,128)(2,1)}, bf16[3,1,512,512]{3,2,0,1:T(8,128)(2,1)}, u32[]{:S(2)}, u32[]{:S(2)}) collective-permute-start(bf16[3,1,512,512]{3,2,0,1:T(8,128)(2,1)} %get-tuple-element.110), channel_id=1, source_target_pairs={{0,4},{4,0},{1,5},{5,1},{2,6},{6,2},{3,7},{7,3}} | collective-permute-start | bytes 4718600 | tf_op jit(solution)/shard_map/ppermute | solution.py:618
  280.5 64.7 %collective-permute-start.6 = (bf16[3,1,512,512]{3,2,0,1:T(8,128)(2,1)S(1)}, bf16[3,1,512,512]{3,2,0,1:T(8,128)(2,1)}, u32[]{:S(2)}, u32[]{:S(2)}) collective-permute-start(bf16[3,1,512,512]{3,2,0,1:T(8,128)(2,1)S(1)} %collective-permute-done.4), channel_id=1, source_target_pairs={{0,4},{4,0},{1,5},{5,1},{2,6},{6,2},{3,7},{7,3}} | collective-permute-start | bytes 4718600 | tf_op jit(solution)/shard_map/ppermute | solution.py:618
  571.4 1.0 copy-start.3
  571.4 1.2 copy-start.4
  571.4 1.3 copy-start.5
  571.4 1035.4 %reduce-scatter.7.cloned.1.call-start = ((), (), s32[]{:S(2)}) async-start(), calls=%async_computation.5 | async-start | bytes 62914560
  573.0 39.0 %collective-permute-start.8 = (bf16[3,1,512,512]{3,2,0,1:T(8,128)(2,1)S(1)}, bf16[3,1,512,512]{3,2,0,1:T(8,128)(2,1)S(1)}, u32[]{:S(2)}, u32[]{:S(2)}) collective-permute-start(bf16[3,1,512,512]{3,2,0,1:T(8,128)(2,1)S(1)} %get-tuple-element.108), channel_id=1, source_target_pairs={{0,4},{4,0},{1,5},{5,1},{2,6},{6,2},{3,7},{7,3}} | collective-permute-start | bytes 4718600 | tf_op jit(solution)/shard_map/ppermute | solution.py:618
  593.5 21.2 %collective-permute-start.7 = (bf16[3,1,512,512]{3,2,0,1:T(8,128)(2,1)S(1)}, bf16[3,1,512,512]{3,2,0,1:T(8,128)(2,1)S(1)}, u32[]{:S(2)}, u32[]{:S(2)}) collective-permute-start(bf16[3,1,512,512]{3,2,0,1:T(8,128)(2,1)S(1)} %get-tuple-element.108), channel_id=1, source_target_pairs={{0,2},{1,3},{2,0},{3,1},{4,6},{5,7},{6,4},{7,5}} | collective-permute-start | bytes 4718600 | tf_op jit(solution)/shard_map/ppermute | solution.py:615
  612.0 70.2 %collective-permute-start.9 = (bf16[3,1,512,512]{3,2,0,1:T(8,128)(2,1)S(1)}, bf16[3,1,512,512]{3,2,0,1:T(8,128)(2,1)S(1)}, u32[]{:S(2)}, u32[]{:S(2)}) collective-permute-start(bf16[3,1,512,512]{3,2,0,1:T(8,128)(2,1)S(1)} %collective-permute-done.8), channel_id=1, source_target_pairs={{0,2},{1,3},{2,0},{3,1},{4,6},{5,7},{6,4},{7,5}} | collective-permute-start | bytes 4718600 | tf_op jit(solution)/shard_map/ppermute | solution.py:615
  981.6 360.7 %collective-permute-start.10 = (f32[4096,1024]{1,0:T(8,128)}, f32[4096,1024]{1,0:T(8,128)}, u32[]{:S(2)}, u32[]{:S(2)}) collective-permute-start(f32[4096,1024]{1,0:T(8,128)} %get-tuple-element.74), channel_id=1, source_target_pairs={{0,1},{1,0},{2,3},{3,2},{4,5},{5,4},{6,7},{7,6}} | collective-permute-start | bytes 50331656 | tf_op jit(solution)/shard_map/ppermute | solution.py:612
  1046.2 296.2 %collective-permute-start.11 = (f32[4096,1024]{1,0:T(8,128)}, f32[4096,1024]{1,0:T(8,128)}, u32[]{:S(2)}, u32[]{:S(2)}) collective-permute-start(f32[4096,1024]{1,0:T(8,128)} %get-tuple-element.75), channel_id=1, source_target_pairs={{0,1},{1,0},{2,3},{3,2},{4,5},{5,4},{6,7},{7,6}} | collective-permute-start | bytes 50331656 | tf_op jit(solution)/shard_map/ppermute | solution.py:612
  1046.3 7.0 copy-start.2
  1050.1 272.2 %collective-permute-start.14 = (f32[2,3,1,512,512]{4,3,1,2,0:T(8,128)S(1)}, f32[2,3,1,512,512]{4,3,1,2,0:T(8,128)}, u32[]{:S(2)}, u32[]{:S(2)}) collective-permute-start(f32[2,3,1,512,512]{4,3,1,2,0:T(8,128)S(1)} %slice_bitcast_fusion), channel_id=1, source_target_pairs={{0,2},{1,3},{2,0},{3,1},{4,6},{5,7},{6,4},{7,5}} | collective-permute-start | bytes 18874376 | tf_op jit(solution)/shard_map/ppermute | solution.py:615
  1054.0 278.3 %collective-permute-start.12 = (f32[2,3,1,512,512]{4,3,1,2,0:T(8,128)S(1)}, f32[2,3,1,512,512]{4,3,1,2,0:T(8,128)}, u32[]{:S(2)}, u32[]{:S(2)}) collective-permute-start(f32[2,3,1,512,512]{4,3,1,2,0:T(8,128)S(1)} %slice_bitcast_fusion.2), channel_id=1, source_target_pairs={{0,4},{4,0},{1,5},{5,1},{2,6},{6,2},{3,7},{7,3}} | collective-permute-start | bytes 18874376 | tf_op jit(solution)/shard_map/ppermute | solution.py:618
  1332.3 259.2 %collective-permute-start.15 = (f32[3,1,512,512]{3,2,1,0:T(8,128)}, f32[3,1,512,512]{3,2,1,0:T(8,128)}, u32[]{:S(2)}, u32[]{:S(2)}) collective-permute-start(f32[3,1,512,512]{3,2,1,0:T(8,128)} %get-tuple-element.95), channel_id=1, source_target_pairs={{0,4},{4,0},{1,5},{5,1},{2,6},{6,2},{3,7},{7,3}} | collective-permute-start | bytes 9437192 | tf_op jit(solution)/shard_map/ppermute | solution.py:618
  1342.2 253.9 %collective-permute-start.13 = (f32[3,1,512,512]{3,2,1,0:T(8,128)}, f32[3,1,512,512]{3,2,1,0:T(8,128)}, u32[]{:S(2)}, u32[]{:S(2)}) collective-permute-start(f32[3,1,512,512]{3,2,1,0:T(8,128)} %get-tuple-element.97), channel_id=1, source_target_pairs={{0,2},{1,3},{2,0},{3,1},{4,6},{5,7},{6,4},{7,5}} | collective-permute-start | bytes 9437192 | tf_op jit(solution)/shard_map/ppermute | solution.py:615
  1606.8 9.4 copy-start.1
Sparse Core Ops, SparseCore 0:
  10.4 49.2 all-gather.6
  62.0 116.2 all-gather.8
  180.6 284.9 all-gather.10
  571.5 302.0 reduce-scatter.8
  933.1 673.7 reduce-scatter.6

commit v5 on v4

--- a/solution.py
+++ b/solution.py
@@ -658,14 +658,18 @@
         h_other = swap(h_tok)
         held = dispatch(h_tok, dout_tok, dest, gate, segs, 0, [], n_local, max_rows)
         rows, d_rows = dispatch(h_other, dout_other, dest, gate, segs, n_blocks, held, n_local, max_rows)
-        sums, grads, start = [], [], 0
+        grads, start = [], 0
         for n, size in enumerate(CHUNKS):
-            rows, d_rows, d_w = experts(rows, d_rows, (w_a, w_b)[n], counts, flips, (first, mid)[n], local_experts, x_first=n == 0)
-            sums.append(d_w[0] + (swap_x, swap_y)[n](d_w[1]))
             rows, d_rows, d_w = experts(rows, d_rows, weights[n], counts, jnp.zeros_like(flips), start, local_experts)
             d_w = d_w.reshape(fsdp_size * n_side, *d_w.shape[2:])
             grads.append(([lax.psum_scatter(d_w, ('fsdp', 'ep'), scatter_dimension=0, tiled=False, axis_index_groups=groups)], start))
             start += size
+            if n == 0:
+                rows, d_rows, d_a = experts(rows, d_rows, w_a, counts, flips, first, local_experts, x_first=True)
+                rows, d_rows, d_b = experts(rows, d_rows, w_b, counts, flips, mid, local_experts)
+                d_a, d_b = lax.optimization_barrier((d_a, d_b))
+                more_a, more_b = swap_x(d_a[1]), swap_y(d_b[1])
+        sums = d_a[0] + more_a, d_b[0] + more_b
         more_a, more_b = swap_y(sums[0][1]), swap_x(sums[1][1])
         done = [grads[0], ([sums[0][0], more_a], first), ([sums[1][0], more_b], mid), grads[1]]
         sums = combine(rows, d_rows, dest, gate, segs, n_blocks, n_blocks, [])

time: 1640 us -> 1570 us (0.957)
  waiting for transfers between devices: 505 us -> 454 us
  starting transfers between devices: 89.7 us -> 72 us
    ppermute x5, waiting for transfers between devices: 407 us -> 135 us  [swap_x(): return lax.ppermute(values, 'ep', [(i, i ^ CORES) for i in range(ep_size)])]
    ppermute x5, waiting for transfers between devices: 81.4 us -> 301 us  [swap_y(): return lax.ppermute(values, 'fsdp', [(i, i ^ 1) for i in range(fsdp_size)])]
    ppermute x6, starting transfers between devices: 66.1 us -> 25.5 us  [swap(): return lax.ppermute(values, 'ep', [(i, i ^ 1) for i in range(ep_size)])]
    ppermute x5, starting transfers between devices: 1.05 us -> 34.6 us  [swap_x(): return lax.ppermute(values, 'ep', [(i, i ^ CORES) for i in range(ep_size)])]
  transfers between devices with their start and end apart: 21 -> 21, of which waited for: 9 -> 8; matrix products, arithmetic and copies ran while one was open for 4% -> 5% of each run, Pallas kernels for 57% -> 60%
where the time goes in v5:
time: 1570 us; the launch traced here: 1560 us
  Pallas kernels  938 us (60%)
  waiting for transfers between devices  454 us (29%)
  starting transfers between devices  72 us (5%)
  local copies, waits for them, and re-layouts  42.6 us (3%)
  other arithmetic  36.1 us (2%)
    pallas_call x4, Pallas kernels, experts(): pl.pallas_call(functools.partial(expert_kernel, expert_of=expert_of, x_fi...  383 us
    ppermute x5, waiting for transfers between devices, swap_y(): return lax.ppermute(values, 'fsdp', [(i, i ^ 1) for i in range(fsdp_size)])  301 us
    pallas_call x1, Pallas kernels, attention_grad(): pl.pallas_call(functools.partial(attention_grad_kernel, head_dim=head_dim...  185 us
    pallas_call x1, Pallas kernels, attention(): pl.pallas_call(functools.partial(attention_kernel, head_dim=head_dim), gr...  144 us
    ppermute x5, waiting for transfers between devices, swap_x(): return lax.ppermute(values, 'ep', [(i, i ^ CORES) for i in range(ep_size)])  135 us
    pallas_call x2, Pallas kernels, combine(): pl.pallas_call(functools.partial(combine_kernel, base=base, own=bool(extr...  108 us
    pallas_call x2, Pallas kernels, dispatch(): pl.pallas_call(functools.partial(dispatch_kernel, base=base), grid_spec=p...  84.8 us
    ppermute x5, starting transfers between devices, swap_x(): return lax.ppermute(values, 'ep', [(i, i ^ CORES) for i in range(ep_size)])  34.6 us
  transfers between devices with their start and end apart: 21, of which 8 were waited for; matrix products, arithmetic and copies ran while one was open for 5% of the time, Pallas kernels for 60%

profile of v5, /device:TPU:7, one launch (start us, length us, event | category | flops | bytes accessed | tf_op | source)
XLA Modules:
  0.0 1557.2 jit_solution(8513789257421598495)
XLA Ops:
  7.2 1.1 constant_dynamic-slice_fusion
  8.4 0.8 copy-done
  9.2 1.0 pad_maximum_fusion.6
  10.3 1.3 slice_bitcast_fusion.13
  11.6 1.7 slice_bitcast_fusion.11
  13.3 2.0 pad_maximum_fusion.3
  15.4 2.0 slice_bitcast_fusion.10
  17.4 2.8 slice_bitcast_fusion.8
  20.2 3.1 pad_maximum_fusion.2
  23.4 0.8 copy-done.3
  24.2 0.7 collective-permute-start.1
  25.1 0.4 collective-permute-start.3
  25.4 0.3 collective-permute-done.1
  25.8 0.7 fusion.7
  26.4 1.0 fusion.4.loc_ref
  27.5 9.2 route.1
  36.7 2.8 copy.49
  39.4 3.8 copy.50
  43.2 3.8 copy.51
  47.0 1.9 slice_reduce_fusion
  48.8 1.3 slice_bitcast_fusion.20
  50.2 9.5 all-gather.7.cloned.1.call-done
  59.7 144.2 %attention.1 = (bf16[8,512,1024]{2,1,0:T(8,128)(2,1)}, bf16[8,512,3072]{2,1,0:T(8,128)(2,1)}) custom-call(bf16[8,512,1024]{2,1,0:T(8,128)(2,1)} %x_ref.1, bf16[2,4,1024,512]{3,2,1,0:T(8,128)(2,1)} %bitcast.127), custom_call_target="tpu_custom_call" | custom-call | flops 89999998976 | bytes 60000000 | tf_op jit(solution)/shard_map/attention/pallas_call | solution.py:85
  203.8 0.3 collective-permute-start.2
  204.1 42.0 %dispatch.2 = (bf16[16,3072,1024]{2,1,0:T(8,128)(2,1)}, bf16[16,3072,1024]{2,1,0:T(8,128)(2,1)}) custom-call(s32[32,16]{1,0:T(8,128)} %get-tuple-element.56.start_ref, s32[32,16]{1,0:T(8,128)} %get-tuple-element.57.rows_ref, s32[32,16]{1,0:T(8,128)} %get-tuple-element.58.off_ref, bf16[4096,1024]{1,0:T(8,128)(2,1)} %bitcast.112, ...), custom_call_target="tpu_custom_call" | custom-call | flops 40000000000 | bytes 90000000 | tf_op jit(solution)/shard_map/dispatch/pallas_call | solution.py:307
  246.2 42.8 %dispatch.3 = (bf16[16,3072,1024]{2,1,0:T(8,128)(2,1)}, bf16[16,3072,1024]{2,1,0:T(8,128)(2,1)}) custom-call(s32[32,16]{1,0:T(8,128)} %get-tuple-element.56.start_ref, s32[32,16]{1,0:T(8,128)} %get-tuple-element.57.rows_ref, s32[32,16]{1,0:T(8,128)} %get-tuple-element.58.off_ref, ...), custom_call_target="tpu_custom_call", output_to_operand_aliasing={{0}: (7, {}), {1}: (8, {})} | custom-call | flops 40000000000 | bytes 90000000 | tf_op jit(solution)/shard_map/dispatch/pallas_call | solution.py:307
  289.0 0.5 broadcast_2_flip_ref.2.flip_ref
  289.5 84.1 %experts.4 = (bf16[16,3072,1024]{2,1,0:T(8,128)(2,1)}, bf16[16,3072,1024]{2,1,0:T(8,128)(2,1)}, f32[2,2,3,2,512,512]{5,4,3,2,1,0:T(8,128)}) custom-call(s32[16]{0:T(128)} %get-tuple-element.59.count_ref, s32[2]{0:T(128)} %broadcast_2_flip_ref.2.flip_ref, ...), custom_call_target="tpu_custom_call", output_to_operand_aliasing={{0}: (2, {}), {1}: (3, {})} | custom-call | flops 112000000000 | bytes 200000000 | tf_op jit(solution)/shard_map/experts/pallas_call | solution.py:437
  373.7 1.3 slice_bitcast_fusion.16
  374.9 1.7 slice_bitcast_fusion.14
  376.6 1.4 fusion.9
  378.0 9.7 collective-permute-start.8
  387.6 1.4 fusion.10
  389.0 17.8 %collective-permute-start.4 = (bf16[3,1,512,512]{3,2,0,1:T(8,128)(2,1)}, bf16[3,1,512,512]{3,2,0,1:T(8,128)(2,1)}, u32[]{:S(2)}, u32[]{:S(2)}) collective-permute-start(bf16[3,1,512,512]{3,2,0,1:T(8,128)(2,1)} %get-tuple-element.114), channel_id=1, source_target_pairs={{0,2},{1,3},{2,0},{3,1},{4,6},{5,7},{6,4},{7,5}} | collective-permute-start | bytes 4718600 | tf_op jit(solution)/shard_map/ppermute | solution.py:615
  406.8 35.1 %collective-permute-done.8 = bf16[3,1,512,512]{3,2,0,1:T(8,128)(2,1)} collective-permute-done((bf16[3,1,512,512]{3,2,0,1:T(8,128)(2,1)}, bf16[3,1,512,512]{3,2,0,1:T(8,128)(2,1)}, u32[]{:S(2)}, u32[]{:S(2)}) %collective-permute-start.8) | collective-permute-done | bytes 1572896 | tf_op jit(solution)/shard_map/ppermute | solution.py:618
  441.9 16.8 %collective-permute-start.9 = (bf16[3,1,512,512]{3,2,0,1:T(8,128)(2,1)}, bf16[3,1,512,512]{3,2,0,1:T(8,128)(2,1)}, u32[]{:S(2)}, u32[]{:S(2)}) collective-permute-start(bf16[3,1,512,512]{3,2,0,1:T(8,128)(2,1)} %collective-permute-done.8), channel_id=1, source_target_pairs={{0,2},{1,3},{2,0},{3,1},{4,6},{5,7},{6,4},{7,5}} | collective-permute-start | bytes 4718600 | tf_op jit(solution)/shard_map/ppermute | solution.py:615
  458.7 1.8 collective-permute-start.5
  460.5 2.6 collective-permute-done.4
  463.1 0.7 pad_add_fusion.1.flip_ref
  463.8 66.7 %collective-permute-done.7 = bf16[3,1,512,512]{3,2,0,1:T(8,128)(2,1)} collective-permute-done((bf16[3,1,512,512]{3,2,0,1:T(8,128)(2,1)}, bf16[3,1,512,512]{3,2,0,1:T(8,128)(2,1)}, u32[]{:S(2)}, u32[]{:S(2)}) %collective-permute-start.7) | collective-permute-done | bytes 1572896 | tf_op jit(solution)/shard_map/ppermute | solution.py:615
  530.5 66.1 %collective-permute-done.9 = bf16[3,1,512,512]{3,2,0,1:T(8,128)(2,1)} collective-permute-done((bf16[3,1,512,512]{3,2,0,1:T(8,128)(2,1)}, bf16[3,1,512,512]{3,2,0,1:T(8,128)(2,1)}, u32[]{:S(2)}, u32[]{:S(2)}) %collective-permute-start.9) | collective-permute-done | bytes 1572896 | tf_op jit(solution)/shard_map/ppermute | solution.py:615
  596.6 5.8 pad_maximum_fusion.1.w_lo.w_hi
  602.4 5.8 pad_maximum_fusion.w_lo.w_hi
  608.3 51.8 %experts.5 = (bf16[16,3072,1024]{2,1,0:T(8,128)(2,1)}, bf16[16,3072,1024]{2,1,0:T(8,128)(2,1)}, f32[2,2,3,1,512,512]{5,4,3,2,1,0:T(8,128)}) custom-call(s32[16]{0:T(128)} %get-tuple-element.59.count_ref, s32[2]{0:T(128)} %pad_add_fusion.1.flip_ref, bf16[16,3072,1024]{2,1,0:T(8,128)(2,1)} %get-tuple-element.68.r_hbm, ...), custom_call_target="tpu_custom_call", output_to_operand_aliasing={{0}: (2, {}), {1}: (3, {})} | custom-call | flops 56000000000 | bytes 100000000 | tf_op jit(solution)/shard_map/experts/pallas_call | solution.py:437
  660.1 46.2 %experts.6 = (bf16[16,3072,1024]{2,1,0:T(8,128)(2,1)}, bf16[16,3072,1024]{2,1,0:T(8,128)(2,1)}, f32[2,2,3,1,512,512]{5,4,3,2,1,0:T(8,128)}) custom-call(s32[16]{0:T(128)} %get-tuple-element.59.count_ref, s32[2]{0:T(128)} %pad_add_fusion.1.flip_ref, bf16[16,3072,1024]{2,1,0:T(8,128)(2,1)} %get-tuple-element.70.r_hbm, ...), custom_call_target="tpu_custom_call", output_to_operand_aliasing={{0}: (2, {}), {1}: (3, {})} | custom-call | flops 56000000000 | bytes 100000000 | tf_op jit(solution)/shard_map/experts/pallas_call | solution.py:437
  706.3 200.7 %experts.7 = (bf16[16,3072,1024]{2,1,0:T(8,128)(2,1)}, bf16[16,3072,1024]{2,1,0:T(8,128)(2,1)}, f32[2,2,3,4,512,512]{5,4,3,2,1,0:T(8,128)}) custom-call(s32[16]{0:T(128)} %get-tuple-element.59.count_ref, s32[2]{0:T(128)} %broadcast_2_flip_ref.2.flip_ref, ...), custom_call_target="tpu_custom_call", output_to_operand_aliasing={{0}: (2, {}), {1}: (3, {})} | custom-call | flops 224000000000 | bytes 400000000 | tf_op jit(solution)/shard_map/experts/pallas_call | solution.py:437
  907.0 49.4 %combine.2 = (f32[4096,1024]{1,0:T(8,128)}, f32[4096,1024]{1,0:T(8,128)}) custom-call(s32[32,16]{1,0:T(8,128)} %get-tuple-element.56.start_ref, s32[32,16]{1,0:T(8,128)} %get-tuple-element.57.rows_ref, s32[32,16]{1,0:T(8,128)} %get-tuple-element.58.off_ref, bf16[16,3072,1024]{2,1,0:T(8,128)(2,1)} %get-tuple-element.74.y_hbm, ...), custom_call_target="tpu_custom_call" | custom-call | flops 44999999488 | bytes 120000000 | tf_op jit(solution)/shard_map/combine/pallas_call | solution.py:540
  956.5 24.0 %collective-permute-start.10 = (f32[4096,1024]{1,0:T(8,128)}, f32[4096,1024]{1,0:T(8,128)}, u32[]{:S(2)}, u32[]{:S(2)}) collective-permute-start(f32[4096,1024]{1,0:T(8,128)} %get-tuple-element.76), channel_id=1, source_target_pairs={{0,1},{1,0},{2,3},{3,2},{4,5},{5,4},{6,7},{7,6}} | collective-permute-start | bytes 50331656 | tf_op jit(solution)/shard_map/ppermute | solution.py:612
  980.5 3.8 slice_bitcast_fusion.2
  984.3 3.1 copy-done.2
  987.5 3.4 slice_bitcast_fusion
  990.9 265.7 %collective-permute-done.12 = f32[2,3,1,512,512]{4,3,1,2,0:T(8,128)} collective-permute-done((f32[2,3,1,512,512]{4,3,1,2,0:T(8,128)S(1)}, f32[2,3,1,512,512]{4,3,1,2,0:T(8,128)}, u32[]{:S(2)}, u32[]{:S(2)}) %collective-permute-start.12) | collective-permute-done | bytes 6291488 | tf_op jit(solution)/shard_map/ppermute | solution.py:618
  1256.6 6.6 fusion.1
  1263.1 3.4 slice_bitcast_fusion.6
  1266.5 4.7 fusion
  1271.2 3.3 slice_bitcast_fusion.4
  1274.5 0.2 collective-permute-start.15
  1274.8 58.9 %combine.3 = (bf16[4096,1024]{1,0:T(8,128)(2,1)}, bf16[4096,1024]{1,0:T(8,128)(2,1)}) custom-call(s32[32,16]{1,0:T(8,128)} %get-tuple-element.56.start_ref, s32[32,16]{1,0:T(8,128)} %get-tuple-element.57.rows_ref, s32[32,16]{1,0:T(8,128)} %get-tuple-element.58.off_ref, bf16[16,3072,1024]{2,1,0:T(8,128)(2,1)} %get-tuple-element.74.y_hbm, ...), custom_call_target="tpu_custom_call" | custom-call | flops 44999999488 | bytes 120000000 | tf_op jit(solution)/shard_map/combine/pallas_call | solution.py:540
  1333.7 185.1 %attention_grad.1 = bf16[8,512,1024]{2,1,0:T(8,128)(2,1)} custom-call(bf16[8,512,1024]{2,1,0:T(8,128)(2,1)} %bitcast.130, bf16[8,512,1024]{2,1,0:T(8,128)(2,1)} %x_ref.1, bf16[8,512,3072]{2,1,0:T(8,128)(2,1)} %get-tuple-element.80.qkv_ref, bf16[2,4,1024,512]{3,2,1,0:T(8,128)(2,1)} %bitcast.128), custom_call_target="tpu_custom_call" | custom-call | flops 149999992832 | bytes 70000000 | tf_op jit(solution)/shard_map/attention_grad/pallas_call | solution.py:157
  1518.8 5.2 place.4
  1524.0 4.7 place.5
  1528.7 4.6 place.6
  1533.3 7.7 reduce-scatter.7.cloned.1.call-done
  1541.0 9.4 place.7
  (42 shorter events, 0.7 us)
Async XLA Ops:
  7.2 2.0 copy-start
  7.2 52.5 %all-gather.7.cloned.1.call-start = ((), (), s32[]{:S(2)}) async-start(), calls=%async_computation.2 | async-start | bytes 9437184 | tf_op jit(solution)/shard_map/all_gather | solution.py:627
  10.3 278.7 %all-gather.9.cloned.1.call-start = ((), (), s32[]{:S(2)}) async-start(), calls=%async_computation.3 | async-start | bytes 15728640 | tf_op jit(solution)/shard_map/all_gather | solution.py:632
  15.3 691.0 %all-gather.11.cloned.1.call-start = ((), (), s32[]{:S(2)}) async-start(), calls=%async_computation.4 | async-start | bytes 31457280 | tf_op jit(solution)/shard_map/all_gather | solution.py:632
  23.3 0.8 copy-start.3
  23.3 1.5 copy-start.4
  23.3 1.5 copy-start.5
  23.4 1495.5 %reduce-scatter.9.cloned.1.call-start = ((), (), s32[]{:S(2)}) async-start(), calls=%async_computation.6 | async-start | bytes 31457280
  24.2 1.6 collective-permute-start.1
  24.9 1.5 collective-permute-start
  25.1 221.1 %collective-permute-start.3 = (bf16[4096,1024]{1,0:T(8,128)(2,1)}, bf16[4096,1024]{1,0:T(8,128)(2,1)}, u32[]{:S(2)}, u32[]{:S(2)}) collective-permute-start(bf16[4096,1024]{1,0:T(8,128)(2,1)} %bitcast.108), channel_id=1, source_target_pairs={{0,1},{1,0},{2,3},{3,2},{4,5},{5,4},{6,7},{7,6}} | collective-permute-start | bytes 25165832 | tf_op jit(solution)/shard_map/ppermute | solution.py:612
  203.8 42.3 %collective-permute-start.2 = (bf16[4096,1024]{1,0:T(8,128)(2,1)}, bf16[4096,1024]{1,0:T(8,128)(2,1)}, u32[]{:S(2)}, u32[]{:S(2)}) collective-permute-start(bf16[4096,1024]{1,0:T(8,128)(2,1)} %bitcast.111), channel_id=1, source_target_pairs={{0,1},{1,0},{2,3},{3,2},{4,5},{5,4},{6,7},{7,6}} | collective-permute-start | bytes 25165832 | tf_op jit(solution)/shard_map/ppermute | solution.py:612
  373.6 1167.4 %reduce-scatter.7.cloned.1.call-start = ((), (), s32[]{:S(2)}) async-start(), calls=%async_computation.5 | async-start | bytes 62914560
  378.0 64.0 %collective-permute-start.8 = (bf16[3,1,512,512]{3,2,0,1:T(8,128)(2,1)}, bf16[3,1,512,512]{3,2,0,1:T(8,128)(2,1)}, u32[]{:S(2)}, u32[]{:S(2)}) collective-permute-start(bf16[3,1,512,512]{3,2,0,1:T(8,128)(2,1)} %get-tuple-element.112), channel_id=1, source_target_pairs={{0,4},{4,0},{1,5},{5,1},{2,6},{6,2},{3,7},{7,3}} | collective-permute-start | bytes 4718600 | tf_op jit(solution)/shard_map/ppermute | solution.py:618
  389.0 74.1 %collective-permute-start.4 = (bf16[3,1,512,512]{3,2,0,1:T(8,128)(2,1)}, bf16[3,1,512,512]{3,2,0,1:T(8,128)(2,1)}, u32[]{:S(2)}, u32[]{:S(2)}) collective-permute-start(bf16[3,1,512,512]{3,2,0,1:T(8,128)(2,1)} %get-tuple-element.114), channel_id=1, source_target_pairs={{0,2},{1,3},{2,0},{3,1},{4,6},{5,7},{6,4},{7,5}} | collective-permute-start | bytes 4718600 | tf_op jit(solution)/shard_map/ppermute | solution.py:615
  406.8 123.7 %collective-permute-start.7 = (bf16[3,1,512,512]{3,2,0,1:T(8,128)(2,1)}, bf16[3,1,512,512]{3,2,0,1:T(8,128)(2,1)}, u32[]{:S(2)}, u32[]{:S(2)}) collective-permute-start(bf16[3,1,512,512]{3,2,0,1:T(8,128)(2,1)} %get-tuple-element.112), channel_id=1, source_target_pairs={{0,2},{1,3},{2,0},{3,1},{4,6},{5,7},{6,4},{7,5}} | collective-permute-start | bytes 4718600 | tf_op jit(solution)/shard_map/ppermute | solution.py:615
  441.9 154.7 %collective-permute-start.9 = (bf16[3,1,512,512]{3,2,0,1:T(8,128)(2,1)}, bf16[3,1,512,512]{3,2,0,1:T(8,128)(2,1)}, u32[]{:S(2)}, u32[]{:S(2)}) collective-permute-start(bf16[3,1,512,512]{3,2,0,1:T(8,128)(2,1)} %collective-permute-done.8), channel_id=1, source_target_pairs={{0,2},{1,3},{2,0},{3,1},{4,6},{5,7},{6,4},{7,5}} | collective-permute-start | bytes 4718600 | tf_op jit(solution)/shard_map/ppermute | solution.py:615
  458.7 143.7 %collective-permute-start.5 = (bf16[3,1,512,512]{3,2,0,1:T(8,128)(2,1)}, bf16[3,1,512,512]{3,2,0,1:T(8,128)(2,1)}, u32[]{:S(2)}, u32[]{:S(2)}) collective-permute-start(bf16[3,1,512,512]{3,2,0,1:T(8,128)(2,1)} %get-tuple-element.114), channel_id=1, source_target_pairs={{0,4},{4,0},{1,5},{5,1},{2,6},{6,2},{3,7},{7,3}} | collective-permute-start | bytes 4718600 | tf_op jit(solution)/shard_map/ppermute | solution.py:618
  463.1 139.3 %collective-permute-start.6 = (bf16[3,1,512,512]{3,2,0,1:T(8,128)(2,1)}, bf16[3,1,512,512]{3,2,0,1:T(8,128)(2,1)}, u32[]{:S(2)}, u32[]{:S(2)}) collective-permute-start(bf16[3,1,512,512]{3,2,0,1:T(8,128)(2,1)} %collective-permute-done.4), channel_id=1, source_target_pairs={{0,4},{4,0},{1,5},{5,1},{2,6},{6,2},{3,7},{7,3}} | collective-permute-start | bytes 4718600 | tf_op jit(solution)/shard_map/ppermute | solution.py:618
  956.5 318.3 %collective-permute-start.10 = (f32[4096,1024]{1,0:T(8,128)}, f32[4096,1024]{1,0:T(8,128)}, u32[]{:S(2)}, u32[]{:S(2)}) collective-permute-start(f32[4096,1024]{1,0:T(8,128)} %get-tuple-element.76), channel_id=1, source_target_pairs={{0,1},{1,0},{2,3},{3,2},{4,5},{5,4},{6,7},{7,6}} | collective-permute-start | bytes 50331656 | tf_op jit(solution)/shard_map/ppermute | solution.py:612
  980.5 294.3 %collective-permute-start.11 = (f32[4096,1024]{1,0:T(8,128)}, f32[4096,1024]{1,0:T(8,128)}, u32[]{:S(2)}, u32[]{:S(2)}) collective-permute-start(f32[4096,1024]{1,0:T(8,128)} %get-tuple-element.77), channel_id=1, source_target_pairs={{0,1},{1,0},{2,3},{3,2},{4,5},{5,4},{6,7},{7,6}} | collective-permute-start | bytes 50331656 | tf_op jit(solution)/shard_map/ppermute | solution.py:612
  980.5 7.0 copy-start.2
  984.3 272.2 %collective-permute-start.12 = (f32[2,3,1,512,512]{4,3,1,2,0:T(8,128)S(1)}, f32[2,3,1,512,512]{4,3,1,2,0:T(8,128)}, u32[]{:S(2)}, u32[]{:S(2)}) collective-permute-start(f32[2,3,1,512,512]{4,3,1,2,0:T(8,128)S(1)} %slice_bitcast_fusion.2), channel_id=1, source_target_pairs={{0,4},{4,0},{1,5},{5,1},{2,6},{6,2},{3,7},{7,3}} | collective-permute-start | bytes 18874376 | tf_op jit(solution)/shard_map/ppermute | solution.py:618
  990.9 275.6 %collective-permute-start.14 = (f32[2,3,1,512,512]{4,3,1,2,0:T(8,128)}, f32[2,3,1,512,512]{4,3,1,2,0:T(8,128)}, u32[]{:S(2)}, u32[]{:S(2)}) collective-permute-start(f32[2,3,1,512,512]{4,3,1,2,0:T(8,128)} %slice_bitcast_fusion), channel_id=1, source_target_pairs={{0,2},{1,3},{2,0},{3,1},{4,6},{5,7},{6,4},{7,5}} | collective-permute-start | bytes 18874376 | tf_op jit(solution)/shard_map/ppermute | solution.py:615
  1266.5 262.2 %collective-permute-start.13 = (f32[3,1,512,512]{3,2,1,0:T(8,128)}, f32[3,1,512,512]{3,2,1,0:T(8,128)}, u32[]{:S(2)}, u32[]{:S(2)}) collective-permute-start(f32[3,1,512,512]{3,2,1,0:T(8,128)} %get-tuple-element.101), channel_id=1, source_target_pairs={{0,2},{1,3},{2,0},{3,1},{4,6},{5,7},{6,4},{7,5}} | collective-permute-start | bytes 9437192 | tf_op jit(solution)/shard_map/ppermute | solution.py:615
  1274.5 249.5 %collective-permute-start.15 = (f32[3,1,512,512]{3,2,1,0:T(8,128)}, f32[3,1,512,512]{3,2,1,0:T(8,128)}, u32[]{:S(2)}, u32[]{:S(2)}) collective-permute-start(f32[3,1,512,512]{3,2,1,0:T(8,128)} %get-tuple-element.99), channel_id=1, source_target_pairs={{0,4},{4,0},{1,5},{5,1},{2,6},{6,2},{3,7},{7,3}} | collective-permute-start | bytes 9437192 | tf_op jit(solution)/shard_map/ppermute | solution.py:618
  1541.0 9.4 copy-start.1
Sparse Core Ops, SparseCore 0:
  10.4 49.2 all-gather.6
  62.0 116.2 all-gather.8
  180.7 230.0 all-gather.10
  413.7 304.8 reduce-scatter.8
  907.2 633.8 reduce-scatter.6

commit v6 on v5

--- a/solution.py
+++ b/solution.py
@@ -618,7 +618,7 @@
             return lax.ppermute(values, 'fsdp', [(i, i ^ 1) for i in range(fsdp_size)])
 
         def own_weights(part):
-            return jnp.stack([w_gate[part], w_up[part], w_down[part]], axis=0)
+            return jnp.stack([w[part] for w in all_w], axis=0)
 
         _, head_dim, _ = w_out.shape
         qkv_rows = w_qkv.transpose(1, 2, 3, 0).reshape(-1, half)
@@ -626,15 +626,17 @@
         out_rows = lax.dynamic_slice_in_dim(w_out.reshape(-1, half), ep * (d_model // ep_size), d_model // ep_size, axis=0)
         attn_w = lax.all_gather(jnp.concatenate([qkv_rows, out_rows], axis=0), ('fsdp', 'ep'), axis=0, tiled=False)
         attn_w = attn_w.reshape(fsdp_size, ep_size, -1, half)
-        weights, first = [], 0
-        for size in CHUNKS:
-            mine = own_weights(slice(first, first + size))
-            full = lax.all_gather(mine, ('fsdp', 'ep'), axis=0, tiled=False, axis_index_groups=groups)
-            weights.append(full)
-            first += size
+        all_w = w_gate, w_up, w_down
+        first = sum(CHUNKS)
         mid = first + (local_experts - first) // 2
         w_a, w_b = own_weights(slice(first, mid)), own_weights(slice(mid, local_experts))
         w_ax, w_ay, w_bx, w_by = swap_x(w_a), swap_y(w_a), swap_x(w_b), swap_y(w_b)
+        weights, start = [], 0
+        all_w, w_a, w_b = lax.optimization_barrier((all_w, w_a, w_b))
+        for size in CHUNKS:
+            mine = own_weights(slice(start, start + size))
+            weights.append(lax.all_gather(mine, ('fsdp', 'ep'), axis=0, tiled=False, axis_index_groups=groups))
+            start += size
 
         dout_tok = d_out.reshape(tok_count, d_model)
         dout_other = swap(dout_tok)

time: 1570 us -> 1560 us (level)
    ppermute x5, waiting for transfers between devices: 135 us -> 28.2 us  [swap_x(): return lax.ppermute(values, 'ep', [(i, i ^ CORES) for i in range(ep_size)])]
    ppermute x5, waiting for transfers between devices: 301 us -> 398 us  [swap_y(): return lax.ppermute(values, 'fsdp', [(i, i ^ 1) for i in range(fsdp_size)])]
    ppermute x5, starting transfers between devices: 34.6 us -> 5.39 us  [swap_x(): return lax.ppermute(values, 'ep', [(i, i ^ CORES) for i in range(ep_size)])]
    ppermute x5, starting transfers between devices: 11.7 us -> 39.8 us  [swap_y(): return lax.ppermute(values, 'fsdp', [(i, i ^ 1) for i in range(fsdp_size)])]
  transfers between devices with their start and end apart: 21 -> 21, of which waited for: 8 -> 7; matrix products, arithmetic and copies ran while one was open for 5% -> 5% of each run, Pallas kernels for 60% -> 60%
where the time goes in v6:
time: 1560 us; the launch traced here: 1550 us
  Pallas kernels  938 us (60%)
  waiting for transfers between devices  441 us (28%)
  starting transfers between devices  77.4 us (5%)
  local copies, waits for them, and re-layouts  43.8 us (3%)
  other arithmetic  35.8 us (2%)
    ppermute x5, waiting for transfers between devices, swap_y(): return lax.ppermute(values, 'fsdp', [(i, i ^ 1) for i in range(fsdp_size)])  398 us
    pallas_call x4, Pallas kernels, experts(): pl.pallas_call(functools.partial(expert_kernel, expert_of=expert_of, x_fi...  383 us
    pallas_call x1, Pallas kernels, attention_grad(): pl.pallas_call(functools.partial(attention_grad_kernel, head_dim=head_dim...  185 us
    pallas_call x1, Pallas kernels, attention(): pl.pallas_call(functools.partial(attention_kernel, head_dim=head_dim), gr...  144 us
    pallas_call x2, Pallas kernels, combine(): pl.pallas_call(functools.partial(combine_kernel, base=base, own=bool(extr...  108 us
    pallas_call x2, Pallas kernels, dispatch(): pl.pallas_call(functools.partial(dispatch_kernel, base=base), grid_spec=p...  84.9 us
    ppermute x5, starting transfers between devices, swap_y(): return lax.ppermute(values, 'fsdp', [(i, i ^ 1) for i in range(fsdp_size)])  39.8 us
    ppermute x6, starting transfers between devices, swap(): return lax.ppermute(values, 'ep', [(i, i ^ 1) for i in range(ep_size)])  31.7 us
  transfers between devices with their start and end apart: 21, of which 7 were waited for; matrix products, arithmetic and copies ran while one was open for 5% of the time, Pallas kernels for 60%

profile of v6, /device:TPU:7, one launch (start us, length us, event | category | flops | bytes accessed | tf_op | source)
XLA Modules:
  0.0 1549.7 jit_solution(11332547231432887634)
XLA Ops:
  7.2 1.1 constant_dynamic-slice_fusion
  8.4 0.8 copy-done
  9.2 1.1 pad_maximum_fusion.6
  10.3 1.3 slice_bitcast_fusion.16
  11.6 1.7 slice_bitcast_fusion.14
  13.3 1.3 pad_maximum_fusion.5
  14.6 1.3 pad_maximum_fusion.4
  15.9 1.4 slice_bitcast_fusion.13
  17.3 1.3 slice_bitcast_fusion.12
  18.7 1.3 slice_bitcast_fusion.11
  20.0 2.0 pad_maximum_fusion.3
  22.1 1.9 slice_bitcast_fusion.10
  23.9 1.7 slice_bitcast_fusion.9
  25.8 3.1 pad_maximum_fusion.2
  29.3 0.5 copy-done.6
  29.8 0.8 collective-permute-start.1
  30.8 0.4 collective-permute-start.3
  31.5 0.7 fusion.7
  32.2 1.0 fusion.4.loc_ref
  33.2 9.2 route.1
  42.4 2.8 copy.49
  45.2 3.8 copy.50
  48.9 3.8 copy.51
  52.7 1.8 slice_reduce_fusion
  54.6 1.3 slice_bitcast_fusion.20
  55.9 3.7 all-gather.7.cloned.1.call-done
  59.6 144.2 %attention.1 = (bf16[8,512,1024]{2,1,0:T(8,128)(2,1)}, bf16[8,512,3072]{2,1,0:T(8,128)(2,1)}) custom-call(bf16[8,512,1024]{2,1,0:T(8,128)(2,1)} %x_ref.1, bf16[2,4,1024,512]{3,2,1,0:T(8,128)(2,1)} %bitcast.127), custom_call_target="tpu_custom_call" | custom-call | flops 89999998976 | bytes 60000000 | tf_op jit(solution)/shard_map/attention/pallas_call | solution.py:85
  204.1 42.0 %dispatch.2 = (bf16[16,3072,1024]{2,1,0:T(8,128)(2,1)}, bf16[16,3072,1024]{2,1,0:T(8,128)(2,1)}) custom-call(s32[32,16]{1,0:T(8,128)} %get-tuple-element.61.start_ref, s32[32,16]{1,0:T(8,128)} %get-tuple-element.62.rows_ref, s32[32,16]{1,0:T(8,128)} %get-tuple-element.63.off_ref, bf16[4096,1024]{1,0:T(8,128)(2,1)} %bitcast.110, ...), custom_call_target="tpu_custom_call" | custom-call | flops 40000000000 | bytes 90000000 | tf_op jit(solution)/shard_map/dispatch/pallas_call | solution.py:307
  246.1 42.9 %dispatch.3 = (bf16[16,3072,1024]{2,1,0:T(8,128)(2,1)}, bf16[16,3072,1024]{2,1,0:T(8,128)(2,1)}) custom-call(s32[32,16]{1,0:T(8,128)} %get-tuple-element.61.start_ref, s32[32,16]{1,0:T(8,128)} %get-tuple-element.62.rows_ref, s32[32,16]{1,0:T(8,128)} %get-tuple-element.63.off_ref, ...), custom_call_target="tpu_custom_call", output_to_operand_aliasing={{0}: (7, {}), {1}: (8, {})} | custom-call | flops 40000000000 | bytes 90000000 | tf_op jit(solution)/shard_map/dispatch/pallas_call | solution.py:307
  289.0 0.5 broadcast_2_flip_ref.2.flip_ref
  289.6 84.1 %experts.4 = (bf16[16,3072,1024]{2,1,0:T(8,128)(2,1)}, bf16[16,3072,1024]{2,1,0:T(8,128)(2,1)}, f32[2,2,3,2,512,512]{5,4,3,2,1,0:T(8,128)}) custom-call(s32[16]{0:T(128)} %get-tuple-element.64.count_ref, s32[2]{0:T(128)} %broadcast_2_flip_ref.2.flip_ref, ...), custom_call_target="tpu_custom_call", output_to_operand_aliasing={{0}: (2, {}), {1}: (3, {})} | custom-call | flops 112000000000 | bytes 200000000 | tf_op jit(solution)/shard_map/experts/pallas_call | solution.py:437
  373.8 1.3 copy-done.4
  375.1 3.5 collective-permute-start.4
  378.6 23.9 %collective-permute-start.8 = (bf16[3,1,512,512]{3,2,0,1:T(8,128)(2,1)S(1)}, bf16[3,1,512,512]{3,2,0,1:T(8,128)(2,1)}, u32[]{:S(2)}, u32[]{:S(2)}) collective-permute-start(bf16[3,1,512,512]{3,2,0,1:T(8,128)(2,1)S(1)} %copy-done.3), channel_id=1, source_target_pairs={{0,4},{4,0},{1,5},{5,1},{2,6},{6,2},{3,7},{7,3}} | collective-permute-start | bytes 4718600 | tf_op jit(solution)/shard_map/ppermute | solution.py:618
  402.5 28.2 %collective-permute-done.4 = bf16[3,1,512,512]{3,2,0,1:T(8,128)(2,1)} collective-permute-done((bf16[3,1,512,512]{3,2,0,1:T(8,128)(2,1)S(1)}, bf16[3,1,512,512]{3,2,0,1:T(8,128)(2,1)}, u32[]{:S(2)}, u32[]{:S(2)}) %collective-permute-start.4) | collective-permute-done | bytes 1572896 | tf_op jit(solution)/shard_map/ppermute | solution.py:615
  430.7 15.4 collective-permute-start.6
  446.1 1.4 collective-permute-start.7
  447.5 0.5 collective-permute-start.9
  448.0 0.6 pad_add_fusion.1.flip_ref
  448.6 65.8 %collective-permute-done.5 = bf16[3,1,512,512]{3,2,0,1:T(8,128)(2,1)} collective-permute-done((bf16[3,1,512,512]{3,2,0,1:T(8,128)(2,1)S(1)}, bf16[3,1,512,512]{3,2,0,1:T(8,128)(2,1)}, u32[]{:S(2)}, u32[]{:S(2)}) %collective-permute-start.5) | collective-permute-done | bytes 1572896 | tf_op jit(solution)/shard_map/ppermute | solution.py:618
  514.3 66.5 %collective-permute-done.6 = bf16[3,1,512,512]{3,2,0,1:T(8,128)(2,1)} collective-permute-done((bf16[3,1,512,512]{3,2,0,1:T(8,128)(2,1)}, bf16[3,1,512,512]{3,2,0,1:T(8,128)(2,1)}, u32[]{:S(2)}, u32[]{:S(2)}) %collective-permute-start.6) | collective-permute-done | bytes 1572896 | tf_op jit(solution)/shard_map/ppermute | solution.py:618
  580.8 5.8 pad_maximum_fusion.w_lo.w_hi
  586.7 5.9 pad_maximum_fusion.1.w_lo.w_hi
  592.6 51.8 %experts.5 = (bf16[16,3072,1024]{2,1,0:T(8,128)(2,1)}, bf16[16,3072,1024]{2,1,0:T(8,128)(2,1)}, f32[2,2,3,1,512,512]{5,4,3,2,1,0:T(8,128)}) custom-call(s32[16]{0:T(128)} %get-tuple-element.64.count_ref, s32[2]{0:T(128)} %pad_add_fusion.1.flip_ref, bf16[16,3072,1024]{2,1,0:T(8,128)(2,1)} %get-tuple-element.76.r_hbm, ...), custom_call_target="tpu_custom_call", output_to_operand_aliasing={{0}: (2, {}), {1}: (3, {})} | custom-call | flops 56000000000 | bytes 100000000 | tf_op jit(solution)/shard_map/experts/pallas_call | solution.py:437
  644.5 46.1 %experts.6 = (bf16[16,3072,1024]{2,1,0:T(8,128)(2,1)}, bf16[16,3072,1024]{2,1,0:T(8,128)(2,1)}, f32[2,2,3,1,512,512]{5,4,3,2,1,0:T(8,128)}) custom-call(s32[16]{0:T(128)} %get-tuple-element.64.count_ref, s32[2]{0:T(128)} %pad_add_fusion.1.flip_ref, bf16[16,3072,1024]{2,1,0:T(8,128)(2,1)} %get-tuple-element.79.r_hbm, ...), custom_call_target="tpu_custom_call", output_to_operand_aliasing={{0}: (2, {}), {1}: (3, {})} | custom-call | flops 56000000000 | bytes 100000000 | tf_op jit(solution)/shard_map/experts/pallas_call | solution.py:437
  690.6 201.0 %experts.7 = (bf16[16,3072,1024]{2,1,0:T(8,128)(2,1)}, bf16[16,3072,1024]{2,1,0:T(8,128)(2,1)}, f32[2,2,3,4,512,512]{5,4,3,2,1,0:T(8,128)}) custom-call(s32[16]{0:T(128)} %get-tuple-element.64.count_ref, s32[2]{0:T(128)} %broadcast_2_flip_ref.2.flip_ref, ...), custom_call_target="tpu_custom_call", output_to_operand_aliasing={{0}: (2, {}), {1}: (3, {})} | custom-call | flops 224000000000 | bytes 400000000 | tf_op jit(solution)/shard_map/experts/pallas_call | solution.py:437
  891.6 49.5 %combine.2 = (f32[4096,1024]{1,0:T(8,128)}, f32[4096,1024]{1,0:T(8,128)}) custom-call(s32[32,16]{1,0:T(8,128)} %get-tuple-element.61.start_ref, s32[32,16]{1,0:T(8,128)} %get-tuple-element.62.rows_ref, s32[32,16]{1,0:T(8,128)} %get-tuple-element.63.off_ref, bf16[16,3072,1024]{2,1,0:T(8,128)(2,1)} %get-tuple-element.84.y_hbm, ...), custom_call_target="tpu_custom_call" | custom-call | flops 44999999488 | bytes 120000000 | tf_op jit(solution)/shard_map/combine/pallas_call | solution.py:540
  941.2 30.1 %collective-permute-start.10 = (f32[4096,1024]{1,0:T(8,128)}, f32[4096,1024]{1,0:T(8,128)}, u32[]{:S(2)}, u32[]{:S(2)}) collective-permute-start(f32[4096,1024]{1,0:T(8,128)} %get-tuple-element.86), channel_id=1, source_target_pairs={{0,1},{1,0},{2,3},{3,2},{4,5},{5,4},{6,7},{7,6}} | collective-permute-start | bytes 50331656 | tf_op jit(solution)/shard_map/ppermute | solution.py:612
  971.3 3.8 slice_bitcast_fusion.2
  975.2 3.1 copy-done.2
  978.3 3.4 slice_bitcast_fusion
  981.7 265.7 %collective-permute-done.12 = f32[2,3,1,512,512]{4,3,1,2,0:T(8,128)} collective-permute-done((f32[2,3,1,512,512]{4,3,1,2,0:T(8,128)S(1)}, f32[2,3,1,512,512]{4,3,1,2,0:T(8,128)}, u32[]{:S(2)}, u32[]{:S(2)}) %collective-permute-start.12) | collective-permute-done | bytes 6291488 | tf_op jit(solution)/shard_map/ppermute | solution.py:618
  1247.4 6.6 fusion.1
  1254.0 3.4 slice_bitcast_fusion.6
  1257.4 4.5 fusion
  1261.8 3.3 slice_bitcast_fusion.4
  1265.1 0.5 collective-permute-start.15
  1265.6 58.7 %combine.3 = (bf16[4096,1024]{1,0:T(8,128)(2,1)}, bf16[4096,1024]{1,0:T(8,128)(2,1)}) custom-call(s32[32,16]{1,0:T(8,128)} %get-tuple-element.61.start_ref, s32[32,16]{1,0:T(8,128)} %get-tuple-element.62.rows_ref, s32[32,16]{1,0:T(8,128)} %get-tuple-element.63.off_ref, bf16[16,3072,1024]{2,1,0:T(8,128)(2,1)} %get-tuple-element.84.y_hbm, ...), custom_call_target="tpu_custom_call" | custom-call | flops 44999999488 | bytes 120000000 | tf_op jit(solution)/shard_map/combine/pallas_call | solution.py:540
  1324.3 184.8 %attention_grad.1 = bf16[8,512,1024]{2,1,0:T(8,128)(2,1)} custom-call(bf16[8,512,1024]{2,1,0:T(8,128)(2,1)} %bitcast.130, bf16[8,512,1024]{2,1,0:T(8,128)(2,1)} %x_ref.1, bf16[8,512,3072]{2,1,0:T(8,128)(2,1)} %get-tuple-element.90.qkv_ref, bf16[2,4,1024,512]{3,2,1,0:T(8,128)(2,1)} %bitcast.128), custom_call_target="tpu_custom_call" | custom-call | flops 149999992832 | bytes 70000000 | tf_op jit(solution)/shard_map/attention_grad/pallas_call | solution.py:157
  1509.1 4.8 place.4
  1513.9 4.7 place.5
  1518.6 4.7 place.6
  1523.3 10.3 reduce-scatter.7.cloned.1.call-done
  1533.6 9.4 place.7
  (50 shorter events, 1.8 us)
Async XLA Ops:
  7.2 2.0 copy-start
  7.2 52.4 %all-gather.7.cloned.1.call-start = ((), (), s32[]{:S(2)}) async-start(), calls=%async_computation.2 | async-start | bytes 9437184 | tf_op jit(solution)/shard_map/all_gather | solution.py:627
  10.3 278.7 %all-gather.9.cloned.1.call-start = ((), (), s32[]{:S(2)}) async-start(), calls=%async_computation.3 | async-start | bytes 15728640 | tf_op jit(solution)/shard_map/all_gather | solution.py:638
  22.0 668.6 %all-gather.11.cloned.1.call-start = ((), (), s32[]{:S(2)}) async-start(), calls=%async_computation.4 | async-start | bytes 31457280 | tf_op jit(solution)/shard_map/all_gather | solution.py:638
  22.0 3.6 copy-start.5
  29.0 0.8 copy-start.6
  29.0 1.6 copy-start.7
  29.0 1.6 copy-start.8
  29.0 1480.1 %reduce-scatter.9.cloned.1.call-start = ((), (), s32[]{:S(2)}) async-start(), calls=%async_computation.6 | async-start | bytes 31457280
  29.8 1.7 collective-permute-start.1
  30.6 1.5 collective-permute-start
  30.8 215.3 %collective-permute-start.3 = (bf16[4096,1024]{1,0:T(8,128)(2,1)}, bf16[4096,1024]{1,0:T(8,128)(2,1)}, u32[]{:S(2)}, u32[]{:S(2)}) collective-permute-start(bf16[4096,1024]{1,0:T(8,128)(2,1)} %bitcast.106), channel_id=1, source_target_pairs={{0,1},{1,0},{2,3},{3,2},{4,5},{5,4},{6,7},{7,6}} | collective-permute-start | bytes 25165832 | tf_op jit(solution)/shard_map/ppermute | solution.py:612
  203.8 42.3 %collective-permute-start.2 = (bf16[4096,1024]{1,0:T(8,128)(2,1)}, bf16[4096,1024]{1,0:T(8,128)(2,1)}, u32[]{:S(2)}, u32[]{:S(2)}) collective-permute-start(bf16[4096,1024]{1,0:T(8,128)(2,1)} %bitcast.109), channel_id=1, source_target_pairs={{0,1},{1,0},{2,3},{3,2},{4,5},{5,4},{6,7},{7,6}} | collective-permute-start | bytes 25165832 | tf_op jit(solution)/shard_map/ppermute | solution.py:612
  373.7 1.4 copy-start.4
  373.7 4.9 copy-start.3
  373.8 1159.8 %reduce-scatter.7.cloned.1.call-start = ((), (), s32[]{:S(2)}) async-start(), calls=%async_computation.5 | async-start | bytes 62914560
  375.1 55.6 %collective-permute-start.4 = (bf16[3,1,512,512]{3,2,0,1:T(8,128)(2,1)S(1)}, bf16[3,1,512,512]{3,2,0,1:T(8,128)(2,1)}, u32[]{:S(2)}, u32[]{:S(2)}) collective-permute-start(bf16[3,1,512,512]{3,2,0,1:T(8,128)(2,1)S(1)} %copy-done.4), channel_id=1, source_target_pairs={{0,2},{1,3},{2,0},{3,1},{4,6},{5,7},{6,4},{7,5}} | collective-permute-start | bytes 4718600 | tf_op jit(solution)/shard_map/ppermute | solution.py:615
  378.6 68.9 %collective-permute-start.8 = (bf16[3,1,512,512]{3,2,0,1:T(8,128)(2,1)S(1)}, bf16[3,1,512,512]{3,2,0,1:T(8,128)(2,1)}, u32[]{:S(2)}, u32[]{:S(2)}) collective-permute-start(bf16[3,1,512,512]{3,2,0,1:T(8,128)(2,1)S(1)} %copy-done.3), channel_id=1, source_target_pairs={{0,4},{4,0},{1,5},{5,1},{2,6},{6,2},{3,7},{7,3}} | collective-permute-start | bytes 4718600 | tf_op jit(solution)/shard_map/ppermute | solution.py:618
  402.5 111.8 %collective-permute-start.5 = (bf16[3,1,512,512]{3,2,0,1:T(8,128)(2,1)S(1)}, bf16[3,1,512,512]{3,2,0,1:T(8,128)(2,1)}, u32[]{:S(2)}, u32[]{:S(2)}) collective-permute-start(bf16[3,1,512,512]{3,2,0,1:T(8,128)(2,1)S(1)} %copy-done.4), channel_id=1, source_target_pairs={{0,4},{4,0},{1,5},{5,1},{2,6},{6,2},{3,7},{7,3}} | collective-permute-start | bytes 4718600 | tf_op jit(solution)/shard_map/ppermute | solution.py:618
  430.7 150.2 %collective-permute-start.6 = (bf16[3,1,512,512]{3,2,0,1:T(8,128)(2,1)}, bf16[3,1,512,512]{3,2,0,1:T(8,128)(2,1)}, u32[]{:S(2)}, u32[]{:S(2)}) collective-permute-start(bf16[3,1,512,512]{3,2,0,1:T(8,128)(2,1)} %collective-permute-done.4), channel_id=1, source_target_pairs={{0,4},{4,0},{1,5},{5,1},{2,6},{6,2},{3,7},{7,3}} | collective-permute-start | bytes 4718600 | tf_op jit(solution)/shard_map/ppermute | solution.py:618
  446.1 140.6 %collective-permute-start.7 = (bf16[3,1,512,512]{3,2,0,1:T(8,128)(2,1)S(1)}, bf16[3,1,512,512]{3,2,0,1:T(8,128)(2,1)}, u32[]{:S(2)}, u32[]{:S(2)}) collective-permute-start(bf16[3,1,512,512]{3,2,0,1:T(8,128)(2,1)S(1)} %copy-done.3), channel_id=1, source_target_pairs={{0,2},{1,3},{2,0},{3,1},{4,6},{5,7},{6,4},{7,5}} | collective-permute-start | bytes 4718600 | tf_op jit(solution)/shard_map/ppermute | solution.py:615
  447.5 139.2 %collective-permute-start.9 = (bf16[3,1,512,512]{3,2,0,1:T(8,128)(2,1)}, bf16[3,1,512,512]{3,2,0,1:T(8,128)(2,1)}, u32[]{:S(2)}, u32[]{:S(2)}) collective-permute-start(bf16[3,1,512,512]{3,2,0,1:T(8,128)(2,1)} %collective-permute-done.8), channel_id=1, source_target_pairs={{0,2},{1,3},{2,0},{3,1},{4,6},{5,7},{6,4},{7,5}} | collective-permute-start | bytes 4718600 | tf_op jit(solution)/shard_map/ppermute | solution.py:615
  941.2 324.4 %collective-permute-start.10 = (f32[4096,1024]{1,0:T(8,128)}, f32[4096,1024]{1,0:T(8,128)}, u32[]{:S(2)}, u32[]{:S(2)}) collective-permute-start(f32[4096,1024]{1,0:T(8,128)} %get-tuple-element.86), channel_id=1, source_target_pairs={{0,1},{1,0},{2,3},{3,2},{4,5},{5,4},{6,7},{7,6}} | collective-permute-start | bytes 50331656 | tf_op jit(solution)/shard_map/ppermute | solution.py:612
  971.3 294.3 %collective-permute-start.11 = (f32[4096,1024]{1,0:T(8,128)}, f32[4096,1024]{1,0:T(8,128)}, u32[]{:S(2)}, u32[]{:S(2)}) collective-permute-start(f32[4096,1024]{1,0:T(8,128)} %get-tuple-element.87), channel_id=1, source_target_pairs={{0,1},{1,0},{2,3},{3,2},{4,5},{5,4},{6,7},{7,6}} | collective-permute-start | bytes 50331656 | tf_op jit(solution)/shard_map/ppermute | solution.py:612
  971.3 7.0 copy-start.2
  975.1 272.3 %collective-permute-start.12 = (f32[2,3,1,512,512]{4,3,1,2,0:T(8,128)S(1)}, f32[2,3,1,512,512]{4,3,1,2,0:T(8,128)}, u32[]{:S(2)}, u32[]{:S(2)}) collective-permute-start(f32[2,3,1,512,512]{4,3,1,2,0:T(8,128)S(1)} %slice_bitcast_fusion.2), channel_id=1, source_target_pairs={{0,4},{4,0},{1,5},{5,1},{2,6},{6,2},{3,7},{7,3}} | collective-permute-start | bytes 18874376 | tf_op jit(solution)/shard_map/ppermute | solution.py:618
  981.7 275.6 %collective-permute-start.14 = (f32[2,3,1,512,512]{4,3,1,2,0:T(8,128)}, f32[2,3,1,512,512]{4,3,1,2,0:T(8,128)}, u32[]{:S(2)}, u32[]{:S(2)}) collective-permute-start(f32[2,3,1,512,512]{4,3,1,2,0:T(8,128)} %slice_bitcast_fusion), channel_id=1, source_target_pairs={{0,2},{1,3},{2,0},{3,1},{4,6},{5,7},{6,4},{7,5}} | collective-permute-start | bytes 18874376 | tf_op jit(solution)/shard_map/ppermute | solution.py:615
  1257.4 261.2 %collective-permute-start.13 = (f32[3,1,512,512]{3,2,1,0:T(8,128)}, f32[3,1,512,512]{3,2,1,0:T(8,128)}, u32[]{:S(2)}, u32[]{:S(2)}) collective-permute-start(f32[3,1,512,512]{3,2,1,0:T(8,128)} %get-tuple-element.111), channel_id=1, source_target_pairs={{0,2},{1,3},{2,0},{3,1},{4,6},{5,7},{6,4},{7,5}} | collective-permute-start | bytes 9437192 | tf_op jit(solution)/shard_map/ppermute | solution.py:615
  1265.1 248.8 %collective-permute-start.15 = (f32[3,1,512,512]{3,2,1,0:T(8,128)}, f32[3,1,512,512]{3,2,1,0:T(8,128)}, u32[]{:S(2)}, u32[]{:S(2)}) collective-permute-start(f32[3,1,512,512]{3,2,1,0:T(8,128)} %get-tuple-element.109), channel_id=1, source_target_pairs={{0,4},{4,0},{1,5},{5,1},{2,6},{6,2},{3,7},{7,3}} | collective-permute-start | bytes 9437192 | tf_op jit(solution)/shard_map/ppermute | solution.py:618
  1533.6 9.4 copy-start.1
Sparse Core Ops, SparseCore 0:
  10.4 49.1 all-gather.6
  61.9 116.2 all-gather.8
  180.6 237.2 all-gather.10
  420.8 293.1 reduce-scatter.8
  891.7 641.7 reduce-scatter.6

commit v7 on v5

--- a/solution.py
+++ b/solution.py
@@ -46,9 +46,13 @@
     n_qkv = rows * 3 // 4
     x = x_ref[0].astype(F32)
     normed = (x * lax.rsqrt(jnp.mean(x * x, axis=-1, keepdims=True) + EPS)).astype(BF16)
-    for p in range(n_ep):
+
+    def project(p, carry):
         part = nt_dot(normed[:, :half], w_ref[0, p, :n_qkv]) + nt_dot(normed[:, half:], w_ref[1, p, :n_qkv])
-        qkv_ref[0, :, p * n_qkv:(p + 1) * n_qkv] = part.astype(BF16)
+        qkv_ref[0, :, pl.ds(pl.multiple_of(p * n_qkv, LANES), n_qkv)] = part.astype(BF16)
+        return carry
+
+    lax.fori_loop(0, n_ep, project, 0)
     scale = head_dim ** -0.5 * LOG2E
 
     diagonal = lax.broadcasted_iota(jnp.int32, (BLOCK, BLOCK), 1) >= lax.broadcasted_iota(jnp.int32, (BLOCK, BLOCK), 0)
@@ -71,10 +75,14 @@
         return carry
 
     lax.fori_loop(0, d_model // LANES, pair, 0)
-    for f in range(n_fsdp):
+
+    def finish(f, carry):
         w_out = jnp.concatenate([w_ref[f, p, n_qkv:] for p in range(n_ep)], axis=0)
-        cols = slice(f * half, (f + 1) * half)
+        cols = pl.ds(pl.multiple_of(f * half, LANES), half)
         h_ref[0, :, cols] = (x_ref[0, :, cols].astype(F32) + tn_dot(ctx[...], w_out)).astype(BF16)
+        return carry
+
+    lax.fori_loop(0, n_fsdp, finish, 0)
 
 
 def attention(tokens, weights, head_dim):
@@ -100,9 +108,13 @@
     n_qkv = rows * 3 // 4
     n_out = rows - n_qkv
     dh = dh_ref[0]
-    for p in range(n_ep):
+
+    def project(p, carry):
         part = nt_dot(dh[:, :half], w_ref[0, p, n_qkv:]) + nt_dot(dh[:, half:], w_ref[1, p, n_qkv:])
-        dctx[:, p * n_out:(p + 1) * n_out] = part.astype(BF16)
+        dctx[:, pl.ds(pl.multiple_of(p * n_out, LANES), n_out)] = part.astype(BF16)
+        return carry
+
+    lax.fori_loop(0, n_ep, project, 0)
     scale = head_dim ** -0.5
 
     def pair(i, carry):
@@ -138,11 +150,14 @@
 
     lax.fori_loop(0, d_model // LANES, pair, 0)
     x = x_ref[0].astype(F32)
-    d_normed = []
-    for f in range(n_fsdp):
+
+    def back(f, carry):
         w_qkv = jnp.concatenate([w_ref[f, p, :n_qkv] for p in range(n_ep)], axis=0)
-        d_normed.append(jnp.dot(dqkv[...], w_qkv, preferred_element_type=F32).astype(BF16))
-    d_normed = jnp.concatenate(d_normed, axis=1).astype(F32)
+        dctx[:, pl.ds(pl.multiple_of(f * half, LANES), half)] = jnp.dot(dqkv[...], w_qkv, preferred_element_type=F32).astype(BF16)
+        return carry
+
+    lax.fori_loop(0, n_fsdp, back, 0)
+    d_normed = dctx[...].astype(F32)
     inv = lax.rsqrt(jnp.mean(x * x, axis=-1, keepdims=True) + EPS)
     proj = jnp.mean(d_normed * x, axis=-1, keepdims=True)
     d_x = (d_normed * inv - x * (inv * inv * inv * proj)).astype(BF16).astype(F32)
@@ -652,8 +667,7 @@
         tokens, dest, segs, counts, gate = lax.optimization_barrier((tokens, dest, segs, counts, gate))
         h_seq, qkv = attention(tokens, attn_w, head_dim)
         w_axy, w_byx = swap_y(w_ax), swap_x(w_by)
-        w_a = jnp.stack([w_a, w_ax, w_ay, w_axy])
-        w_b = jnp.stack([w_b, w_bx, w_by, w_byx])
+        w_rest = jnp.stack([jnp.concatenate(pair, axis=1) for pair in ((w_a, w_b), (w_ax, w_bx), (w_ay, w_by), (w_axy, w_byx))])
         h_tok = h_seq.reshape(tok_count, d_model)
         h_other = swap(h_tok)
         held = dispatch(h_tok, dout_tok, dest, gate, segs, 0, [], n_local, max_rows)
@@ -665,11 +679,10 @@
             grads.append(([lax.psum_scatter(d_w, ('fsdp', 'ep'), scatter_dimension=0, tiled=False, axis_index_groups=groups)], start))
             start += size
             if n == 0:
-                rows, d_rows, d_a = experts(rows, d_rows, w_a, counts, flips, first, local_experts, x_first=True)
-                rows, d_rows, d_b = experts(rows, d_rows, w_b, counts, flips, mid, local_experts)
-                d_a, d_b = lax.optimization_barrier((d_a, d_b))
-                more_a, more_b = swap_x(d_a[1]), swap_y(d_b[1])
-        sums = d_a[0] + more_a, d_b[0] + more_b
+                rows, d_rows, d_rest = experts(rows, d_rows, w_rest, counts, flips, first, local_experts)
+                d_a, d_b = d_rest[:, :, :, :mid - first], d_rest[:, :, :, mid - first:]
+                more_a, more_b = swap_x(d_a[:, 1]), swap_y(d_b[1])
+        sums = d_a[:, 0] + more_a, d_b[0] + more_b
         more_a, more_b = swap_y(sums[0][1]), swap_x(sums[1][1])
         done = [grads[0], ([sums[0][0], more_a], first), ([sums[1][0], more_b], mid), grads[1]]
         sums = combine(rows, d_rows, dest, gate, segs, n_blocks, n_blocks, [])

time: 1570 us -> 1600 us (1.019)
  starting transfers between devices: 72 us -> 102 us
  waiting for transfers between devices: 454 us -> 427 us
  Pallas kernels: 938 us -> 957 us
    ppermute x5, starting transfers between devices: 34.6 us -> 66 us  [swap_x(): return lax.ppermute(values, 'ep', [(i, i ^ CORES) for i in range(ep_size)])]
    pallas_call x4 -> x3, Pallas kernels: 383 us -> 380 us  [experts(): pl.pallas_call(functools.partial(expert_kernel, expert_of=expert_of, x_fi...]
  transfers between devices with their start and end apart: 21 -> 21, of which waited for: 8 -> 7; matrix products, arithmetic and copies ran while one was open for 5% -> 5% of each run, Pallas kernels for 60% -> 60%
where the time goes in v7:
time: 1600 us; the launch traced here: 1580 us
  Pallas kernels  957 us (60%)
  waiting for transfers between devices  427 us (27%)
  starting transfers between devices  102 us (6%)
  other arithmetic  40.8 us (3%)
  local copies, waits for them, and re-layouts  39.7 us (2%)
    pallas_call x3, Pallas kernels, experts(): pl.pallas_call(functools.partial(expert_kernel, expert_of=expert_of, x_fi...  380 us
    ppermute x5, waiting for transfers between devices, swap_y(): return lax.ppermute(values, 'fsdp', [(i, i ^ 1) for i in range(fsdp_size)])  288 us
    pallas_call x1, Pallas kernels, attention_grad(): pl.pallas_call(functools.partial(attention_grad_kernel, head_dim=head_dim...  196 us
    pallas_call x1, Pallas kernels, attention(): pl.pallas_call(functools.partial(attention_kernel, head_dim=head_dim), gr...  154 us
    ppermute x5, waiting for transfers between devices, swap_x(): return lax.ppermute(values, 'ep', [(i, i ^ CORES) for i in range(ep_size)])  128 us
    pallas_call x2, Pallas kernels, combine(): pl.pallas_call(functools.partial(combine_kernel, base=base, own=bool(extr...  110 us
    pallas_call x2, Pallas kernels, dispatch(): pl.pallas_call(functools.partial(dispatch_kernel, base=base), grid_spec=p...  84.9 us
    ppermute x5, starting transfers between devices, swap_x(): return lax.ppermute(values, 'ep', [(i, i ^ CORES) for i in range(ep_size)])  66 us
  transfers between devices with their start and end apart: 21, of which 7 were waited for; matrix products, arithmetic and copies ran while one was open for 5% of the time, Pallas kernels for 60%

profile of v7, /device:TPU:7, one launch (start us, length us, event | category | flops | bytes accessed | tf_op | source)
XLA Modules:
  0.0 1580.8 jit_solution(3673815124672539766)
XLA Ops:
  7.2 1.1 constant_dynamic-slice_fusion
  8.4 0.8 copy-done
  9.2 1.0 pad_maximum_fusion.5
  10.3 1.3 slice_bitcast_fusion.13
  11.6 1.7 slice_bitcast_fusion.11
  13.3 2.0 pad_maximum_fusion.2
  15.4 2.2 slice_bitcast_fusion.10
  17.5 1.3 copy-done.8
  18.8 1.9 slice_bitcast_fusion.8
  20.7 3.1 pad_maximum_fusion.1
  23.9 0.8 copy-done.10
  24.7 0.8 collective-permute-start.1
  25.6 0.4 collective-permute-start.3
  26.0 0.3 collective-permute-done.1
  26.3 0.7 fusion.7
  27.0 1.0 fusion.4.loc_ref
  28.1 9.2 route.1
  37.2 2.8 copy.41
  40.1 3.8 copy.42
  43.9 2.8 copy.43
  46.7 1.9 slice_reduce_fusion
  48.5 1.3 slice_bitcast_fusion.20
  49.9 9.7 all-gather.7.cloned.1.call-done
  59.6 153.9 %attention.1 = (bf16[8,512,1024]{2,1,0:T(8,128)(2,1)}, bf16[8,512,3072]{2,1,0:T(8,128)(2,1)}) custom-call(bf16[8,512,1024]{2,1,0:T(8,128)(2,1)} %x_ref.1, bf16[2,4,1024,512]{3,2,1,0:T(8,128)(2,1)} %bitcast.107), custom_call_target="tpu_custom_call" | custom-call | flops 89999998976 | bytes 60000000 | tf_op jit(solution)/shard_map/attention/pallas_call | solution.py:93
  213.5 0.3 collective-permute-start.2
  213.8 42.1 %dispatch.2 = (bf16[16,3072,1024]{2,1,0:T(8,128)(2,1)}, bf16[16,3072,1024]{2,1,0:T(8,128)(2,1)}) custom-call(s32[32,16]{1,0:T(8,128)} %get-tuple-element.51.start_ref, s32[32,16]{1,0:T(8,128)} %get-tuple-element.52.rows_ref, s32[32,16]{1,0:T(8,128)} %get-tuple-element.53.off_ref, bf16[4096,1024]{1,0:T(8,128)(2,1)} %bitcast.92, bf16[4096,1024]{1,0:T(8,128)(2,1)} %bitcast.89, ...), custom_call_target="tpu_custom_call" | custom-call | flops 40000000000 | bytes 90000000 | tf_op jit(solution)/shard_map/dispatch/pallas_call | solution.py:322
  255.9 42.8 %dispatch.3 = (bf16[16,3072,1024]{2,1,0:T(8,128)(2,1)}, bf16[16,3072,1024]{2,1,0:T(8,128)(2,1)}) custom-call(s32[32,16]{1,0:T(8,128)} %get-tuple-element.51.start_ref, s32[32,16]{1,0:T(8,128)} %get-tuple-element.52.rows_ref, s32[32,16]{1,0:T(8,128)} %get-tuple-element.53.off_ref, ...), custom_call_target="tpu_custom_call", output_to_operand_aliasing={{0}: (7, {}), {1}: (8, {})} | custom-call | flops 40000000000 | bytes 90000000 | tf_op jit(solution)/shard_map/dispatch/pallas_call | solution.py:322
  298.7 0.6 broadcast_2_flip_ref.2.flip_ref
  299.3 83.6 %experts.3 = (bf16[16,3072,1024]{2,1,0:T(8,128)(2,1)}, bf16[16,3072,1024]{2,1,0:T(8,128)(2,1)}, f32[2,2,3,2,512,512]{5,4,3,2,1,0:T(8,128)}) custom-call(s32[16]{0:T(128)} %get-tuple-element.54.count_ref, s32[2]{0:T(128)} %broadcast_2_flip_ref.2.flip_ref, ...), custom_call_target="tpu_custom_call", output_to_operand_aliasing={{0}: (2, {}), {1}: (3, {})} | custom-call | flops 112000000000 | bytes 200000000 | tf_op jit(solution)/shard_map/experts/pallas_call | solution.py:452
  382.9 0.3 reduce-scatter.7.cloned.1.call-start
  383.2 1.3 slice_bitcast_fusion.19
  384.5 2.0 slice_bitcast_fusion.17
  386.6 1.5 pad_maximum_fusion.4
  388.0 9.6 collective-permute-start.7
  397.6 1.3 pad_maximum_fusion.3
  398.9 18.1 %collective-permute-start.4 = (bf16[3,1,512,512]{3,2,1,0:T(8,128)(2,1)}, bf16[3,1,512,512]{3,2,1,0:T(8,128)(2,1)}, u32[]{:S(2)}, u32[]{:S(2)}) collective-permute-start(bf16[3,1,512,512]{3,2,1,0:T(8,128)(2,1)} %pad_maximum_fusion.3), channel_id=1, source_target_pairs={{0,2},{1,3},{2,0},{3,1},{4,6},{5,7},{6,4},{7,5}} | collective-permute-start | bytes 4718600 | tf_op jit(solution)/shard_map/ppermute | solution.py:630
  417.1 19.8 %collective-permute-done.7 = bf16[3,1,512,512]{3,2,1,0:T(8,128)(2,1)} collective-permute-done((bf16[3,1,512,512]{3,2,1,0:T(8,128)(2,1)}, bf16[3,1,512,512]{3,2,1,0:T(8,128)(2,1)}, u32[]{:S(2)}, u32[]{:S(2)}) %collective-permute-start.7) | collective-permute-done | bytes 1572896 | tf_op jit(solution)/shard_map/ppermute | solution.py:633
  436.9 47.8 %collective-permute-start.9 = (bf16[3,1,512,512]{3,2,1,0:T(8,128)(2,1)}, bf16[3,1,512,512]{3,2,1,0:T(8,128)(2,1)}, u32[]{:S(2)}, u32[]{:S(2)}) collective-permute-start(bf16[3,1,512,512]{3,2,1,0:T(8,128)(2,1)} %collective-permute-done.7), channel_id=1, source_target_pairs={{0,2},{1,3},{2,0},{3,1},{4,6},{5,7},{6,4},{7,5}} | collective-permute-start | bytes 4718600 | tf_op jit(solution)/shard_map/ppermute | solution.py:630
  484.7 1.3 collective-permute-done.4
  486.2 0.7 pad_add_fusion.1.flip_ref
  486.9 2.0 maximum_bitcast_fusion
  488.9 64.6 %collective-permute-done.5 = bf16[3,1,512,512]{3,2,1,0:T(8,128)(2,1)} collective-permute-done((bf16[3,1,512,512]{3,2,1,0:T(8,128)(2,1)}, bf16[3,1,512,512]{3,2,1,0:T(8,128)(2,1)}, u32[]{:S(2)}, u32[]{:S(2)}) %collective-permute-start.5) | collective-permute-done | bytes 1572896 | tf_op jit(solution)/shard_map/ppermute | solution.py:630
  553.5 2.2 maximum_bitcast_fusion.1
  555.7 2.2 maximum_bitcast_fusion.2
  557.8 62.6 %collective-permute-done.9 = bf16[3,1,512,512]{3,2,1,0:T(8,128)(2,1)} collective-permute-done((bf16[3,1,512,512]{3,2,1,0:T(8,128)(2,1)}, bf16[3,1,512,512]{3,2,1,0:T(8,128)(2,1)}, u32[]{:S(2)}, u32[]{:S(2)}) %collective-permute-start.9) | collective-permute-done | bytes 1572896 | tf_op jit(solution)/shard_map/ppermute | solution.py:630
  620.4 2.6 maximum_bitcast_fusion.3
  623.0 5.5 pad_maximum_fusion.w_lo.w_hi
  628.4 95.9 %experts.4 = (bf16[16,3072,1024]{2,1,0:T(8,128)(2,1)}, bf16[16,3072,1024]{2,1,0:T(8,128)(2,1)}, f32[2,2,3,2,512,512]{5,4,3,2,1,0:T(8,128)}) custom-call(s32[16]{0:T(128)} %get-tuple-element.54.count_ref, s32[2]{0:T(128)} %pad_add_fusion.1.flip_ref, bf16[16,3072,1024]{2,1,0:T(8,128)(2,1)} %get-tuple-element.63.r_hbm, ...), custom_call_target="tpu_custom_call", output_to_operand_aliasing={{0}: (2, {}), {1}: (3, {})} | custom-call | flops 112000000000 | bytes 200000000 | tf_op jit(solution)/shard_map/experts/pallas_call | solution.py:452
  724.4 200.6 %experts.5 = (bf16[16,3072,1024]{2,1,0:T(8,128)(2,1)}, bf16[16,3072,1024]{2,1,0:T(8,128)(2,1)}, f32[2,2,3,4,512,512]{5,4,3,2,1,0:T(8,128)}) custom-call(s32[16]{0:T(128)} %get-tuple-element.54.count_ref, s32[2]{0:T(128)} %broadcast_2_flip_ref.2.flip_ref, ...), custom_call_target="tpu_custom_call", output_to_operand_aliasing={{0}: (2, {}), {1}: (3, {})} | custom-call | flops 224000000000 | bytes 400000000 | tf_op jit(solution)/shard_map/experts/pallas_call | solution.py:452
  925.1 50.6 %combine.2 = (f32[4096,1024]{1,0:T(8,128)}, f32[4096,1024]{1,0:T(8,128)}) custom-call(s32[32,16]{1,0:T(8,128)} %get-tuple-element.51.start_ref, s32[32,16]{1,0:T(8,128)} %get-tuple-element.52.rows_ref, s32[32,16]{1,0:T(8,128)} %get-tuple-element.53.off_ref, bf16[16,3072,1024]{2,1,0:T(8,128)(2,1)} %get-tuple-element.67.y_hbm, ...), custom_call_target="tpu_custom_call" | custom-call | flops 44999999488 | bytes 120000000 | tf_op jit(solution)/shard_map/combine/pallas_call | solution.py:555
  975.7 24.4 %collective-permute-start.10 = (f32[4096,1024]{1,0:T(8,128)}, f32[4096,1024]{1,0:T(8,128)}, u32[]{:S(2)}, u32[]{:S(2)}) collective-permute-start(f32[4096,1024]{1,0:T(8,128)} %get-tuple-element.69), channel_id=1, source_target_pairs={{0,1},{1,0},{2,3},{3,2},{4,5},{5,4},{6,7},{7,6}} | collective-permute-start | bytes 50331656 | tf_op jit(solution)/shard_map/ppermute | solution.py:627
  1000.1 3.6 slice_bitcast_fusion.2
  1003.8 3.8 slice_bitcast_fusion
  1007.6 268.3 %collective-permute-done.12 = f32[2,3,1,512,512]{4,3,1,2,0:T(8,128)} collective-permute-done((f32[2,3,1,512,512]{4,3,1,2,0:T(8,128)S(1)}, f32[2,3,1,512,512]{4,3,1,2,0:T(8,128)}, u32[]{:S(2)}, u32[]{:S(2)}) %collective-permute-start.12) | collective-permute-done | bytes 6291488 | tf_op jit(solution)/shard_map/ppermute | solution.py:633
  1276.0 6.6 fusion.1
  1282.5 3.3 slice_bitcast_fusion.6
  1285.9 6.5 fusion
  1292.4 3.3 slice_bitcast_fusion.4
  1295.9 59.0 %combine.3 = (bf16[4096,1024]{1,0:T(8,128)(2,1)}, bf16[4096,1024]{1,0:T(8,128)(2,1)}) custom-call(s32[32,16]{1,0:T(8,128)} %get-tuple-element.51.start_ref, s32[32,16]{1,0:T(8,128)} %get-tuple-element.52.rows_ref, s32[32,16]{1,0:T(8,128)} %get-tuple-element.53.off_ref, bf16[16,3072,1024]{2,1,0:T(8,128)(2,1)} %get-tuple-element.67.y_hbm, ...), custom_call_target="tpu_custom_call" | custom-call | flops 44999999488 | bytes 120000000 | tf_op jit(solution)/shard_map/combine/pallas_call | solution.py:555
  1354.9 195.5 %attention_grad.1 = bf16[8,512,1024]{2,1,0:T(8,128)(2,1)} custom-call(bf16[8,512,1024]{2,1,0:T(8,128)(2,1)} %bitcast.110, bf16[8,512,1024]{2,1,0:T(8,128)(2,1)} %x_ref.1, bf16[8,512,3072]{2,1,0:T(8,128)(2,1)} %get-tuple-element.73.qkv_ref, bf16[2,4,1024,512]{3,2,1,0:T(8,128)(2,1)} %bitcast.108), custom_call_target="tpu_custom_call" | custom-call | flops 149999992832 | bytes 70000000 | tf_op jit(solution)/shard_map/attention_grad/pallas_call | solution.py:172
  1550.4 4.9 place.4
  1555.3 4.7 place.5
  1560.0 4.6 place.6
  1564.7 9.4 place.7
  (58 shorter events, 1.0 us)
Async XLA Ops:
  7.2 2.0 copy-start
  7.2 52.4 %all-gather.7.cloned.1.call-start = ((), (), s32[]{:S(2)}) async-start(), calls=%async_computation.2 | async-start | bytes 9437184 | tf_op jit(solution)/shard_map/all_gather | solution.py:642
  10.3 288.4 %all-gather.9.cloned.1.call-start = ((), (), s32[]{:S(2)}) async-start(), calls=%async_computation.3 | async-start | bytes 15728640 | tf_op jit(solution)/shard_map/all_gather | solution.py:647
  15.3 709.1 %all-gather.11.cloned.1.call-start = ((), (), s32[]{:S(2)}) async-start(), calls=%async_computation.4 | async-start | bytes 31457280 | tf_op jit(solution)/shard_map/all_gather | solution.py:647
  15.4 3.4 copy-start.8
  23.8 0.8 copy-start.10
  23.8 1.6 copy-start.11
  23.8 1.6 copy-start.12
  23.8 1526.6 %reduce-scatter.9.cloned.1.call-start = ((), (), s32[]{:S(2)}) async-start(), calls=%async_computation.6 | async-start | bytes 31457280
  24.7 1.7 collective-permute-start.1
  25.4 1.6 collective-permute-start
  25.6 230.2 %collective-permute-start.3 = (bf16[4096,1024]{1,0:T(8,128)(2,1)}, bf16[4096,1024]{1,0:T(8,128)(2,1)}, u32[]{:S(2)}, u32[]{:S(2)}) collective-permute-start(bf16[4096,1024]{1,0:T(8,128)(2,1)} %bitcast.88), channel_id=1, source_target_pairs={{0,1},{1,0},{2,3},{3,2},{4,5},{5,4},{6,7},{7,6}} | collective-permute-start | bytes 25165832 | tf_op jit(solution)/shard_map/ppermute | solution.py:627
  37.2 6.6 copy-start.9
  213.5 42.4 %collective-permute-start.2 = (bf16[4096,1024]{1,0:T(8,128)(2,1)}, bf16[4096,1024]{1,0:T(8,128)(2,1)}, u32[]{:S(2)}, u32[]{:S(2)}) collective-permute-start(bf16[4096,1024]{1,0:T(8,128)(2,1)} %bitcast.91), channel_id=1, source_target_pairs={{0,1},{1,0},{2,3},{3,2},{4,5},{5,4},{6,7},{7,6}} | collective-permute-start | bytes 25165832 | tf_op jit(solution)/shard_map/ppermute | solution.py:627
  382.9 1181.8 %reduce-scatter.7.cloned.1.call-start = ((), (), s32[]{:S(2)}) async-start(), calls=%async_computation.5 | async-start | bytes 62914560
  384.5 14.5 copy-start.2
  384.5 14.5 copy-start.3
  386.5 99.7 %copy-start.4 = (bf16[1,1,512,512]{3,2,1,0:T(8,128)(2,1)}, bf16[1,1,512,512]{3,2,1,0:T(8,128)(2,1)S(1)}, u32[]{:S(2)}) copy-start(bf16[1,1,512,512]{3,2,1,0:T(8,128)(2,1)S(1)} %get-tuple-element.97) | copy-start | bytes 1572868
  386.5 99.7 %copy-start.5 = (bf16[1,1,512,512]{3,2,1,0:T(8,128)(2,1)}, bf16[1,1,512,512]{3,2,1,0:T(8,128)(2,1)S(1)}, u32[]{:S(2)}) copy-start(bf16[1,1,512,512]{3,2,1,0:T(8,128)(2,1)S(1)} %get-tuple-element.98) | copy-start | bytes 1572868
  386.5 99.7 %copy-start.6 = (bf16[1,1,512,512]{3,2,1,0:T(8,128)(2,1)}, bf16[1,1,512,512]{3,2,1,0:T(8,128)(2,1)S(1)}, u32[]{:S(2)}) copy-start(bf16[1,1,512,512]{3,2,1,0:T(8,128)(2,1)S(1)} %get-tuple-element.105) | copy-start | bytes 1572868
  386.5 99.7 %copy-start.7 = (bf16[1,1,512,512]{3,2,1,0:T(8,128)(2,1)}, bf16[1,1,512,512]{3,2,1,0:T(8,128)(2,1)S(1)}, u32[]{:S(2)}) copy-start(bf16[1,1,512,512]{3,2,1,0:T(8,128)(2,1)S(1)} %get-tuple-element.106) | copy-start | bytes 1572868
  388.0 48.9 %collective-permute-start.7 = (bf16[3,1,512,512]{3,2,1,0:T(8,128)(2,1)}, bf16[3,1,512,512]{3,2,1,0:T(8,128)(2,1)}, u32[]{:S(2)}, u32[]{:S(2)}) collective-permute-start(bf16[3,1,512,512]{3,2,1,0:T(8,128)(2,1)} %pad_maximum_fusion.4), channel_id=1, source_target_pairs={{0,4},{4,0},{1,5},{5,1},{2,6},{6,2},{3,7},{7,3}} | collective-permute-start | bytes 4718600 | tf_op jit(solution)/shard_map/ppermute | solution.py:633
  398.9 87.1 %collective-permute-start.4 = (bf16[3,1,512,512]{3,2,1,0:T(8,128)(2,1)}, bf16[3,1,512,512]{3,2,1,0:T(8,128)(2,1)}, u32[]{:S(2)}, u32[]{:S(2)}) collective-permute-start(bf16[3,1,512,512]{3,2,1,0:T(8,128)(2,1)} %pad_maximum_fusion.3), channel_id=1, source_target_pairs={{0,2},{1,3},{2,0},{3,1},{4,6},{5,7},{6,4},{7,5}} | collective-permute-start | bytes 4718600 | tf_op jit(solution)/shard_map/ppermute | solution.py:630
  417.1 136.4 %collective-permute-start.5 = (bf16[3,1,512,512]{3,2,1,0:T(8,128)(2,1)}, bf16[3,1,512,512]{3,2,1,0:T(8,128)(2,1)}, u32[]{:S(2)}, u32[]{:S(2)}) collective-permute-start(bf16[3,1,512,512]{3,2,1,0:T(8,128)(2,1)} %pad_maximum_fusion.4), channel_id=1, source_target_pairs={{0,2},{1,3},{2,0},{3,1},{4,6},{5,7},{6,4},{7,5}} | collective-permute-start | bytes 4718600 | tf_op jit(solution)/shard_map/ppermute | solution.py:630
  417.1 138.5 %collective-permute-start.6 = (bf16[3,1,512,512]{3,2,1,0:T(8,128)(2,1)}, bf16[3,1,512,512]{3,2,1,0:T(8,128)(2,1)}, u32[]{:S(2)}, u32[]{:S(2)}) collective-permute-start(bf16[3,1,512,512]{3,2,1,0:T(8,128)(2,1)} %pad_maximum_fusion.3), channel_id=1, source_target_pairs={{0,4},{4,0},{1,5},{5,1},{2,6},{6,2},{3,7},{7,3}} | collective-permute-start | bytes 4718600 | tf_op jit(solution)/shard_map/ppermute | solution.py:633
  436.9 183.5 %collective-permute-start.9 = (bf16[3,1,512,512]{3,2,1,0:T(8,128)(2,1)}, bf16[3,1,512,512]{3,2,1,0:T(8,128)(2,1)}, u32[]{:S(2)}, u32[]{:S(2)}) collective-permute-start(bf16[3,1,512,512]{3,2,1,0:T(8,128)(2,1)} %collective-permute-done.7), channel_id=1, source_target_pairs={{0,2},{1,3},{2,0},{3,1},{4,6},{5,7},{6,4},{7,5}} | collective-permute-start | bytes 4718600 | tf_op jit(solution)/shard_map/ppermute | solution.py:630
  486.1 134.3 %collective-permute-start.8 = (bf16[3,1,512,512]{3,2,1,0:T(8,128)(2,1)}, bf16[3,1,512,512]{3,2,1,0:T(8,128)(2,1)}, u32[]{:S(2)}, u32[]{:S(2)}) collective-permute-start(bf16[3,1,512,512]{3,2,1,0:T(8,128)(2,1)} %collective-permute-done.4), channel_id=1, source_target_pairs={{0,4},{4,0},{1,5},{5,1},{2,6},{6,2},{3,7},{7,3}} | collective-permute-start | bytes 4718600 | tf_op jit(solution)/shard_map/ppermute | solution.py:633
  975.7 320.2 %collective-permute-start.10 = (f32[4096,1024]{1,0:T(8,128)}, f32[4096,1024]{1,0:T(8,128)}, u32[]{:S(2)}, u32[]{:S(2)}) collective-permute-start(f32[4096,1024]{1,0:T(8,128)} %get-tuple-element.69), channel_id=1, source_target_pairs={{0,1},{1,0},{2,3},{3,2},{4,5},{5,4},{6,7},{7,6}} | collective-permute-start | bytes 50331656 | tf_op jit(solution)/shard_map/ppermute | solution.py:627
  1000.1 295.8 %collective-permute-start.11 = (f32[4096,1024]{1,0:T(8,128)}, f32[4096,1024]{1,0:T(8,128)}, u32[]{:S(2)}, u32[]{:S(2)}) collective-permute-start(f32[4096,1024]{1,0:T(8,128)} %get-tuple-element.70), channel_id=1, source_target_pairs={{0,1},{1,0},{2,3},{3,2},{4,5},{5,4},{6,7},{7,6}} | collective-permute-start | bytes 50331656 | tf_op jit(solution)/shard_map/ppermute | solution.py:627
  1003.7 272.2 %collective-permute-start.12 = (f32[2,3,1,512,512]{4,3,1,2,0:T(8,128)S(1)}, f32[2,3,1,512,512]{4,3,1,2,0:T(8,128)}, u32[]{:S(2)}, u32[]{:S(2)}) collective-permute-start(f32[2,3,1,512,512]{4,3,1,2,0:T(8,128)S(1)} %slice_bitcast_fusion.2), channel_id=1, source_target_pairs={{0,4},{4,0},{1,5},{5,1},{2,6},{6,2},{3,7},{7,3}} | collective-permute-start | bytes 18874376 | tf_op jit(solution)/shard_map/ppermute | solution.py:633
  1007.6 278.3 %collective-permute-start.14 = (f32[2,3,1,512,512]{4,3,1,2,0:T(8,128)S(1)}, f32[2,3,1,512,512]{4,3,1,2,0:T(8,128)}, u32[]{:S(2)}, u32[]{:S(2)}) collective-permute-start(f32[2,3,1,512,512]{4,3,1,2,0:T(8,128)S(1)} %slice_bitcast_fusion), channel_id=1, source_target_pairs={{0,2},{1,3},{2,0},{3,1},{4,6},{5,7},{6,4},{7,5}} | collective-permute-start | bytes 18874376 | tf_op jit(solution)/shard_map/ppermute | solution.py:630
  1285.9 274.1 %collective-permute-start.13 = (f32[3,1,512,512]{3,2,1,0:T(8,128)}, f32[3,1,512,512]{3,2,1,0:T(8,128)}, u32[]{:S(2)}, u32[]{:S(2)}) collective-permute-start(f32[3,1,512,512]{3,2,1,0:T(8,128)} %get-tuple-element.91), channel_id=1, source_target_pairs={{0,2},{1,3},{2,0},{3,1},{4,6},{5,7},{6,4},{7,5}} | collective-permute-start | bytes 9437192 | tf_op jit(solution)/shard_map/ppermute | solution.py:630
  1295.8 259.5 %collective-permute-start.15 = (f32[3,1,512,512]{3,2,1,0:T(8,128)}, f32[3,1,512,512]{3,2,1,0:T(8,128)}, u32[]{:S(2)}, u32[]{:S(2)}) collective-permute-start(f32[3,1,512,512]{3,2,1,0:T(8,128)} %get-tuple-element.89), channel_id=1, source_target_pairs={{0,4},{4,0},{1,5},{5,1},{2,6},{6,2},{3,7},{7,3}} | collective-permute-start | bytes 9437192 | tf_op jit(solution)/shard_map/ppermute | solution.py:633
  1564.7 9.4 copy-start.1
Sparse Core Ops, SparseCore 0:
  10.4 49.1 all-gather.6
  61.9 116.3 all-gather.8
  180.6 223.8 all-gather.10
  407.4 317.6 reduce-scatter.8
  925.2 635.2 reduce-scatter.6
